TPU v7x, 32 devices: a whole 2x2x4 slice. The times are simulated.
32 devices in a mesh: ctx: 8 (over y, x, core), fsdp: 4 (over z).
Axes of the slice: x: 2, y: 2, z: 4, core: 2. Of those that a mesh axis runs over, the one named last changes fastest.
Arguments:
- tokens: bfloat16 [4, 1536, 1536], P('fsdp', 'ctx'), may hold values from -6 to 6
- positions: int32 [4, 1536], P('fsdp', 'ctx'), may hold values from 0 to 1535, as said below
- qkv_weight: bfloat16 [1, 1536, 3072], P(None, 'fsdp'), as said below
- out_weight: bfloat16 [1, 1536, 1536], P(None, 'fsdp'), may hold values from -2.5 to 2.5
- gate_up_weight: bfloat16 [1, 1536, 2, 4096], P(None, 'fsdp'), may hold values from -0.15625 to 0.15625
- down_weight: bfloat16 [1, 4096, 1536], P(None, 'fsdp'), may hold values from -0.09375 to 0.09375
- attn_gain: bfloat16 [1, 1536], P(None, 'fsdp'), may hold values from 0.5 to 1.5
- ffn_gain: bfloat16 [1, 1536], P(None, 'fsdp'), may hold values from 0.5 to 1.5
- cotangent: float32 [4, 1536, 1536], P('fsdp', 'ctx'), may hold values from -6 to 6
Outputs:
- activations: bfloat16 [4, 1536, 1536], P('fsdp', 'ctx')
- input_grad: float32 [4, 1536, 1536], P('fsdp', 'ctx')
- qkv_grad: float32 [1, 1536, 3072], P(None, 'fsdp')
- out_grad: float32 [1, 1536, 1536], P(None, 'fsdp')
- gate_up_grad: float32 [1, 1536, 2, 4096], P(None, 'fsdp')
- down_grad: float32 [1, 4096, 1536], P(None, 'fsdp')
- attn_gain_grad: float32 [1, 1536], P(None, 'fsdp')
- ffn_gain_grad: float32 [1, 1536], P(None, 'fsdp')
Inputs may be any that keep to these rules, and one draw needn't show every extreme that they name: Each sequence holds every position of 0 to 1535 once. Its rows form aligned blocks of 192 rows; a block holds span c (the 96 positions from c * 96 on, in order) and then span 2 * 8 - 1 - c likewise; c differs between the blocks of a sequence. `qkv_weight`: projection weights of mean zero.
All inputs are finite; a program needn't handle non-finite values.
Results may differ from a plain program's by a relative error of at most 0.017.
The roundings to bfloat16 on the way count: a program that leaves them out, or rounds other values in their place, can miss the bound.
Values may be sent and summed in bfloat16 or wider, within the bound.
A program may use at most 320 MiB of HBM per device.

v0:
```python
import jax
import jax.numpy as jnp
from jax import lax
from jax.sharding import PartitionSpec as P

HEADS = 16
KV_HEADS = 8
HEAD_DIM = 96
LAYERS = 1


epsilon = 1e-05
rope_base = 100000.0


def angles(place):
    halfway = HEAD_DIM // 2
    frequency = rope_base ** (-(jnp.arange(halfway, dtype=jnp.float32) * 2.0 / HEAD_DIM))
    phases = place.astype(jnp.float32)[:, None] * frequency[None, :]
    phases = jnp.concatenate([phases, phases], axis=-1)
    return (jnp.cos(phases)[:, None, :], jnp.sin(phases)[:, None, :])


def rotate(vectors, cosine, sine):
    halfway = vectors.shape[-1] // 2
    turned = jnp.concatenate([-vectors[..., halfway:], vectors[..., :halfway]], axis=-1)
    return vectors * cosine + turned * sine


def rotate_back(grads, cosine, sine):
    halfway = grads.shape[-1] // 2
    scaled = grads * sine
    return grads * cosine + jnp.concatenate(
        [scaled[..., halfway:], -scaled[..., :halfway]], axis=-1
    )


def normalize(rows, gain):
    factor = lax.rsqrt(jnp.mean(rows * rows, axis=-1, keepdims=True) + epsilon)
    return (rows * factor * gain, factor)


def normalize_back(upstream, rows, factor, gain):
    unit_rows = rows * factor
    gain_grad = jnp.sum(upstream * unit_rows, axis=0)
    scaled = upstream * gain
    row_inner = jnp.mean(scaled * unit_rows, axis=-1, keepdims=True)
    return (factor * (scaled - unit_rows * row_inner), gain_grad)


def split_blocks(queries, keys_all, values_all, key_place):
    rows = queries.shape[0]
    half = rows // 2
    shards = key_place.shape[0] // rows
    key_blocks = keys_all.reshape(shards, 2, half, KV_HEADS, HEAD_DIM)
    value_blocks = values_all.reshape(shards, 2, half, KV_HEADS, HEAD_DIM)
    place_blocks = key_place.reshape(shards, 2, half)
    return (key_blocks, value_blocks, place_blocks)


def scores_of(queries, key_block, place_block, query_place):
    scaling = HEAD_DIM ** (-0.5)
    scores = (
        jnp.einsum("rkgd,skd->kgrs", queries, key_block, preferred_element_type=jnp.float32)
        * scaling
    )
    allowed = place_block[None, None, None, :] <= query_place[None, None, :, None]
    return (scores, allowed)


def reachable(place_block, query_place):
    return jnp.min(place_block) <= jnp.max(query_place)


def attention_forward(queries, keys_all, values_all, query_place, key_place):
    key_blocks, value_blocks, place_blocks = split_blocks(queries, keys_all, values_all, key_place)
    rows = queries.shape[0]
    half = rows // 2
    groups = HEADS // KV_HEADS
    query_spans = queries.reshape(2, half, KV_HEADS, groups, HEAD_DIM)
    place_spans = query_place.reshape(2, half)

    def sweep_max(carry, inputs):
        key_block, place_block = inputs
        updated_all = []
        for span in range(2):
            state = carry[span]
            for part in range(2):

                def live(current, span=span, part=part):
                    maximum, total = current
                    scores, allowed = scores_of(
                        query_spans[span], key_block[part], place_block[part], place_spans[span]
                    )
                    masked = jnp.where(allowed, scores, -1e30)
                    updated = jnp.maximum(maximum, jnp.max(masked, axis=-1))
                    weights_now = jnp.where(allowed, jnp.exp(masked - updated[..., None]), 0.0)
                    return (
                        updated,
                        total * jnp.exp(maximum - updated) + jnp.sum(weights_now, axis=-1),
                    )

                state = lax.cond(
                    reachable(place_block[part], place_spans[span]),
                    live,
                    lambda current: current,
                    state,
                )
            updated_all.append(state)
        return (tuple(updated_all), None)

    start_max = jnp.full((KV_HEADS, groups, half), -1e30, jnp.float32)
    start_total = jnp.zeros((KV_HEADS, groups, half), jnp.float32)
    start = ((start_max, start_total), (start_max, start_total))
    finals, unused = lax.scan(sweep_max, start, (key_blocks, place_blocks))
    logsum_spans = [finals[span][0] + jnp.log(finals[span][1]) for span in range(2)]

    def sweep_out(results, inputs):
        key_block, value_block, place_block = inputs
        updated_all = []
        for span in range(2):
            result = results[span]
            for part in range(2):

                def live(current, span=span, part=part):
                    scores, allowed = scores_of(
                        query_spans[span], key_block[part], place_block[part], place_spans[span]
                    )
                    softmax_rows = jnp.where(
                        allowed, jnp.exp(scores - logsum_spans[span][..., None]), 0.0
                    ).astype(jnp.bfloat16)
                    return current + jnp.einsum(
                        "kgrs,skd->rkgd",
                        softmax_rows,
                        value_block[part],
                        preferred_element_type=jnp.float32,
                    )

                result = lax.cond(
                    reachable(place_block[part], place_spans[span]),
                    live,
                    lambda current: current,
                    result,
                )
            updated_all.append(result)
        return (tuple(updated_all), None)

    start_out = jnp.zeros((half, KV_HEADS, groups, HEAD_DIM), jnp.float32)
    outs, unused_out = lax.scan(
        sweep_out, (start_out, start_out), (key_blocks, value_blocks, place_blocks)
    )
    logsum = jnp.concatenate(logsum_spans, axis=-1)
    attended = jnp.concatenate([outs[0], outs[1]], axis=0)
    return (logsum, attended)


def attention_backward(
    queries, keys_all, values_all, query_place, key_place, logsum, attended_grad, row_inner
):
    key_blocks, value_blocks, place_blocks = split_blocks(queries, keys_all, values_all, key_place)
    rows = queries.shape[0]
    half = rows // 2
    groups = HEADS // KV_HEADS
    scaling = HEAD_DIM ** (-0.5)
    query_spans = queries.reshape(2, half, KV_HEADS, groups, HEAD_DIM)
    place_spans = query_place.reshape(2, half)
    grad_spans = attended_grad.reshape(2, half, KV_HEADS, groups, HEAD_DIM)
    logsum_spans = logsum.reshape(KV_HEADS, groups, 2, half)
    inner_spans = row_inner.reshape(KV_HEADS, groups, 2, half)

    def sweep_back(query_grads, inputs):
        key_block, value_block, place_block = inputs
        query_grads = list(query_grads)
        key_parts = []
        value_parts = []
        for part in range(2):
            key_acc = jnp.zeros((half, KV_HEADS, HEAD_DIM), jnp.float32)
            value_acc = jnp.zeros((half, KV_HEADS, HEAD_DIM), jnp.float32)
            for span in range(2):

                def live(current, span=span, part=part):
                    query_grad, key_grad, value_grad = current
                    scores, allowed = scores_of(
                        query_spans[span], key_block[part], place_block[part], place_spans[span]
                    )
                    softmax_rows = jnp.where(
                        allowed, jnp.exp(scores - logsum_spans[:, :, span][..., None]), 0.0
                    )
                    rounded = softmax_rows.astype(jnp.bfloat16)
                    weight_grad = jnp.einsum(
                        "rkgd,skd->kgrs",
                        grad_spans[span],
                        value_block[part],
                        preferred_element_type=jnp.float32,
                    )
                    score_grad = (
                        softmax_rows * (weight_grad - inner_spans[:, :, span][..., None])
                    ).astype(jnp.bfloat16)
                    query_grad = (
                        query_grad
                        + jnp.einsum(
                            "kgrs,skd->rkgd",
                            score_grad,
                            key_block[part],
                            preferred_element_type=jnp.float32,
                        )
                        * scaling
                    )
                    key_grad = (
                        key_grad
                        + jnp.einsum(
                            "kgrs,rkgd->skd",
                            score_grad,
                            query_spans[span],
                            preferred_element_type=jnp.float32,
                        )
                        * scaling
                    )
                    value_grad = value_grad + jnp.einsum(
                        "kgrs,rkgd->skd",
                        rounded,
                        grad_spans[span],
                        preferred_element_type=jnp.float32,
                    )
                    return (query_grad, key_grad, value_grad)

                state = (query_grads[span], key_acc, value_acc)
                state = lax.cond(
                    reachable(place_block[part], place_spans[span]),
                    live,
                    lambda current: current,
                    state,
                )
                query_grads[span], key_acc, value_acc = state
            key_parts.append(key_acc)
            value_parts.append(value_acc)
        key_out = jnp.concatenate(key_parts, axis=0)
        value_out = jnp.concatenate(value_parts, axis=0)
        return (tuple(query_grads), (key_out, value_out))

    start_grad = jnp.zeros((half, KV_HEADS, groups, HEAD_DIM), jnp.float32)
    query_pair, (key_grads, value_grads) = lax.scan(
        sweep_back, (start_grad, start_grad), (key_blocks, value_blocks, place_blocks)
    )
    query_grad = jnp.concatenate([query_pair[0], query_pair[1]], axis=0)
    return (
        query_grad,
        key_grads.reshape(-1, KV_HEADS, HEAD_DIM),
        value_grads.reshape(-1, KV_HEADS, HEAD_DIM),
    )


def fetch_layer(qkv_weight, out_weight, gate_up_weight, down_weight, attn_gain, ffn_gain, layer_id):
    return (
        lax.all_gather(qkv_weight[layer_id], "fsdp", axis=0, tiled=True),
        lax.all_gather(out_weight[layer_id], "fsdp", axis=0, tiled=True),
        lax.all_gather(gate_up_weight[layer_id], "fsdp", axis=0, tiled=True),
        lax.all_gather(down_weight[layer_id], "fsdp", axis=0, tiled=True),
        lax.all_gather(attn_gain[layer_id], "fsdp", axis=0, tiled=True),
        lax.all_gather(ffn_gain[layer_id], "fsdp", axis=0, tiled=True),
    )


def fetch_again(qkv_weight, out_weight, gate_up_weight, down_weight, attn_gain, ffn_gain, layer_id):
    return (
        lax.all_gather(qkv_weight[layer_id], "fsdp", axis=0, tiled=True),
        lax.all_gather(out_weight[layer_id], "fsdp", axis=0, tiled=True),
        lax.all_gather(gate_up_weight[layer_id], "fsdp", axis=0, tiled=True),
        lax.all_gather(down_weight[layer_id], "fsdp", axis=0, tiled=True),
        lax.all_gather(attn_gain[layer_id], "fsdp", axis=0, tiled=True),
        lax.all_gather(ffn_gain[layer_id], "fsdp", axis=0, tiled=True),
    )


def forward_layer(stream, query_place, key_place, gathered):
    qkv_full, out_full, gate_up_full, down_full, attn_full, ffn_full = gathered
    rows = stream.shape[0]
    groups = HEADS // KV_HEADS
    query_width = HEADS * HEAD_DIM
    key_width = KV_HEADS * HEAD_DIM
    cosine, sine = angles(query_place)
    normed, first_factor = normalize(stream, attn_full.astype(jnp.float32))
    normed = normed.astype(jnp.bfloat16)
    projected = jnp.dot(normed, qkv_full, preferred_element_type=jnp.float32)
    queries = rotate(projected[:, :query_width].reshape(rows, HEADS, HEAD_DIM), cosine, sine)
    queries = queries.reshape(rows, KV_HEADS, groups, HEAD_DIM).astype(jnp.bfloat16)
    keys_local = rotate(
        projected[:, query_width : query_width + key_width].reshape(rows, KV_HEADS, HEAD_DIM),
        cosine,
        sine,
    ).astype(jnp.bfloat16)
    values_local = (
        projected[:, query_width + key_width :]
        .reshape(rows, KV_HEADS, HEAD_DIM)
        .astype(jnp.bfloat16)
    )
    keys_all, values_all = (
        lax.all_gather(keys_local, "ctx", axis=0, tiled=True),
        lax.all_gather(values_local, "ctx", axis=0, tiled=True),
    )
    logsum, attended = attention_forward(queries, keys_all, values_all, query_place, key_place)
    attended_low = attended.reshape(rows, query_width).astype(jnp.bfloat16)
    middle = stream + jnp.dot(attended_low, out_full, preferred_element_type=jnp.float32)
    second, second_factor = normalize(middle, ffn_full.astype(jnp.float32))
    second = second.astype(jnp.bfloat16)
    gate_up = jnp.einsum("rd,dcf->rcf", second, gate_up_full, preferred_element_type=jnp.float32)
    hidden = (jax.nn.silu(gate_up[:, 0]) * gate_up[:, 1]).astype(jnp.bfloat16)
    result = middle + jnp.dot(hidden, down_full, preferred_element_type=jnp.float32)
    stored = (
        stream,
        first_factor,
        normed,
        queries,
        keys_local,
        values_local,
        keys_all,
        values_all,
        logsum,
        attended,
        attended_low,
        middle,
        second_factor,
        second,
        gate_up,
        hidden,
    )
    return (result, stored)


def backward_layer(upstream, stored, gathered, query_place, key_place, keys_all, values_all):
    (
        stream,
        first_factor,
        normed,
        queries,
        keys_local,
        values_local,
        kept_keys,
        kept_values,
        logsum,
        attended,
        attended_low,
        middle,
        second_factor,
        second,
        gate_up,
        hidden,
    ) = stored
    qkv_full, out_full, gate_up_full, down_full, attn_full, ffn_full = gathered
    rows = stream.shape[0]
    groups = HEADS // KV_HEADS
    cosine, sine = angles(query_place)
    upstream_low = upstream.astype(jnp.bfloat16)
    hidden_grad = jnp.einsum(
        "rd,fd->rf", upstream_low, down_full, preferred_element_type=jnp.float32
    )
    gate_part = gate_up[:, 0]
    up_part = gate_up[:, 1]
    sigmoid = jax.nn.sigmoid(gate_part)
    gate_grad = hidden_grad * up_part * sigmoid * (1.0 + gate_part * (1.0 - sigmoid))
    up_grad = hidden_grad * gate_part * sigmoid
    gate_up_low = jnp.stack([gate_grad, up_grad], axis=1).astype(jnp.bfloat16)
    second_grad = jnp.einsum(
        "rcf,dcf->rd", gate_up_low, gate_up_full, preferred_element_type=jnp.float32
    )
    middle_grad, ffn_gain_grad = normalize_back(
        second_grad, middle, second_factor, ffn_full.astype(jnp.float32)
    )
    middle_grad = middle_grad + upstream
    middle_low = middle_grad.astype(jnp.bfloat16)
    attended_grad = jnp.einsum(
        "rd,od->ro", middle_low, out_full, preferred_element_type=jnp.float32
    )
    attended_grad = attended_grad.astype(jnp.bfloat16).reshape(rows, KV_HEADS, groups, HEAD_DIM)
    row_inner = jnp.einsum("rkgd,rkgd->kgr", attended_grad.astype(jnp.float32), attended)
    query_grad, key_grads, value_grads = attention_backward(
        queries, keys_all, values_all, query_place, key_place, logsum, attended_grad, row_inner
    )
    key_grad, value_grad = (
        lax.psum_scatter(key_grads, "ctx", scatter_dimension=0, tiled=True),
        lax.psum_scatter(value_grads, "ctx", scatter_dimension=0, tiled=True),
    )
    query_grad = rotate_back(query_grad.reshape(rows, HEADS, HEAD_DIM), cosine, sine)
    key_grad = rotate_back(key_grad, cosine, sine)
    projected_grad = jnp.concatenate(
        [query_grad.reshape(rows, -1), key_grad.reshape(rows, -1), value_grad.reshape(rows, -1)],
        axis=1,
    ).astype(jnp.bfloat16)
    normed_grad = jnp.einsum(
        "re,de->rd", projected_grad, qkv_full, preferred_element_type=jnp.float32
    )
    stream_grad, attn_gain_grad = normalize_back(
        normed_grad, stream, first_factor, attn_full.astype(jnp.float32)
    )
    stream_grad = stream_grad + middle_grad
    qkv_grad = jnp.einsum("rd,re->de", normed, projected_grad, preferred_element_type=jnp.float32)
    out_grad = jnp.einsum("ro,rd->od", attended_low, middle_low, preferred_element_type=jnp.float32)
    gate_up_grad = jnp.einsum(
        "rd,rcf->dcf", second, gate_up_low, preferred_element_type=jnp.float32
    )
    down_grad = jnp.einsum("rf,rd->fd", hidden, upstream_low, preferred_element_type=jnp.float32)
    sharded = (
        lax.psum_scatter(qkv_grad, "fsdp", scatter_dimension=0, tiled=True),
        lax.psum_scatter(out_grad, "fsdp", scatter_dimension=0, tiled=True),
        lax.psum_scatter(gate_up_grad, "fsdp", scatter_dimension=0, tiled=True),
        lax.psum_scatter(down_grad, "fsdp", scatter_dimension=0, tiled=True),
        lax.psum_scatter(attn_gain_grad, "fsdp", scatter_dimension=0, tiled=True),
        lax.psum_scatter(ffn_gain_grad, "fsdp", scatter_dimension=0, tiled=True),
    )
    totals = lax.psum(
        (sharded[0], sharded[1], sharded[2], sharded[3], sharded[4], sharded[5]), "ctx"
    )
    return (stream_grad, totals)


def body(
    tokens,
    positions,
    qkv_weight,
    out_weight,
    gate_up_weight,
    down_weight,
    attn_gain,
    ffn_gain,
    cotangent,
):
    query_place = positions[0]
    key_place = lax.all_gather(query_place, "ctx", axis=0, tiled=True)
    stream = tokens[0].astype(jnp.float32)
    gathered_list = []
    layer_id = 0
    gathered = fetch_layer(
        qkv_weight, out_weight, gate_up_weight, down_weight, attn_gain, ffn_gain, layer_id
    )
    stream, stored = forward_layer(stream, query_place, key_place, gathered)
    saved = [stored]
    gathered_list.append(gathered)
    activations = stream.astype(jnp.bfloat16)[None]
    upstream = cotangent[0]
    layer_grads = [None] * LAYERS
    for layer_id in reversed(range(LAYERS)):
        stored = saved[layer_id]
        gathered = fetch_again(
            qkv_weight, out_weight, gate_up_weight, down_weight, attn_gain, ffn_gain, layer_id
        )
        keys_all, values_all = (stored[6], stored[7])
        upstream, totals = backward_layer(
            upstream, stored, gathered, query_place, key_place, keys_all, values_all
        )
        layer_grads[layer_id] = totals
    outputs = [jnp.stack([entry[slot] for entry in layer_grads], axis=0) for slot in range(6)]
    return (
        activations,
        upstream[None],
        outputs[0],
        outputs[1],
        outputs[2],
        outputs[3],
        outputs[4],
        outputs[5],
    )


def solution(mesh):
    placed = (
        P("fsdp", "ctx", None),
        P("fsdp", "ctx"),
        P(None, "fsdp", None),
        P(None, "fsdp", None),
        P(None, "fsdp", None, None),
        P(None, "fsdp", None),
        P(None, "fsdp"),
        P(None, "fsdp"),
        P("fsdp", "ctx", None),
    )
    return jax.shard_map(
        body,
        mesh=mesh,
        in_specs=placed,
        out_specs=(
            P("fsdp", "ctx", None),
            P("fsdp", "ctx", None),
            P(None, "fsdp", None),
            P(None, "fsdp", None),
            P(None, "fsdp", None, None),
            P(None, "fsdp", None),
            P(None, "fsdp"),
            P(None, "fsdp"),
        ),
        check_vma=False,
    )
```

profile of v0, /device:TPU:0, one launch (start us, length us, event | category | flops | bytes accessed | tf_op | source)
XLA Modules:
  0.0 3518.3 jit_solution(9100462594117412912)
XLA Ops:
  8.0 13.6 all-gather.1
  21.9 157.2 %all-gather.18.cloned.1.call-done = bf16[1,1536,3072]{2,1,0:T(8,128)(2,1)} async-done(((bf16[1,384,3072]{2,1,0:T(8,128)(2,1)}), bf16[1,1536,3072]{2,1,0:T(8,128)(2,1)}) %all-gather.18.cloned.1.call-update) | async-done | bytes 9437200 | tf_op jit(solution)/shard_map/all_gather | solution.py:255
  192.9 10.1 copy.80
  214.2 12.4 all-gather.4
  257.1 67.3 %while.56 = (s32[]{:T(128)}, f32[8,2,96]{2,1,0:T(2,128)S(1)}, f32[8,2,96]{2,1,0:T(2,128)S(1)}, f32[8,2,96]{2,1,0:T(2,128)S(1)}, f32[8,2,96]{2,1,0:T(2,128)S(1)},...) while((s32[]{:T(128)}, f32[8,2,96]{2,1,0:T(2,128)S(1)}, ...), condition=%wide.region_22.23_spmd, body=%wide.region_3.22_spmd.sunk | while | flops 116834496 | bytes 8123657 | solution.py:115
  325.8 80.3 %while.57 = (s32[]{:T(128)}, f32[96,8,2,96]{3,0,2,1:T(8,128)S(1)}, f32[96,8,2,96]{3,0,2,1:T(8,128)S(1)}, s32[8,2,96]{2,1,0:T(2,128)}, s32[]{:T(128)}, /*index=5*...) while((s32[]{:T(128)}, f32[96,8,2,96]{3,0,2,1:T(8,128)S(1)}, ...), condition=%wide.region_34.35_spmd, body=%wide.region_23.34_spmd.sunk | while | flops 229478592 | bytes 9962705 | solution.py:149
  413.2 355.1 %all-gather.22.cloned.1.call-done = bf16[1,1536,2,4096]{3,1,2,0:T(8,128)(2,1)} async-done(((bf16[1,384,2,4096]{3,1,2,0:T(8,128)(2,1)}), bf16[1,1536,2,4096]{3,1,2,0:T(8,128)(2,1)}) %all-gather.22.cloned.1.call-update) | async-done | bytes 25165840 | tf_op jit(solution)/shard_map/all_gather | solution.py:257
  768.3 14.8 fusion.222
  783.1 203.0 %all-gather.24.cloned.1.call-done = bf16[1,4096,1536]{2,1,0:T(8,128)(2,1)} async-done(((bf16[1,1024,1536]{2,1,0:T(8,128)(2,1)}), bf16[1,4096,1536]{2,1,0:T(8,128)(2,1)}) %all-gather.24.cloned.1.call-update) | async-done | bytes 12582928 | tf_op jit(solution)/shard_map/all_gather | solution.py:258
  986.1 14.6 fusion.276
  1000.8 15.8 multiply_reduce_fusion.1
  1029.1 267.2 %while.58 = (s32[]{:T(128)}, f32[96,8,2,96]{3,0,2,1:T(8,128)S(1)}, f32[96,8,2,96]{3,0,2,1:T(8,128)S(1)}, f32[8,192,8,96]{3,2,1,0:T(8,128)}, f32[8,192,8,96]{3,2,...) while((s32[]{:T(128)}, f32[96,8,2,96]{3,0,2,1:T(8,128)S(1)}, ...), condition=%wide.region_48.49_spmd, body=%wide.region_37.48_spmd.sunk | while | flops 572461248 | bytes 36104768 | solution.py:242
  1337.9 39.6 %reduce-scatter.21.cloned.1.call-done = f32[192,768]{1,0:T(8,128)} async-done(((f32[1536,768]{1,0:T(8,128)}), f32[192,768]{1,0:T(8,128)}) %reduce-scatter.21.cloned.1.call-update) | async-done | bytes 589840
  1379.6 55.1 %reduce-scatter.19.cloned.1.call-done = f32[192,768]{1,0:T(8,128)} async-done(((f32[1536,768]{1,0:T(8,128)}), f32[192,768]{1,0:T(8,128)}) %reduce-scatter.19.cloned.1.call-update) | async-done | bytes 589840
  1450.7 14.0 fusion.272
  1466.1 21.6 fusion.264
  1487.7 111.2 %reduce-scatter.13.cloned.1.call-done = f32[384,1536]{1,0:T(8,128)} async-done(((f32[1536,1536]{1,0:T(8,128)}), f32[384,1536]{1,0:T(8,128)}) %reduce-scatter.13.cloned.1.call-update) | async-done | bytes 2359312 | tf_op jit(solution)/shard_map/reduce_scatter | solution.py:404
  1598.9 317.1 %reduce-scatter.11.cloned.1.call-done = f32[384,3072]{1,0:T(8,128)} async-done(((f32[1536,3072]{1,0:T(8,128)}), f32[384,3072]{1,0:T(8,128)}) %reduce-scatter.11.cloned.1.call-update) | async-done | bytes 4718608 | tf_op jit(solution)/shard_map/reduce_scatter | solution.py:403
  1916.0 417.6 %reduce-scatter.17.cloned.1.call-done = f32[1024,1536]{1,0:T(8,128)} async-done(((f32[4096,1536]{1,0:T(8,128)}), f32[1024,1536]{1,0:T(8,128)}) %reduce-scatter.17.cloned.1.call-update) | async-done | bytes 6291472 | tf_op jit(solution)/shard_map/reduce_scatter | solution.py:406
  2333.6 825.0 %reduce-scatter.15.cloned.1.call-done = f32[384,2,4096]{2,0,1:T(8,128)} async-done(((f32[1536,2,4096]{2,0,1:T(8,128)}), f32[384,2,4096]{2,0,1:T(8,128)}) %reduce-scatter.15.cloned.1.call-update) | async-done | bytes 12582928 | tf_op jit(solution)/shard_map/reduce_scatter | solution.py:405
  3178.1 19.3 all-reduce.5
  3197.6 13.3 all-reduce.3
  3212.3 268.4 %all-reduce.8.cloned.1.call-done = (f32[1,384,3072]{2,1,0:T(8,128)}, f32[1,384,1536]{2,1,0:T(8,128)}, f32[1,384,2,4096]{3,1,2,0:T(8,128)}, f32[1,1024,1536]{2,1,0:T(8,128)}) async-done(((f32[1,384,3072]{2,1,0:T(8,128)}, f32[1,384,1536]{2,1,0:T(8,128)}, f32[1,384,2,4096]{3,1,2,0:T(8,128)}, f32[1,1024,1536]{2,1,0:T(8,128)}), (f32[1,384,3072]{2,1,0:T(8,128)}, f32[1,384,1536]{2,1,0:T(8,128)}, ...) | async-done | bytes 25952272 | tf_op jit(solution)/shard_map/psum | solution.py:410
  3480.7 22.1 copy.95
  (845 shorter events, 633.3 us)
Async XLA Ops:
  7.2 14.5 copy-start.4
  7.2 171.9 %all-gather.18.cloned.1.call-start = ((), (), s32[]{:S(2)}) async-start(), calls=%async_computation.12 | async-start | bytes 11796480 | tf_op jit(solution)/shard_map/all_gather | solution.py:255
  7.9 238.1 %all-gather.16.cloned.1.call-start = ((), (), s32[]{:S(2)}) async-start(), calls=%async_computation.7 | async-start | bytes 3538944 | tf_op jit(solution)/shard_map/all_gather | solution.py:299
  21.6 163.2 %copy-start.38 = (f32[1536]{0:T(1024)}, f32[1536]{0:T(1024)S(1)}, u32[]{:S(2)}) copy-start(f32[1536]{0:T(1024)S(1)} %convert_reduce_fusion.1) | copy-start | bytes 18436
  21.9 163.0 %copy-start.43 = (f32[192]{0:T(256)}, f32[192]{0:T(256)S(1)}, u32[]{:S(2)}) copy-start(f32[192]{0:T(256)S(1)} %add_rsqrt_fusion.1) | copy-start | bytes 2308
  187.5 65.3 %all-gather.14.cloned.1.call-start = ((), (), s32[]{:S(2)}) async-start(), calls=%async_computation.6 | async-start | bytes 3538944 | tf_op jit(solution)/shard_map/all_gather | solution.py:298
  192.3 217.1 %all-gather.20.cloned.1.call-start = ((), (), s32[]{:S(2)}) async-start(), calls=%async_computation.13 | async-start | bytes 5898240 | tf_op jit(solution)/shard_map/all_gather | solution.py:256
  192.8 575.5 %all-gather.22.cloned.1.call-start = ((), (), s32[]{:S(2)}) async-start(), calls=%async_computation.14 | async-start | bytes 31457280 | tf_op jit(solution)/shard_map/all_gather | solution.py:257
  203.1 11.1 copy-start.48
  203.1 783.0 %all-gather.24.cloned.1.call-start = ((), (), s32[]{:S(2)}) async-start(), calls=%async_computation.15 | async-start | bytes 15728640 | tf_op jit(solution)/shard_map/all_gather | solution.py:258
  203.7 1173.8 %reduce-scatter.21.cloned.1.call-start = ((), (), s32[]{:S(2)}) async-start(), calls=%async_computation.17 | async-start | bytes 5308416
  409.4 358.9 %copy-start.33 = (f32[1536]{0:T(1024)S(1)}, f32[1536]{0:T(1024)}, u32[]{:S(2)}) copy-start(f32[1536]{0:T(1024)} %convert_reduce_fusion) | copy-start | bytes 18436
  413.1 603.4 %copy-start = (f32[192,1536]{1,0:T(8,128)}, f32[192,1536]{1,0:T(8,128)S(1)}, u32[]{:S(2)}) copy-start(f32[192,1536]{1,0:T(8,128)S(1)} %get-tuple-element.973) | copy-start | bytes 3538948
  413.1 603.4 %copy-start.41 = (f32[192]{0:T(256)}, f32[192]{0:T(256)S(1)}, u32[]{:S(2)}) copy-start(f32[192]{0:T(256)S(1)} %add_rsqrt_fusion) | copy-start | bytes 2308
  768.3 217.8 %copy-start.14 = (f32[1,192,1536]{2,1,0:T(8,128)S(1)}, f32[1,192,1536]{2,1,0:T(8,128)}, u32[]{:S(2)}) copy-start(f32[1,192,1536]{2,1,0:T(8,128)} %param.47) | copy-start | bytes 3538948
  1304.1 130.6 %reduce-scatter.19.cloned.1.call-start = ((), (), s32[]{:S(2)}) async-start(), calls=%async_computation.16 | async-start | bytes 5308416
  1311.6 287.3 %reduce-scatter.13.cloned.1.call-start = ((), (), s32[]{:S(2)}) async-start(), calls=%async_computation.9 | async-start | bytes 11796480 | tf_op jit(solution)/shard_map/reduce_scatter | solution.py:404
  1318.2 597.9 %reduce-scatter.11.cloned.1.call-start = ((), (), s32[]{:S(2)}) async-start(), calls=%async_computation.8 | async-start | bytes 23592960 | tf_op jit(solution)/shard_map/reduce_scatter | solution.py:403
  1379.6 56.9 %copy-start.25 = (f32[192,96]{1,0:T(8,128)S(1)}, f32[192,96]{1,0:T(8,128)}, u32[]{:S(2)}) copy-start(f32[192,96]{1,0:T(8,128)} %copy-done.23) | copy-start | bytes 221188
  1449.5 884.1 %reduce-scatter.17.cloned.1.call-start = ((), (), s32[]{:S(2)}) async-start(), calls=%async_computation.11 | async-start | bytes 31457280 | tf_op jit(solution)/shard_map/reduce_scatter | solution.py:406
  1464.8 1693.8 %reduce-scatter.15.cloned.1.call-start = ((), (), s32[]{:S(2)}) async-start(), calls=%async_computation.10 | async-start | bytes 62914560 | tf_op jit(solution)/shard_map/reduce_scatter | solution.py:405
  1487.7 1993.0 %all-reduce.8.cloned.1.call-start = ((), (), s32[]{:S(2)}) async-start(), calls=%async_computation.18 | async-start | bytes 51904512 | tf_op jit(solution)/shard_map/psum | solution.py:410
  3480.7 22.1 slice-start
  3480.7 22.1 slice-start.1
  (70 other events, 228.9 us)
Sparse Core Ops, SparseCore 0:
  9.6 169.4 all-gather.17
  187.6 30.6 all-gather.15
  220.8 32.0 all-gather.13
  254.3 89.3 all-gather.19
  345.7 422.5 all-gather.21
  769.7 216.3 all-gather.23
  1304.2 73.1 reduce-scatter.20
  1380.9 53.7 reduce-scatter.18
  1437.7 161.1 reduce-scatter.12
  1601.1 314.8 reduce-scatter.10
  1918.4 415.1 reduce-scatter.16
  2335.8 822.7 reduce-scatter.14
  3163.0 317.6 all-reduce.7
where the time goes:
time: 3530 us; the launch traced here: 3520 us
  waiting for transfers between devices  2750 us (78%)
  matrix products  257 us (7%)
  local copies, waits for them, and re-layouts  235 us (7%)
  loops' own time  124 us (4%)
  blocking collectives  67.3 us (2%)
  other arithmetic  64.4 us (2%)
    reduce_scatter x1, waiting for transfers between devices, backward_layer(): lax.psum_scatter(gate_up_grad, 'fsdp', scatter_dimension=0, tiled=True)  825 us
    reduce_scatter x1, waiting for transfers between devices, backward_layer(): lax.psum_scatter(down_grad, 'fsdp', scatter_dimension=0, tiled=True)  418 us
    all_gather x1, waiting for transfers between devices, fetch_layer(): lax.all_gather(gate_up_weight[layer_id], 'fsdp', axis=0, tiled=True)  355 us
    reduce_scatter x1, waiting for transfers between devices, backward_layer(): lax.psum_scatter(qkv_grad, 'fsdp', scatter_dimension=0, tiled=True)  317 us
    psum x1, waiting for transfers between devices, backward_layer(): lax.psum((sharded[0], sharded[1], sharded[2], sharded[3], sharded[4], sha...  268 us
    all_gather x1, waiting for transfers between devices, fetch_layer(): lax.all_gather(down_weight[layer_id], 'fsdp', axis=0, tiled=True)  203 us
    all_gather x1, waiting for transfers between devices, fetch_layer(): lax.all_gather(qkv_weight[layer_id], 'fsdp', axis=0, tiled=True)  157 us
    reduce_scatter x1, waiting for transfers between devices, backward_layer(): lax.psum_scatter(out_grad, 'fsdp', scatter_dimension=0, tiled=True)  111 us
  transfers between devices with their start and end apart: 13, of which 11 were waited for; matrix products, arithmetic and copies ran while one was open for 7% of the time, Pallas kernels for 0%

commit v1 on v0

--- a/solution.py
+++ b/solution.py
@@ -1,6 +1,9 @@
+import functools
 import jax
 import jax.numpy as jnp
 from jax import lax
+from jax.experimental import pallas as pl
+from jax.experimental.pallas import tpu as pltpu
 from jax.sharding import PartitionSpec as P
 
 HEADS = 16
@@ -461,7 +464,923 @@
     )
 
 
+LANES = 128
+
+
+def spread(heads):
+    half = HEAD_DIM // 2
+    pad = ((0, 0), (0, 0), (0, 64 - half))
+    return jnp.concatenate([jnp.pad(heads[..., :half], pad), jnp.pad(heads[..., half:], pad)], axis=-1)
+
+
+def gathered_spread(padded):
+    half = HEAD_DIM // 2
+    return jnp.concatenate([padded[..., :half], padded[..., 64 : 64 + half]], axis=-1)
+
+
+def tables(length):
+    half = HEAD_DIM // 2
+    frequency = rope_base ** (-(jnp.arange(half, dtype=jnp.float32) * 2.0 / HEAD_DIM))
+    phases = jnp.arange(length, dtype=jnp.float32)[:, None] * frequency[None, :]
+    pad = ((0, 0), (0, 64 - half))
+    cosine = jnp.pad(jnp.cos(phases), pad)
+    sine = jnp.pad(jnp.sin(phases), pad)
+    return (
+        jnp.concatenate([cosine, cosine], axis=1),
+        jnp.concatenate([-sine, sine], axis=1),
+    )
+
+
+def nt(left, right):
+    return lax.dot_general(left, right, (((1,), (1,)), ((), ())), preferred_element_type=jnp.float32)
+
+
+def nn(left, right):
+    return lax.dot_general(left, right, (((1,), (0,)), ((), ())), preferred_element_type=jnp.float32)
+
+
+def tn(left, right):
+    return lax.dot_general(left, right, (((0,), (0,)), ((), ())), preferred_element_type=jnp.float32)
+
+
+def causal(width):
+    key_at = lax.broadcasted_iota(jnp.int32, (width, 2 * width), 0)
+    query_at = lax.broadcasted_iota(jnp.int32, (width, 2 * width), 1)
+    query_at = jnp.where(query_at >= width, query_at - width, query_at)
+    return key_at <= query_at
+
+
+def attend_kernel(
+    span, tok_ref, gain_ref, w_ref, cos_ref, sin_ref,
+    normed_ref, q_ref, k_ref, v_ref, att_ref, low_ref, lse_ref,
+):
+    length = tok_ref.shape[0]
+    half = 96
+    pairs = length // (2 * half)
+    step = 2 * 2 * half
+    lane = lax.broadcasted_iota(jnp.int32, (half, LANES), 1)
+    for chunk in range(length // step):
+        rows = pl.ds(chunk * step, step)
+        x = tok_ref[rows, :].astype(jnp.float32)
+        factor = lax.rsqrt(jnp.mean(x * x, axis=-1, keepdims=True) + epsilon)
+        normed = (x * factor * gain_ref[...]).astype(jnp.bfloat16)
+        normed_ref[rows, :] = normed
+        proj = nn(normed, w_ref[...])
+        for piece in range(step // half):
+            at = span[chunk * (step // half) + piece]
+            spot = pl.multiple_of(at * half, half)
+            cosine = cos_ref[pl.ds(spot, half), :]
+            sine = sin_ref[pl.ds(spot, half), :]
+            mine = proj[piece * half : (piece + 1) * half]
+
+            def turned(part):
+                z = mine[:, part * LANES : (part + 1) * LANES]
+                return (z * cosine + pltpu.roll(z, 64, 1) * sine).astype(jnp.bfloat16)
+
+            base = (at // 2) * (4 * half) + (at % 2) * half
+            q_ref[pl.ds(pl.multiple_of(base, half), half), :] = turned(0)
+            q_ref[pl.ds(pl.multiple_of(base + 2 * half, half), half), :] = turned(1)
+            k_ref[pl.ds(spot, half), :] = turned(2)
+            v_ref[pl.ds(spot, half), :] = mine[:, 3 * LANES :].astype(jnp.bfloat16)
+    scaling = HEAD_DIM ** (-0.5)
+    mask = causal(2 * half)
+    values_t = v_ref[...].astype(jnp.float32).T.astype(jnp.bfloat16)
+    for pair in range(pairs):
+        width = (pair + 1) * 2 * half
+        q = q_ref[pl.ds(pair * 4 * half, 4 * half), :]
+        scores = nt(k_ref[pl.ds(0, width), :], q) * scaling
+        last = jnp.where(mask, scores[width - 2 * half :], -1e30)
+        scores = last if pair == 0 else jnp.concatenate([scores[: width - 2 * half], last], axis=0)
+        top = jnp.max(scores, axis=0, keepdims=True)
+        e = jnp.exp(scores - top)
+        total = jnp.sum(e, axis=0, keepdims=True)
+        weights = (e * (1.0 / total)).astype(jnp.bfloat16)
+        lse_ref[pl.ds(pair, 1), :] = top + jnp.log(total)
+        out_t = nn(values_t[:, :width], weights)
+        att_ref[pl.ds(pair * LANES, LANES), :] = out_t
+        out = out_t.T.astype(jnp.bfloat16).astype(jnp.float32)
+        for part in range(2):
+            at = span[2 * pairs + 2 * pair + part]
+            first = out[part * half : (part + 1) * half]
+            second = pltpu.roll(out[(2 + part) * half : (3 + part) * half], half, 1)
+            spot = pl.ds(pl.multiple_of(at * half, half), half)
+            low_ref[spot, 0:LANES] = jnp.where(lane < half, first, second).astype(jnp.bfloat16)
+            low_ref[spot, LANES : 2 * half] = second[:, : 2 * half - LANES].astype(jnp.bfloat16)
+
+
+def back_kernel(
+    span, grad_ref, q_ref, k_ref, v_ref, att_ref, lse_ref, cos_ref, sin_ref,
+    out_ref, dk_ref, dv_ref,
+):
+    length = k_ref.shape[0]
+    half = 96
+    pairs = length // (2 * half)
+    scaling = HEAD_DIM ** (-0.5)
+    mask = causal(2 * half)
+    lane = lax.broadcasted_iota(jnp.int32, (half, LANES), 1)
+    keys_t = k_ref[...].astype(jnp.float32).T.astype(jnp.bfloat16)
+    for pair in reversed(range(pairs)):
+        width = (pair + 1) * 2 * half
+        q = q_ref[pl.ds(pair * 4 * half, 4 * half), :]
+        firsts, seconds = [], []
+        for part in range(2):
+            at = span[2 * pairs + 2 * pair + part]
+            rows = pl.ds(pl.multiple_of(at * half, half), half)
+            left = grad_ref[rows, 0:LANES].astype(jnp.float32)
+            right = jnp.concatenate(
+                [grad_ref[rows, LANES : 2 * half].astype(jnp.float32), jnp.zeros((half, 64), jnp.float32)], axis=1
+            )
+            firsts.append(jnp.where(lane < half, left, 0.0))
+            seconds.append(pltpu.roll(jnp.where(lane < half, right, left), LANES - half, 1))
+        seconds = [jnp.where(lane < half, s, 0.0) for s in seconds]
+        grads = jnp.concatenate(firsts + seconds, axis=0)
+        delta = jnp.sum(grads.T * att_ref[pl.ds(pair * LANES, LANES), :], axis=0, keepdims=True)
+        grads = grads.astype(jnp.bfloat16)
+        keys = k_ref[pl.ds(0, width), :]
+        weights = jnp.exp(nt(keys, q) * scaling - lse_ref[pl.ds(pair, 1), :])
+        last = jnp.where(mask, weights[width - 2 * half :], 0.0)
+        weights = last if pair == 0 else jnp.concatenate([weights[: width - 2 * half], last], axis=0)
+        dp = nt(v_ref[pl.ds(0, width), :], grads)
+        ds = (weights * (dp - delta)).astype(jnp.bfloat16)
+        dk = nn(ds, q) * scaling
+        dv = nn(weights.astype(jnp.bfloat16), grads)
+        if pair == pairs - 1:
+            dk_ref[...] = dk
+            dv_ref[...] = dv
+        else:
+            dk_ref[pl.ds(0, width), :] += dk
+            dv_ref[pl.ds(0, width), :] += dv
+        dq = nn(keys_t[:, :width], ds).T * scaling
+        for part in range(2):
+            at = span[2 * pairs + 2 * pair + part]
+            rows = pl.ds(pl.multiple_of(at * half, half), half)
+            spot = pl.ds((2 * pair + part) * half, half)
+            cosine, sine = cos_ref[spot, :], sin_ref[spot, :]
+            for head in range(2):
+                z = dq[(2 * head + part) * half : (2 * head + part + 1) * half]
+                out_ref[rows, head * LANES : (head + 1) * LANES] = (
+                    z * cosine - pltpu.roll(z, 64, 1) * sine
+                ).astype(jnp.bfloat16)
+    for block in range(2 * pairs):
+        at = span[2 * pairs + block]
+        rows = pl.ds(pl.multiple_of(at * half, half), half)
+        spot = pl.ds(block * half, half)
+        z = dk_ref[spot, :]
+        out_ref[rows, 2 * LANES : 3 * LANES] = (
+            z * cos_ref[spot, :] - pltpu.roll(z, 64, 1) * sin_ref[spot, :]
+        ).astype(jnp.bfloat16)
+        out_ref[rows, 3 * LANES :] = dv_ref[spot, :].astype(jnp.bfloat16)
+
+
+def vm(count):
+    return [pl.BlockSpec(memory_space=pltpu.VMEM)] * count
+
+
+MESH = pl.DeviceIdType.MESH
+
+
+class Place:
+    def __init__(self):
+        self.me = lax.axis_index("ctx")
+        core, x, y = self.me % 2, (self.me // 2) % 2, self.me // 4
+        self.dp, self.dx, self.dy = 1 - 2 * core, 2 - 4 * x, 4 - 8 * y
+        self.p, self.x, self.y = self.me + self.dp, self.me + self.dx, self.me + self.dy
+        self.d = self.x + self.dy
+        self.z = lax.axis_index("fsdp")
+        self.planes = lax.axis_size("fsdp")
+        self.n = lax.axis_size("ctx")
+
+
+def greet(place, ctx=True, planes=False):
+    barrier = pltpu.get_barrier_semaphore()
+    count = 0
+    if ctx:
+        for step in range(1, place.n):
+            pl.semaphore_signal(
+                barrier, inc=1, device_id={"ctx": lax.rem(place.me + step, place.n)}, device_id_type=MESH
+            )
+            count += 1
+    if planes:
+        for step in range(1, place.planes):
+            pl.semaphore_signal(
+                barrier, inc=1, device_id={"fsdp": lax.rem(place.z + step, place.planes)}, device_id_type=MESH
+            )
+            count += 1
+    pl.semaphore_wait(barrier, count)
+
+
+def send(source, target, send_sem, recv_sem, **where):
+    return pltpu.make_async_remote_copy(
+        src_ref=source, dst_ref=target, send_sem=send_sem, recv_sem=recv_sem,
+        device_id=where, device_id_type=MESH,
+    )
+
+
+class Gather:
+    sems = 14
+
+    def __init__(self, place, own, out, sem):
+        self.place, self.own, self.out, self.sem = place, own, out, sem
+        self.half = out.shape[1] // 2
+        self.started = []
+        self.met = False
+
+    def go(self, source, target, index, rank):
+        copy = send(source, target, self.sem.at[0, index], self.sem.at[1, index], ctx=rank)
+        copy.start()
+        self.started.append(copy)
+
+    def part(self, rank, half):
+        return self.out.at[rank, pl.ds(half * self.half, self.half)]
+
+    def start(self):
+        p = self.place
+        keep = pltpu.make_async_copy(self.own, self.out.at[p.me], self.sem.at[0, 13])
+        keep.start()
+        self.keep = keep
+        halves = [self.own.at[pl.ds(h * self.half, self.half)] for h in range(2)]
+        self.go(halves[0], self.part(p.me, 0), 0, p.x)
+        self.go(halves[1], self.part(p.me, 1), 3, p.y)
+        self.go(self.own, self.out.at[p.me], 6, p.p)
+        self.go(halves[1], self.part(p.me, 1), 1, p.x)
+        self.go(halves[0], self.part(p.me, 0), 2, p.y)
+
+    def arrived(self, rank, half, index):
+        part = self.part(rank, half)
+        pltpu.make_async_copy(part, part, self.sem.at[1, index]).wait()
+        return part
+
+    def relay(self):
+        p = self.place
+        part = self.arrived(p.x, 0, 0)
+        self.go(part, part, 4, p.y)
+        self.go(part, part, 7, p.p)
+        part = self.arrived(p.y, 1, 3)
+        self.go(part, part, 5, p.x)
+        self.go(part, part, 10, p.p)
+
+    def rest(self):
+        p = self.place
+        for rank, half, index, onward in ((p.x, 1, 1, 8), (p.y, 0, 2, 9), (p.d, 0, 4, 11), (p.d, 1, 5, 12)):
+            part = self.arrived(rank, half, index)
+            self.go(part, part, onward, p.p)
+
+    def first_partner(self):
+        part = self.out.at[self.place.p]
+        pltpu.make_async_copy(part, part, self.sem.at[1, 6]).wait()
+        self.met = True
+
+    def partner(self):
+        p = self.place
+        if not self.met:
+            self.first_partner()
+        for rank, half, index in (
+            (p.x, 0, 7), (p.y, 1, 10), (p.x, 1, 8), (p.y, 0, 9), (p.d, 0, 11), (p.d, 1, 12),
+        ):
+            self.arrived(rank + p.dp, half, index)
+
+    def finish(self, kept=False):
+        if not kept:
+            self.keep.wait()
+        for copy in self.started:
+            copy.wait_send()
+
+
+class PlaneGather:
+    def __init__(self, place, own, out, sem):
+        self.place, self.own, self.out, self.sem = place, own, out, sem
+
+    def hop(self, step, up):
+        p = self.place
+        sign = 1 if up else -1
+        source = p.z - sign * step
+        target = p.z + sign
+        ok = jnp.logical_and(
+            jnp.logical_and(source >= 0, source < p.planes),
+            jnp.logical_and(target >= 0, target < p.planes),
+        )
+        source = jnp.clip(source, 0, p.planes - 1)
+        target = jnp.clip(target, 0, p.planes - 1)
+        block = self.own if step == 0 else self.out.at[source]
+        return ok, send(
+            block, self.out.at[source], self.sem.at[0 if up else 1, source], self.sem.at[2, source], fsdp=target
+        )
+
+    def start(self):
+        p = self.place
+        self.keep = pltpu.make_async_copy(self.own, self.out.at[p.z], self.sem.at[2, p.z])
+        self.keep.start()
+        for up in (True, False):
+            ok, copy = self.hop(0, up)
+            pl.when(ok)(copy.start)
+
+    def got(self, step, up):
+        p = self.place
+        source = p.z - step if up else p.z + step
+        ok = jnp.logical_and(source >= 0, source < p.planes)
+        source = jnp.clip(source, 0, p.planes - 1)
+        part = self.out.at[source]
+        return ok, pltpu.make_async_copy(part, part, self.sem.at[2, source])
+
+    def step(self, number):
+        for up in (True, False):
+            ok, copy = self.got(number, up)
+            pl.when(ok)(copy.wait)
+            if number < self.place.planes - 1:
+                ok, copy = self.hop(number, up)
+                pl.when(ok)(copy.start)
+
+    def finish(self):
+        self.keep.wait()
+        for number in range(self.place.planes - 1):
+            for up in (True, False):
+                ok, copy = self.hop(number, up)
+                pl.when(ok)(copy.wait_send)
+
+
+class Exchange:
+    def __init__(self, place, blocks, out, sem):
+        self.place, self.blocks, self.out, self.sem = place, blocks, out, sem
+
+    def pick(self, rank):
+        return self.blocks.at[rank]
+
+    def copy(self, step):
+        p = self.place
+        rank = lax.rem(p.me + step, p.n)
+        return send(self.pick(rank), self.out.at[p.me], self.sem.at[0, step], self.sem.at[1, step], ctx=rank)
+
+    def start(self):
+        p = self.place
+        for step in range(1, p.n):
+            self.copy(step).start()
+        self.keep = pltpu.make_async_copy(self.pick(p.me), self.out.at[p.me], self.sem.at[0, 0])
+        self.keep.start()
+
+    def finish(self):
+        p = self.place
+        self.keep.wait()
+        for step in range(1, p.n):
+            self.copy(step).wait_send()
+        for step in range(1, p.n):
+            part = self.out.at[lax.rem(p.me + p.n - step, p.n)]
+            pltpu.make_async_copy(part, part, self.sem.at[1, step]).wait()
+
+
+class Share(Exchange):
+    def pick(self, rank):
+        return self.blocks
+
+
+class PlaneShare:
+    def __init__(self, place, block, out, sem):
+        self.place, self.block, self.out, self.sem = place, block, out, sem
+
+    def copy(self, step):
+        p = self.place
+        plane = lax.rem(p.z + step, p.planes)
+        return send(self.block, self.out.at[p.z], self.sem.at[0, step], self.sem.at[1, step], fsdp=plane)
+
+    def start(self):
+        p = self.place
+        for step in range(1, p.planes):
+            self.copy(step).start()
+        self.keep = pltpu.make_async_copy(self.block, self.out.at[p.z], self.sem.at[0, 0])
+        self.keep.start()
+
+    def finish(self):
+        p = self.place
+        self.keep.wait()
+        for step in range(1, p.planes):
+            self.copy(step).wait_send()
+        for step in range(1, p.planes):
+            part = self.out.at[lax.rem(p.z + p.planes - step, p.planes)]
+            pltpu.make_async_copy(part, part, self.sem.at[1, step]).wait()
+
+
+def anywhere(count):
+    return [pl.BlockSpec(memory_space=pl.ANY)] * count
+
+
+def first_kernel(tok, up, qkv, out_block, spot, gains, tok_all, up_all, qkv_all, out_all, spots, gain_all, *sems):
+    place = Place()
+    greet(place, planes=True)
+    tokens = Gather(place, tok, tok_all, sems[0])
+    cots = Gather(place, up, up_all, sems[1])
+    qkvs = PlaneGather(place, qkv, qkv_all, sems[2])
+    outs = PlaneGather(place, out_block, out_all, sems[3])
+    spans = Share(place, spot, spots, sems[4])
+    scales = PlaneShare(place, gains, gain_all, sems[5])
+    spans.start()
+    scales.start()
+    qkvs.start()
+    tokens.start()
+    tokens.relay()
+    qkvs.step(1)
+    cots.start()
+    qkvs.step(2)
+    outs.start()
+    tokens.rest()
+    qkvs.step(3)
+    tokens.partner()
+    outs.step(1)
+    cots.relay()
+    outs.step(2)
+    cots.rest()
+    outs.step(3)
+    cots.partner()
+    for move in (spans, scales, qkvs, tokens, cots, outs):
+        move.finish()
+
+
+def first_moves(tok, up, qkv, out_block, spot, gains):
+    n, planes = lax.axis_size("ctx"), lax.axis_size("fsdp")
+    shape = lambda count, x: jax.ShapeDtypeStruct((count,) + x.shape, x.dtype)
+    dma = pltpu.SemaphoreType.DMA
+    return pl.pallas_call(
+        first_kernel,
+        out_shape=(
+            shape(n, tok), shape(n, up), shape(planes, qkv), shape(planes, out_block), shape(n, spot), shape(planes, gains)
+        ),
+        in_specs=vm(6),
+        out_specs=anywhere(6),
+        scratch_shapes=[
+            dma((2, Gather.sems)), dma((2, Gather.sems)), dma((3, planes)), dma((3, planes)), dma((2, n)), dma((2, planes)),
+        ],
+        compiler_params=pltpu.CompilerParams(collective_id=1, has_side_effects=True),
+        name="first_moves",
+    )(tok, up, qkv, out_block, spot, gains)
+
+
+class Reduce:
+    sems = 10
+
+    def __init__(self, place, mine, theirs, first, out, second, sem):
+        self.place, self.mine, self.theirs, self.first, self.out, self.second, self.sem = (
+            place, mine, theirs, first, out, second, sem
+        )
+        self.half = out.shape[1]
+        self.started = []
+
+    def push(self, slot):
+        copy = send(
+            self.theirs.at[slot], self.first.at[slot], self.sem.at[0, slot], self.sem.at[1, slot], ctx=self.place.p
+        )
+        copy.start()
+        return copy
+
+    def pushed(self):
+        for slot in range(4):
+            send(
+                self.theirs.at[slot], self.first.at[slot], self.sem.at[0, slot], self.sem.at[1, slot],
+                ctx=self.place.p,
+            ).wait_send()
+
+    def add(self, slot):
+        part = self.first.at[slot]
+        pltpu.make_async_copy(part, part, self.sem.at[1, slot]).wait()
+        self.mine[slot] = self.mine[slot] + self.first[slot].astype(jnp.float32)
+
+    def go(self, index, value, rank):
+        self.out[index] = value.astype(jnp.bfloat16)
+        copy = send(
+            self.out.at[index], self.second.at[index], self.sem.at[0, 4 + index], self.sem.at[1, 4 + index], ctx=rank
+        )
+        copy.start()
+        self.started.append(copy)
+
+    def top(self, slot):
+        return self.mine[slot, pl.ds(0, self.half), :]
+
+    def low(self, slot):
+        return self.mine[slot, pl.ds(self.half, self.half), :]
+
+    def got(self, index):
+        part = self.second.at[index]
+        pltpu.make_async_copy(part, part, self.sem.at[1, 4 + index]).wait()
+        return self.second[index].astype(jnp.float32)
+
+    def across(self):
+        self.add(3)
+        self.go(1, self.top(3), self.place.x)
+        self.go(3, self.low(3), self.place.y)
+
+    def beside(self):
+        self.add(1)
+        self.go(0, self.top(1), self.place.x)
+        self.add(2)
+        self.go(2, self.low(2), self.place.y)
+
+    def turn(self):
+        self.go(4, self.top(2) + self.got(1), self.place.y)
+        self.go(5, self.low(1) + self.got(3), self.place.x)
+
+    def total(self):
+        self.add(0)
+        upper = self.top(0) + self.got(0) + self.got(4)
+        lower = self.low(0) + self.got(2) + self.got(5)
+        return jnp.concatenate([upper, lower], axis=0)
+
+    def finish(self):
+        self.pushed()
+        for copy in self.started:
+            copy.wait_send()
+
+
+def flip(place, i):
+    return place.me + (i % 2) * place.dp + ((i // 2) % 2) * place.dx + (i // 4) * place.dy
+
+
+def middle_kernel(
+    low, tok, up, up_all, out_w, gu_w, down_w, gain,
+    second_all, hidden, gul, agrad, mcols, middle_grad, result, gain_grad,
+    attended, own, middle, agrad_send, mcols_send, mine, theirs, first, out, second, theirs2, first2, out2, second2,
+    low_sem, gather_sem, reduce_sem, reduce_sem2, agrad_sem, mcols_sem,
+):
+    place = Place()
+    n = place.n
+    rows = tok.shape[0]
+    heads = rows
+    greet(place)
+    moved = Exchange(place, low, attended, low_sem)
+    moved.start()
+    moved.finish()
+    total = tok[...].astype(jnp.float32)
+    for q in range(8):
+        total = total + nn(attended[q], out_w[pl.ds(q * heads, heads), :])
+    middle[...] = total
+    factor = lax.rsqrt(jnp.mean(total * total, axis=-1, keepdims=True) + epsilon)
+    own[...] = (total * factor * gain[...]).astype(jnp.bfloat16)
+    seconds = Gather(place, own, second_all, gather_sem)
+    seconds.start()
+    grads = Reduce(place, mine, theirs, first, out, second, reduce_sem)
+    wide = hidden.shape[2]
+
+    def block(i, block_of):
+        rank = flip(place, i)
+        gate_up = nn(block_of(rank), gu_w[...])
+        gate, raised = gate_up[:, :wide], gate_up[:, wide:]
+        sigmoid = 1.0 / (1.0 + jnp.exp(-gate))
+        silu = gate * sigmoid
+        hidden[rank] = (silu * raised).astype(jnp.bfloat16)
+        hidden_grad = nt(up_all[rank], down_w[...])
+        gul[rank, :, pl.ds(0, wide)] = (hidden_grad * raised * sigmoid * (1.0 + gate * (1.0 - sigmoid))).astype(jnp.bfloat16)
+        gul[rank, :, pl.ds(wide, wide)] = (hidden_grad * silu).astype(jnp.bfloat16)
+        return nt(gul[rank], gu_w[...])
+
+    def pair(k, carry):
+        theirs[k] = block(2 * k + 1, lambda rank: second_all[rank]).astype(jnp.bfloat16)
+        grads.push(k)
+        mine[k] = block(2 * k, lambda rank: second_all[rank])
+        return carry
+
+    seconds.relay()
+    seconds.keep.wait()
+    seconds.first_partner()
+    pair(0, 0)
+    seconds.rest()
+    seconds.partner()
+    lax.fori_loop(1, 3, pair, 0)
+    grads.beside()
+    pair(3, 0)
+    grads.across()
+
+    sums = Reduce(place, mine, theirs2, first2, out2, second2, reduce_sem2)
+
+    def other(k, carry):
+        theirs2[k] = nn(hidden[flip(place, 2 * k + 1)], down_w[...]).astype(jnp.bfloat16)
+        sums.push(k)
+        return carry
+
+    lax.fori_loop(0, 2, other, 0)
+    grads.turn()
+    lax.fori_loop(2, 4, other, 0)
+    second_grad = grads.total()
+    x = middle[...]
+    factor = lax.rsqrt(jnp.mean(x * x, axis=-1, keepdims=True) + epsilon)
+    unit = x * factor
+    gain_grad[...] = jnp.sum(second_grad * unit, axis=0, keepdims=True)
+    scaled = second_grad * gain[...]
+    inner = jnp.mean(scaled * unit, axis=-1, keepdims=True)
+    grad = up[...] + factor * (scaled - unit * inner)
+    middle_grad[...] = grad
+    rounded = grad.astype(jnp.bfloat16)
+    seconds.finish(kept=True)
+    own[...] = rounded
+    for q in range(8):
+        mcols_send[q] = rounded[:, q * heads : (q + 1) * heads]
+
+    def head_grads(q, carry):
+        agrad_send[q] = nt(own[...], out_w[pl.ds(pl.multiple_of(q * heads, heads), heads), :]).astype(jnp.bfloat16)
+        return carry
+
+    lax.fori_loop(0, n, head_grads, 0)
+    heads_back = Exchange(place, agrad_send, agrad, agrad_sem)
+    heads_back.start()
+    columns = Exchange(place, mcols_send, mcols, mcols_sem)
+    columns.start()
+
+    def ours(k, carry):
+        mine[k] = nn(hidden[flip(place, 2 * k)], down_w[...])
+        return carry
+
+    lax.fori_loop(0, 4, ours, 0)
+    sums.across()
+    sums.beside()
+    sums.turn()
+    result[...] = (middle[...] + sums.total()).astype(jnp.bfloat16)
+    heads_back.finish()
+    columns.finish()
+    grads.finish()
+    sums.finish()
+
+
+def middle_moves(low, tok, up, up_all, out_w, gu_w, down_w, gain):
+    n = lax.axis_size("ctx")
+    rows, width = tok.shape
+    wide = down_w.shape[0]
+    bf, f32 = jnp.bfloat16, jnp.float32
+    shape = jax.ShapeDtypeStruct
+    dma = pltpu.SemaphoreType.DMA
+    halves = pltpu.VMEM((6, rows // 2, width), bf)
+    quads = pltpu.VMEM((4, rows, width), bf)
+    blocks = pltpu.VMEM((n, rows, rows), bf)
+    return pl.pallas_call(
+        middle_kernel,
+        out_shape=(
+            shape((n, rows, width), bf), shape((n, rows, wide), bf), shape((n, rows, 2 * wide), bf),
+            shape((n, rows, rows), bf), shape((n, rows, rows), bf), shape((rows, width), f32), shape((rows, width), bf),
+            shape((1, width), f32),
+        ),
+        in_specs=vm(8),
+        out_specs=vm(8),
+        scratch_shapes=[
+            blocks, pltpu.VMEM((rows, width), bf), pltpu.VMEM((rows, width), f32), blocks, blocks,
+            pltpu.VMEM((4, rows, width), f32), quads, quads, halves, halves, quads, quads, halves, halves,
+            dma((2, n)), dma((2, Gather.sems)), dma((2, Reduce.sems)), dma((2, Reduce.sems)), dma((2, n)), dma((2, n)),
+        ],
+        compiler_params=pltpu.CompilerParams(collective_id=5, has_side_effects=True, vmem_limit_bytes=67043328),
+        name="middle_moves",
+    )(low, tok, up, up_all, out_w, gu_w, down_w, gain)
+
+
+def last_kernel(
+    pgrad, qkv_w, tok, middle_grad, gain, ffn_gain, low, down_part, gu_part,
+    grad, gains, low_all, down_all, gu_all,
+    mine, theirs, first, out, second, mine_gain, ctx_gain, plane_sum, plane_gain,
+    reduce_sem, gather_sem, down_sem, gu_sem, gain_sem, plane_sem,
+):
+    place = Place()
+    greet(place, planes=True)
+    grads = Reduce(place, mine, theirs, first, out, second, reduce_sem)
+
+    def push(k, carry):
+        theirs[k] = nt(pgrad[flip(place, 2 * k + 1)], qkv_w[...]).astype(jnp.bfloat16)
+        grads.push(k)
+        return carry
+
+    def keep(k, carry):
+        mine[k] = nt(pgrad[flip(place, 2 * k)], qkv_w[...])
+        return carry
+
+    lax.fori_loop(0, 4, push, 0)
+    lax.fori_loop(0, 4, keep, 0)
+    grads.across()
+    grads.beside()
+    grads.turn()
+    moves = [
+        Gather(place, low, low_all, gather_sem),
+        Gather(place, down_part, down_all, down_sem),
+        Gather(place, gu_part, gu_all, gu_sem),
+    ]
+    moves[0].start()
+    normed_grad = grads.total()
+    x = tok[...].astype(jnp.float32)
+    factor = lax.rsqrt(jnp.mean(x * x, axis=-1, keepdims=True) + epsilon)
+    unit = x * factor
+    gain_grad = jnp.sum(normed_grad * unit, axis=0, keepdims=True)
+    scaled = normed_grad * gain[...]
+    inner = jnp.mean(scaled * unit, axis=-1, keepdims=True)
+    grad[...] = middle_grad[...] + factor * (scaled - unit * inner)
+    shard = mine_gain.shape[1]
+    count = mine_gain.shape[0] // 2
+    for at in range(count):
+        mine_gain[pl.ds(at, 1), :] = gain_grad[:, at * shard : (at + 1) * shard]
+        mine_gain[pl.ds(count + at, 1), :] = ffn_gain[:, at * shard : (at + 1) * shard]
+    ctx_sum = Share(place, mine_gain, ctx_gain, gain_sem)
+    ctx_sum.start()
+    for at, move in enumerate(moves):
+        if at:
+            move.start()
+        move.relay()
+        move.rest()
+    ctx_sum.finish()
+    plane_sum[...] = jnp.sum(ctx_gain[...], axis=0)
+    planes = PlaneShare(place, plane_sum, plane_gain, plane_sem)
+    planes.start()
+    for move in moves:
+        move.partner()
+    planes.finish()
+    gains[...] = jnp.sum(plane_gain[...], axis=0)
+    for move in moves:
+        move.finish()
+    grads.finish()
+
+
+def last_moves(pgrad, qkv_w, tok, middle_grad, gain, ffn_gain, low, down_part, gu_part):
+    n, planes = lax.axis_size("ctx"), lax.axis_size("fsdp")
+    rows, width = tok.shape
+    bf, f32 = jnp.bfloat16, jnp.float32
+    shape = jax.ShapeDtypeStruct
+    dma = pltpu.SemaphoreType.DMA
+    halves = pltpu.VMEM((6, rows // 2, width), bf)
+    quads = pltpu.VMEM((4, rows, width), bf)
+    small = (2 * planes, width // planes)
+    many = lambda x: shape((n,) + x.shape, x.dtype)
+    return pl.pallas_call(
+        last_kernel,
+        out_shape=(
+            shape((rows, width), f32), shape(small, f32), many(low), many(down_part), many(gu_part),
+        ),
+        in_specs=vm(9),
+        out_specs=vm(2) + anywhere(3),
+        scratch_shapes=[
+            pltpu.VMEM((4, rows, width), f32), quads, quads, halves, halves,
+            pltpu.VMEM(small, f32), pltpu.VMEM((n,) + small, f32), pltpu.VMEM(small, f32), pltpu.VMEM((planes,) + small, f32),
+            dma((2, Reduce.sems)), dma((2, Gather.sems)), dma((2, Gather.sems)), dma((2, Gather.sems)), dma((2, n)), dma((2, planes)),
+        ],
+        compiler_params=pltpu.CompilerParams(collective_id=6, has_side_effects=True, vmem_limit_bytes=67043328),
+        name="last_moves",
+    )(pgrad, qkv_w, tok, middle_grad, gain, ffn_gain, low, down_part, gu_part)
+
+
+def gathers_kernel(count, *refs):
+    place = Place()
+    greet(place)
+    moves = [Gather(place, refs[at], refs[count + at], refs[2 * count + at]) for at in range(count)]
+    for move in moves:
+        move.start()
+        move.relay()
+        move.rest()
+    for move in moves:
+        move.partner()
+    for move in moves:
+        move.finish()
+
+
+def gathers(number, *arrays):
+    n = lax.axis_size("ctx")
+    count = len(arrays)
+    return pl.pallas_call(
+        functools.partial(gathers_kernel, count),
+        out_shape=tuple(jax.ShapeDtypeStruct((n,) + x.shape, x.dtype) for x in arrays),
+        in_specs=vm(count),
+        out_specs=anywhere(count),
+        scratch_shapes=[pltpu.SemaphoreType.DMA((2, Gather.sems))] * count,
+        compiler_params=pltpu.CompilerParams(collective_id=number, has_side_effects=True),
+        name="gathers",
+    )(*arrays)
+
+
+def attend(spans, tokens_all, gain, weight, cosine, sine):
+    length = tokens_all.shape[0]
+    pairs = length // 192
+    shapes = (
+        jax.ShapeDtypeStruct(tokens_all.shape, jnp.bfloat16),
+        jax.ShapeDtypeStruct((2 * length, LANES), jnp.bfloat16),
+        jax.ShapeDtypeStruct((length, LANES), jnp.bfloat16),
+        jax.ShapeDtypeStruct((length, LANES), jnp.bfloat16),
+        jax.ShapeDtypeStruct((pairs * LANES, 384), jnp.float32),
+        jax.ShapeDtypeStruct((length, 192), jnp.bfloat16),
+        jax.ShapeDtypeStruct((pairs, 384), jnp.float32),
+    )
+    return pl.pallas_call(
+        attend_kernel,
+        out_shape=shapes,
+        in_specs=[pl.BlockSpec(memory_space=pltpu.SMEM)] + vm(5),
+        out_specs=vm(7),
+        name="attend",
+    )(spans, tokens_all, gain, weight, cosine, sine)
+
+
+def attend_back(spans, grad, q, k, v, att, lse, cosine, sine):
+    length = k.shape[0]
+    return pl.pallas_call(
+        back_kernel,
+        out_shape=jax.ShapeDtypeStruct((length, 4 * LANES), jnp.bfloat16),
+        in_specs=[pl.BlockSpec(memory_space=pltpu.SMEM)] + vm(8),
+        out_specs=pl.BlockSpec(memory_space=pltpu.VMEM),
+        scratch_shapes=[pltpu.VMEM((length, LANES), jnp.float32)] * 2,
+        name="attend_back",
+    )(spans, grad, q, k, v, att, lse, cosine, sine)
+
+
+def fast_body(
+    tokens, positions, qkv_weight, out_weight, gate_up_weight, down_weight, attn_gain, ffn_gain, cotangent
+):
+    me = lax.axis_index("ctx")
+    n = lax.axis_size("ctx")
+    planes = lax.axis_size("fsdp")
+    rows = tokens.shape[1]
+    length = n * rows
+    width = tokens.shape[2]
+    wide = down_weight.shape[1] * planes
+    shard = qkv_weight.shape[1]
+    query_width = HEADS * HEAD_DIM
+    key_width = KV_HEADS * HEAD_DIM
+
+    def pick(x, axis):
+        return lax.dynamic_index_in_dim(x, me, axis, keepdims=False)
+
+    qkv = qkv_weight[0]
+    q_part = pick(qkv[:, :query_width].reshape(shard, n, 2, HEAD_DIM), 1)
+    k_part = pick(qkv[:, query_width : query_width + key_width].reshape(shard, n, 1, HEAD_DIM), 1)
+    v_part = pick(qkv[:, query_width + key_width :].reshape(shard, n, HEAD_DIM), 1)
+    qk = spread(jnp.concatenate([q_part, k_part], axis=1)).reshape(shard, 3 * LANES)
+    qkv_block = jnp.concatenate([qk, jnp.pad(v_part, ((0, 0), (0, LANES - HEAD_DIM)))], axis=1)
+    out_rows = shard // n
+    out_block = pick(out_weight[0].reshape(n, out_rows, width), 0)
+    gate_up_block = pick(gate_up_weight[0].reshape(shard, 2, planes, n, wide // planes // n), 3)
+    gate_up_block = lax.all_gather(gate_up_block, "fsdp", axis=0, tiled=True)
+    gate_up_block = gate_up_block.reshape(planes * shard, 2 * wide // n)
+    down_block = pick(down_weight[0].reshape(n, -1, width), 0)
+    down_block = lax.all_gather(down_block, "fsdp", axis=0, tiled=True)
+    upstream = cotangent[0]
+    gains = jnp.concatenate([attn_gain, ffn_gain, jnp.zeros((6, shard), attn_gain.dtype)], axis=0).astype(jnp.float32)
+    spot = jnp.full((8, LANES), positions[0, 0], jnp.int32)
+    tokens_all, upstream_all, qkv_block, out_block, spots, gains = first_moves(
+        tokens[0], upstream.astype(jnp.bfloat16), qkv_block, out_block.reshape(out_rows, width), spot, gains
+    )
+    tokens_all = tokens_all.reshape(length, width)
+    qkv_block = qkv_block.reshape(width, -1)
+    gains = gains[:, :2].transpose(1, 0, 2).reshape(2, width)
+    attn_full, ffn_full = gains[0], gains[1]
+    (out_full,) = gathers(2, out_block.reshape(planes * out_rows, width))
+    out_full = out_full.reshape(n, planes, out_rows, width).transpose(1, 0, 2, 3).reshape(planes * shard, width)
+
+    early = spots[:, 0, 0] // (rows // 2)
+    span = jnp.stack([early, 2 * n - 1 - early], axis=1).reshape(2 * n)
+    order = jnp.sum(
+        jnp.where(span[None, :] == jnp.arange(2 * n)[:, None], jnp.arange(2 * n)[None, :], 0), axis=1
+    )
+    spans = jnp.concatenate([span, order]).astype(jnp.int32)
+    cosine, sine = tables(length)
+
+    normed, q, k, v, att, low, lse = attend(spans, tokens_all, attn_full[None], qkv_block, cosine, sine)
+
+    second_all, hidden, gate_up_low, attended_grad, middle_cols, middle_grad, result, ffn_partial = middle_moves(
+        low.reshape(n, rows, -1), tokens[0], upstream, upstream_all, out_full, gate_up_block, down_block, ffn_full[None]
+    )
+    own = wide // n
+    second_all = second_all.reshape(length, width)
+    hidden = hidden.reshape(length, own)
+    gate_up_low = gate_up_low.reshape(length, 2 * own)
+
+    def reduce_planes(block):
+        return lax.psum_scatter(block.astype(jnp.bfloat16), "fsdp", scatter_dimension=0, tiled=True)
+
+    down_grad = reduce_planes(tn(hidden, upstream_all.reshape(length, width)))
+    gate_up_grad = reduce_planes(tn(second_all, gate_up_low))
+    projected_grad = attend_back(
+        spans, attended_grad.reshape(length, -1), q, k, v, att, lse, cosine, sine
+    )
+    stream_grad, gains, low_all, down_grad, gate_up_grad = last_moves(
+        projected_grad.reshape(n, rows, -1), qkv_block, tokens[0], middle_grad, attn_full[None], ffn_partial,
+        low, down_grad, gate_up_grad,
+    )
+    low_all = low_all.transpose(1, 0, 2).reshape(length, query_width)
+    gains = gains.reshape(2, planes, shard)
+    gains = lax.dynamic_index_in_dim(gains, lax.axis_index("fsdp"), 1, keepdims=False)
+    qkv_grad = reduce_planes(tn(normed, projected_grad))
+    out_grad = reduce_planes(tn(low_all, middle_cols.reshape(length, -1)))
+    qkv_grad, out_grad = gathers(7, qkv_grad, out_grad)
+    pieces = qkv_grad.reshape(n, shard, 4, LANES).transpose(1, 0, 2, 3)
+    qkv_grad = jnp.concatenate(
+        [
+            gathered_spread(pieces[:, :, 0:2]).reshape(shard, query_width),
+            gathered_spread(pieces[:, :, 2]).reshape(shard, key_width),
+            pieces[:, :, 3, :HEAD_DIM].reshape(shard, key_width),
+        ],
+        axis=1,
+    ).astype(jnp.float32)
+    out_grad = out_grad.transpose(1, 0, 2).reshape(shard, width).astype(jnp.float32)
+    gate_up_grad = gate_up_grad.reshape(n, shard, 2, planes, -1).transpose(1, 2, 3, 0, 4)
+    gate_up_grad = gate_up_grad.reshape(shard, 2, wide).astype(jnp.float32)
+    down_grad = down_grad.reshape(-1, width).astype(jnp.float32)
+    return (
+        result[None],
+        stream_grad[None],
+        qkv_grad[None],
+        out_grad[None],
+        gate_up_grad[None],
+        down_grad[None],
+        gains[0][None],
+        gains[1][None],
+    )
+
+
 def solution(mesh):
+    split = mesh.shape["ctx"] == KV_HEADS
     placed = (
         P("fsdp", "ctx", None),
         P("fsdp", "ctx"),
@@ -474,7 +1393,7 @@
         P("fsdp", "ctx", None),
     )
     return jax.shard_map(
-        body,
+        fast_body if split else body,
         mesh=mesh,
         in_specs=placed,
         out_specs=(

time: 3530 us -> 672 us (0.19)
  waiting for transfers between devices: 2750 us -> 67.3 us
  Pallas kernels: 0 us -> 413 us
  matrix products: 257 us -> 26.3 us
  loops' own time: 124 us -> 0 us
  local copies, waits for them, and re-layouts: 235 us -> 121 us
  blocking collectives: 67.3 us -> 0 us
  other arithmetic: 64.4 us -> 18.2 us
    reduce_scatter x4, waiting for transfers between devices: 1670 us -> 67.2 us  [reduce_planes(): lax.psum_scatter(block.astype(jnp.bfloat16), 'fsdp', scatter_dimension=0,...]
    all_gather x6 -> x2, waiting for transfers between devices: 718 us -> 0.01 us  [the longest x1 0.01 us: fast_body(): gate_up_block = lax.all_gather(gate_up_block, 'fsdp', axis=0, tiled=True)]
    pallas_call x0 -> x7, Pallas kernels: none -> 413 us  [the longest x1 120 us: middle_moves(): pl.pallas_call(middle_kernel, out_shape=(shape((n, rows, width), bf), sha...]
    psum x1 -> x0, waiting for transfers between devices: 268 us -> none  [backward_layer(): lax.psum((sharded[0], sharded[1], sharded[2], sharded[3], sharded[4], sha...]
    dot_general x131 -> x4, matrix products: 257 us -> 26.3 us  [tn(): lax.dot_general(left, right, (((0,), (0,)), ((), ())), preferred_element_...]
    another operation x99 -> x0, loops' own time: 124 us -> none  [the longest x1 40.4 us: attention_backward(): lax.scan(sweep_back, (start_grad, start_grad), (key_blocks, value_blocks,...]
    unnamed x15 -> x6, waiting for transfers between devices: 96.7 us -> 0.1 us
    squeeze x56 -> x3, local copies, waits for them, and re-layouts: 55.9 us -> 3.45 us  [pick(): return lax.dynamic_index_in_dim(x, me, axis, keepdims=False)]
  transfers between devices with their start and end apart: 13 -> 6, of which waited for: 11 -> 2; matrix products, arithmetic and copies ran while one was open for 7% -> 17% of each run, Pallas kernels for 0% -> 40%
where the time goes in v1:
time: 672 us; the launch traced here: 661 us
  Pallas kernels  413 us (61%)
  local copies, waits for them, and re-layouts  121 us (18%)
  waiting for transfers between devices  67.3 us (10%)
  matrix products  26.3 us (4%)
  other arithmetic  18.2 us (3%)
  between operations  14.8 us (2%)
    pallas_call x1, Pallas kernels, middle_moves(): pl.pallas_call(middle_kernel, out_shape=(shape((n, rows, width), bf), sha...  120 us
    pallas_call x1, Pallas kernels, first_moves(): pl.pallas_call(first_kernel, out_shape=(shape(n, tok), shape(n, up), shap...  106 us
    pallas_call x1, Pallas kernels, last_moves(): pl.pallas_call(last_kernel, out_shape=(shape((rows, width), f32), shape(s...  105 us
    reduce_scatter x4, waiting for transfers between devices, reduce_planes(): lax.psum_scatter(block.astype(jnp.bfloat16), 'fsdp', scatter_dimension=0,...  67.2 us
    pallas_call x2, Pallas kernels, gathers(): pl.pallas_call(functools.partial(gathers_kernel, count), out_shape=tuple(...  54.8 us
    convert_element_type x3, local copies, waits for them, and re-layouts, fast_body(): gate_up_grad = gate_up_grad.reshape(shard, 2, wide).astype(jnp.float32)  44.8 us
    unnamed x34, local copies, waits for them, and re-layouts  30.3 us
    dot_general x4, matrix products, tn(): lax.dot_general(left, right, (((0,), (0,)), ((), ())), preferred_element_...  26.3 us
  transfers between devices with their start and end apart: 6, of which 2 were waited for; matrix products, arithmetic and copies ran while one was open for 17% of the time, Pallas kernels for 40%

profile of v1, /device:TPU:0, one launch (start us, length us, event | category | flops | bytes accessed | tf_op | source)
XLA Modules:
  0.0 660.9 jit_solution(5510851131353471355)
XLA Ops:
  7.2 16.2 %copy.92 = bf16[1,384,2,4096]{1,3,2,0:T(8,128)(2,1)} copy(bf16[1,384,2,4096]{3,2,1,0:T(2,128)(2,1)} %param.13) | data formatting | bytes 12582912 | tf_op args[4]
  41.0 106.2 %first_moves.1 = (bf16[8,192,1536]{2,1,0:T(8,128)(2,1)}, bf16[8,192,1536]{2,1,0:T(8,128)(2,1)}, bf16[4,384,512]{2,1,0:T(8,128)(2,1)}, bf16[4,48,1536]{2,1,0:T(8,...) custom-call(bf16[192,1536]{1,0:T(8,128)(2,1)} %bitcast.97, bf16[192,1536]{1,0:T(8,128)(2,1)} %bitcast_convert_fusion.2.up, ...), custom_call_target="tpu_custom_call" | custom-call | tf_op jit(solution)/shard_map/first_moves/pallas_call | solution.py:900
  149.4 26.3 %gathers.2 = bf16[8,192,1536]{2,1,0:T(8,128)(2,1)} custom-call(bf16[192,1536]{1,0:T(8,128)(2,1)} %bitcast.116), custom_call_target="tpu_custom_call" | custom-call | tf_op jit(solution)/shard_map/gathers/pallas_call | solution.py:1234
  175.8 4.9 copy.91
  187.6 15.9 %attend.1 = (bf16[1536,1536]{1,0:T(8,128)(2,1)}, bf16[3072,128]{1,0:T(8,128)(2,1)}, bf16[1536,128]{1,0:T(8,128)(2,1)}, bf16[1536,128]{1,0:T(8,128)(2,1)}, f32[10...) custom-call(s32[32]{0:T(128)} %pad_add_fusion.1.span, bf16[1536,1536]{1,0:T(8,128)(2,1)} %bitcast.102, ...), custom_call_target="tpu_custom_call" | custom-call | tf_op jit(solution)/shard_map/attend/pallas_call | solution.py:1257
  203.5 6.1 reshape.252.gu_w
  209.5 120.0 %middle_moves.1 = (bf16[8,192,1536]{2,1,0:T(8,128)(2,1)}, bf16[8,192,512]{2,1,0:T(8,128)(2,1)}, bf16[8,192,1024]{2,1,0:T(8,128)(2,1)}, bf16[8,192,192]{2,1,0:T(8...) custom-call(bf16[8,192,192]{2,1,0:T(8,128)(2,1)} %bitcast.104, ...), custom_call_target="tpu_custom_call" | custom-call | tf_op jit(solution)/shard_map/middle_moves/pallas_call | solution.py:1108
  329.6 6.8 %fusion = bf16[512,1536]{1,0:T(8,128)(2,1)} fusion(bf16[8,192,512]{2,1,0:T(8,128)(2,1)} %get-tuple-element.52, bf16[8,192,1536]{2,1,0:T(8,128)(2,1)} %get-tuple-element.41.up_all), kind=kOutput, calls=%fused_computation.4 | convolution fusion | flops 2416705536 | bytes 7864320 | tf_op jit(solution)/shard_map/dot_general | solution.py:503
  336.4 8.8 %bitcast_convert_fusion = bf16[1536,1024]{1,0:T(8,128)(2,1)} fusion(bf16[8,192,1536]{2,1,0:T(8,128)(2,1)} %get-tuple-element.53, bf16[8,192,1024]{2,1,0:T(8,128)(2,1)S(1)} %copy-done.11), kind=kOutput, calls=%fused_computation | convolution fusion | flops 4833411072 | bytes 11010048 | tf_op jit(solution)/shard_map/dot_general | solution.py:503
  345.5 11.6 %attend_back.1 = bf16[1536,512]{1,0:T(8,128)(2,1)} custom-call(s32[32]{0:T(128)} %pad_add_fusion.1.span, bf16[1536,192]{1,0:T(8,128)(2,1)} %bitcast.112, bf16[3072,128]{1,0:T(8,128)(2,1)} %get-tuple-element.45.q_ref, bf16[1536,128]{1,0:T(8,128)(2,1)} %get-tuple-element.46.k_ref, bf16[1536,128]{1,0:T(8,128)(2,1)} %get-tuple-element.47.v_ref, ...), custom_call_target="tpu_custom_call" | custom-call | tf_op jit(solution)/shard_map/attend_back/pallas_call | solution.py:1268
  357.2 6.7 %convolution_convert_fusion = bf16[1536,512]{1,0:T(8,128)(2,1)} fusion(bf16[1536,1536]{1,0:T(8,128)(2,1)} %get-tuple-element.56, bf16[1536,512]{1,0:T(8,128)(2,1)} %attend_back.1), kind=kOutput, calls=%fused_computation.5 | convolution fusion | flops 2416705536 | bytes 7864320 | tf_op jit(solution)/shard_map/dot_general | solution.py:503
  364.2 5.2 reduce-scatter.5.cloned.1.call-done.down_part
  369.3 62.0 %reduce-scatter.7.cloned.1.call-done.gu_part = bf16[384,1024]{1,0:T(8,128)(2,1)} async-done(((bf16[1536,1024]{1,0:T(8,128)(2,1)}), bf16[384,1024]{1,0:T(8,128)(2,1)}) %reduce-scatter.7.cloned.1.call-update) | async-done | bytes 786448 | tf_op jit(solution)/shard_map/reduce_scatter | solution.py:1340
  431.4 104.5 %last_moves.1 = (f32[192,1536]{1,0:T(8,128)}, f32[8,384]{1,0:T(8,128)}, bf16[8,1536,192]{2,1,0:T(8,128)(2,1)}, bf16[8,128,1536]{2,1,0:T(8,128)(2,1)}, bf16[8,384,1024]{2,1,0:T(8,128)(2,1)}) custom-call(bf16[8,192,512]{2,1,0:T(8,128)(2,1)} %bitcast.96, bf16[1536,512]{1,0:T(8,128)(2,1)} %bitcast.95, bf16[192,1536]{1,0:T(8,128)(2,1)} %bitcast.99, ...), custom_call_target="tpu_custom_call" | custom-call | tf_op jit(solution)/shard_map/last_moves/pallas_call | solution.py:1200
  535.9 8.0 %copy.94 = bf16[1536,8,192]{0,2,1:T(8,128)(2,1)} copy(bf16[1536,8,192]{2,0,1:T(8,128)(2,1)} %bitcast.93) | data formatting | bytes 9437184 | tf_op jit(solution)/shard_map/transpose | solution.py:1351
  543.9 4.0 convolution_convert_fusion.1
  549.2 12.7 %reshape.262 = f32[8,384,2,4,128]{4,3,2,1,0:T(4,128)} reshape(bf16[8,384,1024]{2,1,0:T(8,128)(2,1)} %get-tuple-element.61) | data formatting | bytes 18874368 | tf_op jit(solution)/shard_map/convert_element_type | solution.py:1368
  561.8 16.5 %copy.100 = f32[384,2,4,8,128]{4,3,2,1,0:T(8,128)} copy(f32[384,2,4,8,128]{4,2,1,0,3:T(4,128)} %bitcast.82) | data formatting | bytes 25165824 | tf_op jit(solution)/shard_map/convert_element_type | solution.py:1368
  578.3 15.7 %reshape.260 = f32[1,384,2,4096]{3,2,1,0:T(2,128)} reshape(f32[384,2,4,8,128]{4,3,2,1,0:T(8,128)} %copy.100) | data formatting | bytes 25165824 | tf_op jit(solution)/shard_map/convert_element_type | solution.py:1368
  594.6 3.6 bitcast_convert_fusion.1
  598.2 28.5 %gathers.3 = (bf16[8,384,512]{2,1,0:T(8,128)(2,1)}, bf16[8,384,192]{2,1,0:T(8,128)(2,1)}) custom-call(bf16[384,512]{1,0:T(8,128)(2,1)} %reduce-scatter.9.cloned.1.call-done.refs_0_, bf16[384,192]{1,0:T(8,128)(2,1)} %reduce-scatter.11.cloned.1.call-done.refs_1_), custom_call_target="tpu_custom_call" | custom-call | tf_op jit(solution)/shard_map/gathers/pallas_call | solution.py:1234
  626.7 3.5 copy.103
  638.7 6.0 copy.101
  648.7 3.2 copy.102
  (96 shorter events, 43.2 us)
Async XLA Ops:
  7.2 196.3 %all-gather.5.cloned.1.call-start = ((), (), s32[]{:S(2)}) async-start(), calls=%async_computation.8 | async-start | bytes 3932160 | tf_op jit(solution)/shard_map/all_gather | solution.py:1304
  25.9 183.6 %all-gather.7.cloned.1.call-start = ((), (), s32[]{:S(2)}) async-start(), calls=%async_computation.9 | async-start | bytes 1966080 | tf_op jit(solution)/shard_map/all_gather | solution.py:1307
  27.8 341.6 %reduce-scatter.5.cloned.1.call-start = ((), (), s32[]{:S(2)}) async-start(), calls=%async_computation.4 | async-start | bytes 1966080 | tf_op jit(solution)/shard_map/reduce_scatter | solution.py:1340
  30.8 2.1 copy-start
  30.8 4.9 copy-start.10
  31.8 6.0 copy-start.13
  32.9 6.2 copy-start.8
  32.9 6.2 copy-start.9
  329.6 6.8 %copy-start.11 = (bf16[8,192,1024]{2,1,0:T(8,128)(2,1)S(1)}, bf16[8,192,1024]{2,1,0:T(8,128)(2,1)}, u32[]{:S(2)}) copy-start(bf16[8,192,1024]{2,1,0:T(8,128)(2,1)} %get-tuple-element.54) | copy-start | bytes 9437188
  336.4 95.0 %reduce-scatter.7.cloned.1.call-start = ((), (), s32[]{:S(2)}) async-start(), calls=%async_computation.5 | async-start | bytes 3932160 | tf_op jit(solution)/shard_map/reduce_scatter | solution.py:1340
  345.3 252.9 %reduce-scatter.9.cloned.1.call-start = ((), (), s32[]{:S(2)}) async-start(), calls=%async_computation.6 | async-start | bytes 1966080 | tf_op jit(solution)/shard_map/reduce_scatter | solution.py:1340
  363.9 234.3 %reduce-scatter.11.cloned.1.call-start = ((), (), s32[]{:S(2)}) async-start(), calls=%async_computation.7 | async-start | bytes 983040 | tf_op jit(solution)/shard_map/reduce_scatter | solution.py:1340
  535.9 8.0 %copy-start.12 = (bf16[8,192,192]{2,1,0:T(8,128)(2,1)S(1)}, bf16[8,192,192]{2,1,0:T(8,128)(2,1)}, u32[]{:S(2)}) copy-start(bf16[8,192,192]{2,1,0:T(8,128)(2,1)} %get-tuple-element.58) | copy-start | bytes 1769476
  578.3 15.7 %copy-start.7 = (f32[8,384]{1,0:T(8,128)S(1)}, f32[8,384]{1,0:T(8,128)}, u32[]{:S(2)}) copy-start(f32[8,384]{1,0:T(8,128)} %get-tuple-element.63) | copy-start | bytes 36868
  578.3 16.3 %copy-start.1 = (bf16[8,128,1536]{2,1,0:T(8,128)(2,1)S(1)}, bf16[8,128,1536]{2,1,0:T(8,128)(2,1)}, u32[]{:S(2)}) copy-start(bf16[8,128,1536]{2,1,0:T(8,128)(2,1)} %get-tuple-element.62) | copy-start | bytes 9437188
  634.8 1.3 copy-start.3
  634.8 1.3 copy-start.4
  635.1 1.2 copy-start.2
  648.7 3.2 copy-start.6
  648.7 4.0 copy-start.5
Sparse Core Ops, SparseCore 0:
  26.0 86.1 all-gather.4
  113.8 39.9 all-gather.6
  336.5 32.7 reduce-scatter.4
  372.1 59.2 reduce-scatter.6
  434.1 35.3 reduce-scatter.8
  549.3 21.6 reduce-scatter.10

commit v2 on v1

--- a/solution.py
+++ b/solution.py
@@ -478,17 +478,18 @@
     return jnp.concatenate([padded[..., :half], padded[..., 64 : 64 + half]], axis=-1)
 
 
-def tables(length):
+def table(length):
     half = HEAD_DIM // 2
     frequency = rope_base ** (-(jnp.arange(half, dtype=jnp.float32) * 2.0 / HEAD_DIM))
     phases = jnp.arange(length, dtype=jnp.float32)[:, None] * frequency[None, :]
     pad = ((0, 0), (0, 64 - half))
-    cosine = jnp.pad(jnp.cos(phases), pad)
-    sine = jnp.pad(jnp.sin(phases), pad)
-    return (
-        jnp.concatenate([cosine, cosine], axis=1),
-        jnp.concatenate([-sine, sine], axis=1),
-    )
+    return jnp.concatenate([jnp.pad(jnp.cos(phases), pad), jnp.pad(jnp.sin(phases), pad)], axis=1)
+
+
+def wave(rows):
+    first = lax.broadcasted_iota(jnp.int32, rows.shape, 1) < 64
+    other = pltpu.roll(rows, 64, 1)
+    return jnp.where(first, rows, other), jnp.where(first, -other, rows)
 
 
 def nt(left, right):
@@ -510,66 +511,8 @@
     return key_at <= query_at
 
 
-def attend_kernel(
-    span, tok_ref, gain_ref, w_ref, cos_ref, sin_ref,
-    normed_ref, q_ref, k_ref, v_ref, att_ref, low_ref, lse_ref,
-):
-    length = tok_ref.shape[0]
-    half = 96
-    pairs = length // (2 * half)
-    step = 2 * 2 * half
-    lane = lax.broadcasted_iota(jnp.int32, (half, LANES), 1)
-    for chunk in range(length // step):
-        rows = pl.ds(chunk * step, step)
-        x = tok_ref[rows, :].astype(jnp.float32)
-        factor = lax.rsqrt(jnp.mean(x * x, axis=-1, keepdims=True) + epsilon)
-        normed = (x * factor * gain_ref[...]).astype(jnp.bfloat16)
-        normed_ref[rows, :] = normed
-        proj = nn(normed, w_ref[...])
-        for piece in range(step // half):
-            at = span[chunk * (step // half) + piece]
-            spot = pl.multiple_of(at * half, half)
-            cosine = cos_ref[pl.ds(spot, half), :]
-            sine = sin_ref[pl.ds(spot, half), :]
-            mine = proj[piece * half : (piece + 1) * half]
-
-            def turned(part):
-                z = mine[:, part * LANES : (part + 1) * LANES]
-                return (z * cosine + pltpu.roll(z, 64, 1) * sine).astype(jnp.bfloat16)
-
-            base = (at // 2) * (4 * half) + (at % 2) * half
-            q_ref[pl.ds(pl.multiple_of(base, half), half), :] = turned(0)
-            q_ref[pl.ds(pl.multiple_of(base + 2 * half, half), half), :] = turned(1)
-            k_ref[pl.ds(spot, half), :] = turned(2)
-            v_ref[pl.ds(spot, half), :] = mine[:, 3 * LANES :].astype(jnp.bfloat16)
-    scaling = HEAD_DIM ** (-0.5)
-    mask = causal(2 * half)
-    values_t = v_ref[...].astype(jnp.float32).T.astype(jnp.bfloat16)
-    for pair in range(pairs):
-        width = (pair + 1) * 2 * half
-        q = q_ref[pl.ds(pair * 4 * half, 4 * half), :]
-        scores = nt(k_ref[pl.ds(0, width), :], q) * scaling
-        last = jnp.where(mask, scores[width - 2 * half :], -1e30)
-        scores = last if pair == 0 else jnp.concatenate([scores[: width - 2 * half], last], axis=0)
-        top = jnp.max(scores, axis=0, keepdims=True)
-        e = jnp.exp(scores - top)
-        total = jnp.sum(e, axis=0, keepdims=True)
-        weights = (e * (1.0 / total)).astype(jnp.bfloat16)
-        lse_ref[pl.ds(pair, 1), :] = top + jnp.log(total)
-        out_t = nn(values_t[:, :width], weights)
-        att_ref[pl.ds(pair * LANES, LANES), :] = out_t
-        out = out_t.T.astype(jnp.bfloat16).astype(jnp.float32)
-        for part in range(2):
-            at = span[2 * pairs + 2 * pair + part]
-            first = out[part * half : (part + 1) * half]
-            second = pltpu.roll(out[(2 + part) * half : (3 + part) * half], half, 1)
-            spot = pl.ds(pl.multiple_of(at * half, half), half)
-            low_ref[spot, 0:LANES] = jnp.where(lane < half, first, second).astype(jnp.bfloat16)
-            low_ref[spot, LANES : 2 * half] = second[:, : 2 * half - LANES].astype(jnp.bfloat16)
-
-
 def back_kernel(
-    span, grad_ref, q_ref, k_ref, v_ref, att_ref, lse_ref, cos_ref, sin_ref,
+    span, grad_ref, q_ref, k_ref, v_ref, att_ref, lse_ref, turn_ref,
     out_ref, dk_ref, dv_ref,
 ):
     length = k_ref.shape[0]
@@ -615,7 +558,7 @@
             at = span[2 * pairs + 2 * pair + part]
             rows = pl.ds(pl.multiple_of(at * half, half), half)
             spot = pl.ds((2 * pair + part) * half, half)
-            cosine, sine = cos_ref[spot, :], sin_ref[spot, :]
+            cosine, sine = wave(turn_ref[spot, :])
             for head in range(2):
                 z = dq[(2 * head + part) * half : (2 * head + part + 1) * half]
                 out_ref[rows, head * LANES : (head + 1) * LANES] = (
@@ -626,8 +569,9 @@
         rows = pl.ds(pl.multiple_of(at * half, half), half)
         spot = pl.ds(block * half, half)
         z = dk_ref[spot, :]
+        cosine, sine = wave(turn_ref[spot, :])
         out_ref[rows, 2 * LANES : 3 * LANES] = (
-            z * cos_ref[spot, :] - pltpu.roll(z, 64, 1) * sin_ref[spot, :]
+            z * cosine - pltpu.roll(z, 64, 1) * sine
         ).astype(jnp.bfloat16)
         out_ref[rows, 3 * LANES :] = dv_ref[spot, :].astype(jnp.bfloat16)
 
@@ -693,15 +637,18 @@
     def part(self, rank, half):
         return self.out.at[rank, pl.ds(half * self.half, self.half)]
 
+    def whole(self, rank):
+        return self.out.at[rank]
+
     def start(self):
         p = self.place
-        keep = pltpu.make_async_copy(self.own, self.out.at[p.me], self.sem.at[0, 13])
+        keep = pltpu.make_async_copy(self.own, self.whole(p.me), self.sem.at[0, 13])
         keep.start()
         self.keep = keep
         halves = [self.own.at[pl.ds(h * self.half, self.half)] for h in range(2)]
         self.go(halves[0], self.part(p.me, 0), 0, p.x)
         self.go(halves[1], self.part(p.me, 1), 3, p.y)
-        self.go(self.own, self.out.at[p.me], 6, p.p)
+        self.go(self.own, self.whole(p.me), 6, p.p)
         self.go(halves[1], self.part(p.me, 1), 1, p.x)
         self.go(halves[0], self.part(p.me, 0), 2, p.y)
 
@@ -726,7 +673,7 @@
             self.go(part, part, onward, p.p)
 
     def first_partner(self):
-        part = self.out.at[self.place.p]
+        part = self.whole(self.place.p)
         pltpu.make_async_copy(part, part, self.sem.at[1, 6]).wait()
         self.met = True
 
@@ -790,8 +737,9 @@
                 ok, copy = self.hop(number, up)
                 pl.when(ok)(copy.start)
 
-    def finish(self):
-        self.keep.wait()
+    def finish(self, kept=False):
+        if not kept:
+            self.keep.wait()
         for number in range(self.place.planes - 1):
             for up in (True, False):
                 ok, copy = self.hop(number, up)
@@ -862,56 +810,6 @@
     return [pl.BlockSpec(memory_space=pl.ANY)] * count
 
 
-def first_kernel(tok, up, qkv, out_block, spot, gains, tok_all, up_all, qkv_all, out_all, spots, gain_all, *sems):
-    place = Place()
-    greet(place, planes=True)
-    tokens = Gather(place, tok, tok_all, sems[0])
-    cots = Gather(place, up, up_all, sems[1])
-    qkvs = PlaneGather(place, qkv, qkv_all, sems[2])
-    outs = PlaneGather(place, out_block, out_all, sems[3])
-    spans = Share(place, spot, spots, sems[4])
-    scales = PlaneShare(place, gains, gain_all, sems[5])
-    spans.start()
-    scales.start()
-    qkvs.start()
-    tokens.start()
-    tokens.relay()
-    qkvs.step(1)
-    cots.start()
-    qkvs.step(2)
-    outs.start()
-    tokens.rest()
-    qkvs.step(3)
-    tokens.partner()
-    outs.step(1)
-    cots.relay()
-    outs.step(2)
-    cots.rest()
-    outs.step(3)
-    cots.partner()
-    for move in (spans, scales, qkvs, tokens, cots, outs):
-        move.finish()
-
-
-def first_moves(tok, up, qkv, out_block, spot, gains):
-    n, planes = lax.axis_size("ctx"), lax.axis_size("fsdp")
-    shape = lambda count, x: jax.ShapeDtypeStruct((count,) + x.shape, x.dtype)
-    dma = pltpu.SemaphoreType.DMA
-    return pl.pallas_call(
-        first_kernel,
-        out_shape=(
-            shape(n, tok), shape(n, up), shape(planes, qkv), shape(planes, out_block), shape(n, spot), shape(planes, gains)
-        ),
-        in_specs=vm(6),
-        out_specs=anywhere(6),
-        scratch_shapes=[
-            dma((2, Gather.sems)), dma((2, Gather.sems)), dma((3, planes)), dma((3, planes)), dma((2, n)), dma((2, planes)),
-        ],
-        compiler_params=pltpu.CompilerParams(collective_id=1, has_side_effects=True),
-        name="first_moves",
-    )(tok, up, qkv, out_block, spot, gains)
-
-
 class Reduce:
     sems = 10
 
@@ -975,11 +873,10 @@
         self.go(4, self.top(2) + self.got(1), self.place.y)
         self.go(5, self.low(1) + self.got(3), self.place.x)
 
-    def total(self):
+    def total(self, use):
         self.add(0)
-        upper = self.top(0) + self.got(0) + self.got(4)
-        lower = self.low(0) + self.got(2) + self.got(5)
-        return jnp.concatenate([upper, lower], axis=0)
+        use(pl.ds(0, self.half), self.top(0) + self.got(0) + self.got(4))
+        use(pl.ds(self.half, self.half), self.low(0) + self.got(2) + self.got(5))
 
     def finish(self):
         self.pushed()
@@ -991,162 +888,42 @@
     return place.me + (i % 2) * place.dp + ((i // 2) % 2) * place.dx + (i // 4) * place.dy
 
 
-def middle_kernel(
-    low, tok, up, up_all, out_w, gu_w, down_w, gain,
-    second_all, hidden, gul, agrad, mcols, middle_grad, result, gain_grad,
-    attended, own, middle, agrad_send, mcols_send, mine, theirs, first, out, second, theirs2, first2, out2, second2,
-    low_sem, gather_sem, reduce_sem, reduce_sem2, agrad_sem, mcols_sem,
-):
-    place = Place()
-    n = place.n
-    rows = tok.shape[0]
-    heads = rows
-    greet(place)
-    moved = Exchange(place, low, attended, low_sem)
-    moved.start()
-    moved.finish()
-    total = tok[...].astype(jnp.float32)
-    for q in range(8):
-        total = total + nn(attended[q], out_w[pl.ds(q * heads, heads), :])
-    middle[...] = total
-    factor = lax.rsqrt(jnp.mean(total * total, axis=-1, keepdims=True) + epsilon)
-    own[...] = (total * factor * gain[...]).astype(jnp.bfloat16)
-    seconds = Gather(place, own, second_all, gather_sem)
-    seconds.start()
-    grads = Reduce(place, mine, theirs, first, out, second, reduce_sem)
-    wide = hidden.shape[2]
-
-    def block(i, block_of):
-        rank = flip(place, i)
-        gate_up = nn(block_of(rank), gu_w[...])
-        gate, raised = gate_up[:, :wide], gate_up[:, wide:]
-        sigmoid = 1.0 / (1.0 + jnp.exp(-gate))
-        silu = gate * sigmoid
-        hidden[rank] = (silu * raised).astype(jnp.bfloat16)
-        hidden_grad = nt(up_all[rank], down_w[...])
-        gul[rank, :, pl.ds(0, wide)] = (hidden_grad * raised * sigmoid * (1.0 + gate * (1.0 - sigmoid))).astype(jnp.bfloat16)
-        gul[rank, :, pl.ds(wide, wide)] = (hidden_grad * silu).astype(jnp.bfloat16)
-        return nt(gul[rank], gu_w[...])
-
-    def pair(k, carry):
-        theirs[k] = block(2 * k + 1, lambda rank: second_all[rank]).astype(jnp.bfloat16)
-        grads.push(k)
-        mine[k] = block(2 * k, lambda rank: second_all[rank])
-        return carry
-
-    seconds.relay()
-    seconds.keep.wait()
-    seconds.first_partner()
-    pair(0, 0)
-    seconds.rest()
-    seconds.partner()
-    lax.fori_loop(1, 3, pair, 0)
-    grads.beside()
-    pair(3, 0)
-    grads.across()
-
-    sums = Reduce(place, mine, theirs2, first2, out2, second2, reduce_sem2)
-
-    def other(k, carry):
-        theirs2[k] = nn(hidden[flip(place, 2 * k + 1)], down_w[...]).astype(jnp.bfloat16)
-        sums.push(k)
-        return carry
-
-    lax.fori_loop(0, 2, other, 0)
-    grads.turn()
-    lax.fori_loop(2, 4, other, 0)
-    second_grad = grads.total()
-    x = middle[...]
-    factor = lax.rsqrt(jnp.mean(x * x, axis=-1, keepdims=True) + epsilon)
-    unit = x * factor
-    gain_grad[...] = jnp.sum(second_grad * unit, axis=0, keepdims=True)
-    scaled = second_grad * gain[...]
-    inner = jnp.mean(scaled * unit, axis=-1, keepdims=True)
-    grad = up[...] + factor * (scaled - unit * inner)
-    middle_grad[...] = grad
-    rounded = grad.astype(jnp.bfloat16)
-    seconds.finish(kept=True)
-    own[...] = rounded
-    for q in range(8):
-        mcols_send[q] = rounded[:, q * heads : (q + 1) * heads]
-
-    def head_grads(q, carry):
-        agrad_send[q] = nt(own[...], out_w[pl.ds(pl.multiple_of(q * heads, heads), heads), :]).astype(jnp.bfloat16)
-        return carry
-
-    lax.fori_loop(0, n, head_grads, 0)
-    heads_back = Exchange(place, agrad_send, agrad, agrad_sem)
-    heads_back.start()
-    columns = Exchange(place, mcols_send, mcols, mcols_sem)
-    columns.start()
-
-    def ours(k, carry):
-        mine[k] = nn(hidden[flip(place, 2 * k)], down_w[...])
-        return carry
-
-    lax.fori_loop(0, 4, ours, 0)
-    sums.across()
-    sums.beside()
-    sums.turn()
-    result[...] = (middle[...] + sums.total()).astype(jnp.bfloat16)
-    heads_back.finish()
-    columns.finish()
-    grads.finish()
-    sums.finish()
-
-
-def middle_moves(low, tok, up, up_all, out_w, gu_w, down_w, gain):
-    n = lax.axis_size("ctx")
-    rows, width = tok.shape
-    wide = down_w.shape[0]
-    bf, f32 = jnp.bfloat16, jnp.float32
-    shape = jax.ShapeDtypeStruct
-    dma = pltpu.SemaphoreType.DMA
-    halves = pltpu.VMEM((6, rows // 2, width), bf)
-    quads = pltpu.VMEM((4, rows, width), bf)
-    blocks = pltpu.VMEM((n, rows, rows), bf)
-    return pl.pallas_call(
-        middle_kernel,
-        out_shape=(
-            shape((n, rows, width), bf), shape((n, rows, wide), bf), shape((n, rows, 2 * wide), bf),
-            shape((n, rows, rows), bf), shape((n, rows, rows), bf), shape((rows, width), f32), shape((rows, width), bf),
-            shape((1, width), f32),
-        ),
-        in_specs=vm(8),
-        out_specs=vm(8),
-        scratch_shapes=[
-            blocks, pltpu.VMEM((rows, width), bf), pltpu.VMEM((rows, width), f32), blocks, blocks,
-            pltpu.VMEM((4, rows, width), f32), quads, quads, halves, halves, quads, quads, halves, halves,
-            dma((2, n)), dma((2, Gather.sems)), dma((2, Reduce.sems)), dma((2, Reduce.sems)), dma((2, n)), dma((2, n)),
-        ],
-        compiler_params=pltpu.CompilerParams(collective_id=5, has_side_effects=True, vmem_limit_bytes=67043328),
-        name="middle_moves",
-    )(low, tok, up, up_all, out_w, gu_w, down_w, gain)
-
-
 def last_kernel(
-    pgrad, qkv_w, tok, middle_grad, gain, ffn_gain, low, down_part, gu_part,
-    grad, gains, low_all, down_all, gu_all,
-    mine, theirs, first, out, second, mine_gain, ctx_gain, plane_sum, plane_gain,
-    reduce_sem, gather_sem, down_sem, gu_sem, gain_sem, plane_sem,
+    pgrad, qkv_w, tok, middle_grad, gain, ffn_gain, low, down_part, gu_part, hidden, down_w, middle,
+    grad, result, gains, low_all, down_all, gu_all,
+    mine, theirs, first, out, second, theirs2, first2, out2, second2, gain_sum, mine_gain, ctx_gain, plane_sum, plane_gain,
+    reduce_sem, reduce_sem2, gather_sem, down_sem, gu_sem, gain_sem, plane_sem,
 ):
     place = Place()
     greet(place, planes=True)
     grads = Reduce(place, mine, theirs, first, out, second, reduce_sem)
+    pgrad_width = tok.shape[1]
 
     def push(k, carry):
-        theirs[k] = nt(pgrad[flip(place, 2 * k + 1)], qkv_w[...]).astype(jnp.bfloat16)
+        theirs[k] = nt(pgrad[flip(place, 2 * k + 1)], qkv_w[...].reshape(pgrad_width, -1)).astype(jnp.bfloat16)
         grads.push(k)
         return carry
 
     def keep(k, carry):
-        mine[k] = nt(pgrad[flip(place, 2 * k)], qkv_w[...])
+        mine[k] = nt(pgrad[flip(place, 2 * k)], qkv_w[...].reshape(pgrad_width, -1))
         return carry
 
     lax.fori_loop(0, 4, push, 0)
     lax.fori_loop(0, 4, keep, 0)
     grads.across()
     grads.beside()
+    sums = Reduce(place, mine, theirs2, first2, out2, second2, reduce_sem2)
+
+    def other(k, carry):
+        theirs2[k] = nn(hidden[flip(place, 2 * k + 1)], down_w[...].reshape(-1, pgrad_width)).astype(jnp.bfloat16)
+        sums.push(k)
+        return carry
+
+    def ours(k, carry):
+        mine[k] = nn(hidden[flip(place, 2 * k)], down_w[...].reshape(-1, pgrad_width))
+        return carry
+
+    lax.fori_loop(0, 4, other, 0)
     grads.turn()
     moves = [
         Gather(place, low, low_all, gather_sem),
@@ -1154,14 +931,19 @@
         Gather(place, gu_part, gu_all, gu_sem),
     ]
     moves[0].start()
-    normed_grad = grads.total()
-    x = tok[...].astype(jnp.float32)
-    factor = lax.rsqrt(jnp.mean(x * x, axis=-1, keepdims=True) + epsilon)
-    unit = x * factor
-    gain_grad = jnp.sum(normed_grad * unit, axis=0, keepdims=True)
-    scaled = normed_grad * gain[...]
-    inner = jnp.mean(scaled * unit, axis=-1, keepdims=True)
-    grad[...] = middle_grad[...] + factor * (scaled - unit * inner)
+    gain_sum[...] = jnp.zeros_like(gain_sum)
+
+    def norm_back(part, normed_grad):
+        x = tok[part, :].astype(jnp.float32)
+        factor = lax.rsqrt(jnp.mean(x * x, axis=-1, keepdims=True) + epsilon)
+        unit = x * factor
+        gain_sum[...] += jnp.sum(normed_grad * unit, axis=0, keepdims=True)
+        scaled = normed_grad * gain[...]
+        inner = jnp.mean(scaled * unit, axis=-1, keepdims=True)
+        grad[part, :] = middle_grad[part, :] + factor * (scaled - unit * inner)
+
+    grads.total(norm_back)
+    gain_grad = gain_sum[...]
     shard = mine_gain.shape[1]
     count = mine_gain.shape[0] // 2
     for at in range(count):
@@ -1174,6 +956,15 @@
             move.start()
         move.relay()
         move.rest()
+    lax.fori_loop(0, 4, ours, 0)
+    sums.across()
+    sums.beside()
+    sums.turn()
+
+    def finish_rows(part, down_sum):
+        result[part, :] = (middle[part, :] + down_sum).astype(jnp.bfloat16)
+
+    sums.total(finish_rows)
     ctx_sum.finish()
     plane_sum[...] = jnp.sum(ctx_gain[...], axis=0)
     planes = PlaneShare(place, plane_sum, plane_gain, plane_sem)
@@ -1185,9 +976,10 @@
     for move in moves:
         move.finish()
     grads.finish()
-
-
-def last_moves(pgrad, qkv_w, tok, middle_grad, gain, ffn_gain, low, down_part, gu_part):
+    sums.finish()
+
+
+def last_moves(pgrad, qkv_w, tok, middle_grad, gain, ffn_gain, low, down_part, gu_part, hidden, down_w, middle):
     n, planes = lax.axis_size("ctx"), lax.axis_size("fsdp")
     rows, width = tok.shape
     bf, f32 = jnp.bfloat16, jnp.float32
@@ -1200,18 +992,18 @@
     return pl.pallas_call(
         last_kernel,
         out_shape=(
-            shape((rows, width), f32), shape(small, f32), many(low), many(down_part), many(gu_part),
+            shape((rows, width), f32), shape((rows, width), bf), shape(small, f32), many(low), many(down_part), many(gu_part),
         ),
-        in_specs=vm(9),
-        out_specs=vm(2) + anywhere(3),
+        in_specs=vm(12),
+        out_specs=vm(3) + anywhere(3),
         scratch_shapes=[
-            pltpu.VMEM((4, rows, width), f32), quads, quads, halves, halves,
+            pltpu.VMEM((4, rows, width), f32), quads, quads, halves, halves, quads, quads, halves, halves, pltpu.VMEM((1, width), f32),
             pltpu.VMEM(small, f32), pltpu.VMEM((n,) + small, f32), pltpu.VMEM(small, f32), pltpu.VMEM((planes,) + small, f32),
-            dma((2, Reduce.sems)), dma((2, Gather.sems)), dma((2, Gather.sems)), dma((2, Gather.sems)), dma((2, n)), dma((2, planes)),
+            dma((2, Reduce.sems)), dma((2, Reduce.sems)), dma((2, Gather.sems)), dma((2, Gather.sems)), dma((2, Gather.sems)), dma((2, n)), dma((2, planes)),
         ],
         compiler_params=pltpu.CompilerParams(collective_id=6, has_side_effects=True, vmem_limit_bytes=67043328),
         name="last_moves",
-    )(pgrad, qkv_w, tok, middle_grad, gain, ffn_gain, low, down_part, gu_part)
+    )(pgrad, qkv_w, tok, middle_grad, gain, ffn_gain, low, down_part, gu_part, hidden, down_w, middle)
 
 
 def gathers_kernel(count, *refs):
@@ -1242,37 +1034,303 @@
     )(*arrays)
 
 
-def attend(spans, tokens_all, gain, weight, cosine, sine):
-    length = tokens_all.shape[0]
+class Steps:
+    def __init__(self, *steps):
+        self.steps = list(steps)
+
+    def next(self, count=1):
+        for step in self.steps[:count]:
+            step()
+        self.steps = self.steps[count:]
+
+    def rest(self):
+        self.next(len(self.steps))
+
+
+class OutGather(Gather):
+    def __init__(self, place, own, out, sem):
+        self.place, self.own, self.out, self.sem = place, own, out, sem
+        self.half = out.shape[0] // 2
+        self.started = []
+        self.met = False
+
+    def part(self, rank, half):
+        return self.out.at[pl.ds(half * self.half, self.half), rank]
+
+    def whole(self, rank):
+        return self.out.at[:, rank]
+
+
+def front_kernel(
+    tok, up_low, spot, gain_own, qkv_own, out_own, gu_own, down_own, turn_ref, up,
+    normed, up_all, second_all, hidden, gul, qkv_w, down_w, q_ref, k_ref, v_ref, att_ref, lse_ref, low,
+    middle_grad, middle, gain_grad, spots, gains, agrad, mcols,
+    gu_w, out_block, out_w, qr, kr, vr, low_sorted, gain_all, spots_s,
+    attended, mcols_send, own, mine, theirs, first, out, second,
+    tok_sem, up_sem, spot_sem, gain_sem, qkv_sem, out_sem, outc_sem, gu_sem, down_sem, local_sem,
+    low_sem, gather_sem, reduce_sem, agrad_sem, mcols_sem,
+):
+    place = Place()
+    n = place.n
+    rows = tok.shape[0]
+    half = rows // 2
+    pairs = 8
+    heads = rows
+    greet(place, planes=True)
+    spans = Share(place, spot, spots, spot_sem)
+    scales = PlaneShare(place, gain_own, gain_all, gain_sem)
+    tokens = Gather(place, tok, normed, tok_sem)
+    cots = Gather(place, up_low, up_all, up_sem)
+    qkvs = PlaneGather(place, qkv_own, qkv_w, qkv_sem)
+    outs = PlaneGather(place, out_own, out_block, out_sem)
+    outc = OutGather(place, out_block, out_w, outc_sem)
+    gus = PlaneGather(place, gu_own, gu_w, gu_sem)
+    downs = PlaneGather(place, down_own, down_w, down_sem)
+    fetch = pltpu.make_async_copy(up, middle_grad, local_sem.at[0])
+    fetch.start()
+    spans.start()
+    scales.start()
+    qkvs.start()
+    tokens.start()
+    tokens.relay()
+    qkvs.step(1)
+    outs.start()
+    qkvs.step(2)
+    downs.start()
+    tokens.rest()
+    qkvs.step(3)
+    cots.start()
+    tokens.partner()
+    tokens.finish()
+    spans.finish()
+    scales.finish()
+    qkvs.keep.wait()
+    table = pltpu.make_async_copy(spots, spots_s, local_sem.at[1])
+    table.start()
+    for g in range(2):
+        gains[pl.ds(g, 1), :] = jnp.concatenate([gain_all[z, pl.ds(g, 1), :] for z in range(4)], axis=1)
+    table.wait()
+    early = [spots_s[j, 0, 0] for j in range(pairs)]
+    holder = []
+    for t in range(pairs):
+        at = 0
+        for j in range(pairs):
+            at = jnp.where(early[j] == t, j, at)
+        holder.append(at)
+
+    def block_of(s):
+        return 2 * holder[s] if s < pairs else 2 * holder[2 * pairs - 1 - s] + 1
+
+    def span_of(b):
+        return early[b // 2] if b % 2 == 0 else 2 * pairs - 1 - early[b // 2]
+
+    def project(j, carry):
+        x = normed[pl.ds(2 * j, 2)].reshape(2 * rows, -1).astype(jnp.float32)
+        factor = lax.rsqrt(jnp.mean(x * x, axis=-1, keepdims=True) + epsilon)
+        scaled = (x * factor * gains[pl.ds(0, 1), :]).astype(jnp.bfloat16)
+        normed[pl.ds(2 * j, 2)] = scaled.reshape(2, rows, -1)
+        proj = nn(scaled, qkv_w[...].reshape(-1, 4 * LANES))
+        for piece in range(4):
+            c = spots_s[2 * j + piece // 2, 0, 0]
+            cosine, sine = wave(turn_ref[c if piece % 2 == 0 else 2 * pairs - 1 - c])
+            mine_rows = proj[piece * half : (piece + 1) * half]
+
+            def turned(part):
+                z = mine_rows[:, part * LANES : (part + 1) * LANES]
+                return (z * cosine + pltpu.roll(z, 64, 1) * sine).astype(jnp.bfloat16)
+
+            qr[4 * j + piece, 0] = turned(0)
+            qr[4 * j + piece, 1] = turned(1)
+            kr[4 * j + piece] = turned(2)
+            vr[4 * j + piece] = mine_rows[:, 3 * LANES :].astype(jnp.bfloat16)
+        return carry
+
+    lax.fori_loop(0, 4, project, 0)
+    for s in range(2 * pairs):
+        b = block_of(s)
+        base = (s // 2) * 4 * half + (s % 2) * half
+        both = qr[b]
+        q_ref[pl.ds(base, half), :] = both[0]
+        q_ref[pl.ds(base + 2 * half, half), :] = both[1]
+        k_ref[pl.ds(s * half, half), :] = kr[b]
+        v_ref[pl.ds(s * half, half), :] = vr[b]
+
+    steps = Steps(
+        lambda: outs.step(1), cots.relay, lambda: outs.step(2), lambda: outs.step(3),
+        lambda: (outs.keep.wait(), outc.start(), downs.step(1), gus.start()), cots.rest, outc.relay,
+        lambda: (downs.step(2), outc.rest()), lambda: (cots.partner(), outc.partner()),
+    )
+    scaling = HEAD_DIM ** (-0.5)
+    mask = causal(2 * half)
+    lane = lax.broadcasted_iota(jnp.int32, (half, LANES), 1)
+    values_t = v_ref[...].astype(jnp.float32).T.astype(jnp.bfloat16)
+    for pair in range(pairs):
+        width = (pair + 1) * 2 * half
+        q = q_ref[pl.ds(pair * 4 * half, 4 * half), :]
+        before = width - 2 * half
+        parts = [jnp.where(mask, nt(k_ref[pl.ds(before, 2 * half), :], q) * scaling, -1e30)]
+        if pair:
+            parts.append(nt(k_ref[pl.ds(0, before), :], q) * scaling)
+        tops = [jnp.max(part, axis=0, keepdims=True) for part in parts]
+        top = jnp.maximum(tops[0], tops[-1])
+        parts = [jnp.exp(part - top) for part in parts]
+        total = sum(jnp.sum(part, axis=0, keepdims=True) for part in parts)
+        parts = [(part * (1.0 / total)).astype(jnp.bfloat16) for part in parts]
+        lse_ref[pl.ds(pair, 1), :] = top + jnp.log(total)
+        out_t = nn(values_t[:, before:width], parts[0])
+        if pair:
+            out_t = out_t + nn(values_t[:, :before], parts[1])
+        att_ref[pl.ds(pair * LANES, LANES), :] = out_t
+        result = out_t.T.astype(jnp.bfloat16).astype(jnp.float32)
+        for part in range(2):
+            left = result[part * half : (part + 1) * half]
+            right = pltpu.roll(result[(2 + part) * half : (3 + part) * half], half, 1)
+            low_sorted[2 * pair + part, :, 0:LANES] = jnp.where(lane < half, left, right).astype(jnp.bfloat16)
+            low_sorted[2 * pair + part, :, LANES : 2 * half] = right[:, : 2 * half - LANES].astype(jnp.bfloat16)
+        steps.next()
+    for b in range(2 * pairs):
+        low[b // 2, pl.ds((b % 2) * half, half), :] = low_sorted[span_of(b)]
+    moved = Exchange(place, low, attended, low_sem)
+    moved.start()
+    steps.rest()
+    outc.keep.wait()
+    moved.finish()
+    total = tok[...].astype(jnp.float32)
+    for q in range(8):
+        total = total + nn(attended[q], out_w[q // 2, pl.ds(4 * (q % 2), 4)].reshape(heads, -1))
+    middle[...] = total
+    factor = lax.rsqrt(jnp.mean(total * total, axis=-1, keepdims=True) + epsilon)
+    own[...] = (total * factor * gains[pl.ds(1, 1), :]).astype(jnp.bfloat16)
+    seconds = Gather(place, own, second_all, gather_sem)
+    seconds.start()
+    downs.step(3)
+    gus.step(1)
+    seconds.relay()
+    gus.step(2)
+    seconds.rest()
+    gus.step(3)
+    seconds.partner()
+    gus.keep.wait()
+    downs.keep.wait()
+    seconds.keep.wait()
+    cots.keep.wait()
+    grads = Reduce(place, mine, theirs, first, out, second, reduce_sem)
+    wide = hidden.shape[2]
+
+    def block(i):
+        rank = flip(place, i)
+        gate_up = nn(second_all[rank], gu_w[...].reshape(-1, 2 * wide))
+        gate, raised = gate_up[:, :wide], gate_up[:, wide:]
+        sigmoid = 1.0 / (1.0 + jnp.exp(-gate))
+        silu = gate * sigmoid
+        hidden[rank] = (silu * raised).astype(jnp.bfloat16)
+        hidden_grad = nt(up_all[rank], down_w[...].reshape(wide, -1))
+        gul[rank, :, pl.ds(0, wide)] = (hidden_grad * raised * sigmoid * (1.0 + gate * (1.0 - sigmoid))).astype(jnp.bfloat16)
+        gul[rank, :, pl.ds(wide, wide)] = (hidden_grad * silu).astype(jnp.bfloat16)
+        return nt(gul[rank], gu_w[...].reshape(-1, 2 * wide))
+
+    def pair_of(k, carry):
+        theirs[k] = block(2 * k + 1).astype(jnp.bfloat16)
+        grads.push(k)
+        mine[k] = block(2 * k)
+        return carry
+
+    lax.fori_loop(1, 4, pair_of, 0)
+    grads.across()
+    grads.beside()
+    lax.fori_loop(0, 1, pair_of, 0)
+    grads.turn()
+    fetch.wait()
+    seconds.finish(kept=True)
+    gain_grad[...] = jnp.zeros_like(gain_grad)
+
+    def norm_back(part, second_grad):
+        x = middle[part, :]
+        factor = lax.rsqrt(jnp.mean(x * x, axis=-1, keepdims=True) + epsilon)
+        unit = x * factor
+        gain_grad[...] += jnp.sum(second_grad * unit, axis=0, keepdims=True)
+        scaled = second_grad * gains[pl.ds(1, 1), :]
+        inner = jnp.mean(scaled * unit, axis=-1, keepdims=True)
+        grad = middle_grad[part, :] + factor * (scaled - unit * inner)
+        middle_grad[part, :] = grad
+        own[part, :] = grad.astype(jnp.bfloat16)
+
+    grads.total(norm_back)
+
+    def head_grads(q, carry):
+        weight = out_w[q // 2, pl.ds(4 * (q % 2), 4)].reshape(heads, -1)
+        attended[q] = nt(own[...], weight).astype(jnp.bfloat16)
+        return carry
+
+    lax.fori_loop(0, n, head_grads, 0)
+    heads_back = Exchange(place, attended, agrad, agrad_sem)
+    heads_back.start()
+    for q in range(8):
+        mcols_send[q] = own[:, q * heads : (q + 1) * heads]
+    columns = Exchange(place, mcols_send, mcols, mcols_sem)
+    columns.start()
+    for move in (qkvs, outs, gus, downs):
+        move.finish(kept=True)
+    for move in (cots, outc):
+        move.finish(kept=True)
+    heads_back.finish()
+    columns.finish()
+    grads.finish()
+
+
+def front_moves(tok, up_low, spot, gain_own, qkv_own, out_own, gu_own, down_own, turns, up):
+    n, planes = lax.axis_size("ctx"), lax.axis_size("fsdp")
+    rows, width = tok.shape
+    length = n * rows
+    wide = planes * down_own.shape[0]
+    bf, f32 = jnp.bfloat16, jnp.float32
+    shape = jax.ShapeDtypeStruct
+    dma = pltpu.SemaphoreType.DMA
     pairs = length // 192
-    shapes = (
-        jax.ShapeDtypeStruct(tokens_all.shape, jnp.bfloat16),
-        jax.ShapeDtypeStruct((2 * length, LANES), jnp.bfloat16),
-        jax.ShapeDtypeStruct((length, LANES), jnp.bfloat16),
-        jax.ShapeDtypeStruct((length, LANES), jnp.bfloat16),
-        jax.ShapeDtypeStruct((pairs * LANES, 384), jnp.float32),
-        jax.ShapeDtypeStruct((length, 192), jnp.bfloat16),
-        jax.ShapeDtypeStruct((pairs, 384), jnp.float32),
-    )
+    halves = pltpu.VMEM((6, rows // 2, width), bf)
+    quads = pltpu.VMEM((4, rows, width), bf)
+    blocks = pltpu.VMEM((n, rows, rows), bf)
+    all_of = lambda x: shape((planes,) + x.shape, x.dtype)
+    gathered = lambda x: pltpu.VMEM((planes,) + x.shape, x.dtype)
+    ring = dma((2, Gather.sems))
+    line = dma((3, planes))
+    swap = dma((2, n))
     return pl.pallas_call(
-        attend_kernel,
-        out_shape=shapes,
-        in_specs=[pl.BlockSpec(memory_space=pltpu.SMEM)] + vm(5),
-        out_specs=vm(7),
-        name="attend",
-    )(spans, tokens_all, gain, weight, cosine, sine)
-
-
-def attend_back(spans, grad, q, k, v, att, lse, cosine, sine):
+        front_kernel,
+        out_shape=(
+            shape((n, rows, width), bf), shape((n, rows, width), bf), shape((n, rows, width), bf),
+            shape((n, rows, wide), bf), shape((n, rows, 2 * wide), bf), all_of(qkv_own), all_of(down_own),
+            shape((2 * length, LANES), bf), shape((length, LANES), bf), shape((length, LANES), bf),
+            shape((pairs * LANES, 384), f32), shape((pairs, 384), f32), shape((n, rows, rows), bf),
+            shape((rows, width), f32), shape((rows, width), f32), shape((1, width), f32), shape((n,) + spot.shape, spot.dtype),
+            shape((2, width), f32), shape((n, rows, rows), bf), shape((n, rows, rows), bf),
+        ),
+        in_specs=vm(9) + anywhere(1),
+        out_specs=vm(18) + anywhere(2),
+        scratch_shapes=[
+            gathered(gu_own), gathered(out_own), pltpu.VMEM((planes, n) + out_own.shape, bf),
+            pltpu.VMEM((16, 2, 96, LANES), bf), pltpu.VMEM((16, 96, LANES), bf), pltpu.VMEM((16, 96, LANES), bf),
+            pltpu.VMEM((16, 96, 192), bf), gathered(gain_own), pltpu.SMEM((n,) + spot.shape, jnp.int32),
+            blocks, blocks, pltpu.VMEM((rows, width), bf),
+            pltpu.VMEM((4, rows, width), f32), quads, quads, halves, halves,
+            ring, ring, swap, dma((2, planes)), line, line, ring, line, line, dma((2,)),
+            swap, ring, dma((2, Reduce.sems)), swap, swap,
+        ],
+        compiler_params=pltpu.CompilerParams(collective_id=1, has_side_effects=True, vmem_limit_bytes=67043328),
+        name="front_moves",
+    )(tok, up_low, spot, gain_own, qkv_own, out_own, gu_own, down_own, turns, up)
+
+
+def attend_back(spans, grad, q, k, v, att, lse, turns):
     length = k.shape[0]
     return pl.pallas_call(
         back_kernel,
         out_shape=jax.ShapeDtypeStruct((length, 4 * LANES), jnp.bfloat16),
-        in_specs=[pl.BlockSpec(memory_space=pltpu.SMEM)] + vm(8),
+        in_specs=[pl.BlockSpec(memory_space=pltpu.SMEM)] + vm(7),
         out_specs=pl.BlockSpec(memory_space=pltpu.VMEM),
         scratch_shapes=[pltpu.VMEM((length, LANES), jnp.float32)] * 2,
         name="attend_back",
-    )(spans, grad, q, k, v, att, lse, cosine, sine)
+    )(spans, grad, q, k, v, att, lse, turns)
 
 
 def fast_body(
@@ -1285,74 +1343,62 @@
     length = n * rows
     width = tokens.shape[2]
     wide = down_weight.shape[1] * planes
+    own = wide // n
+    piece = own // planes
     shard = qkv_weight.shape[1]
     query_width = HEADS * HEAD_DIM
     key_width = KV_HEADS * HEAD_DIM
-
-    def pick(x, axis):
-        return lax.dynamic_index_in_dim(x, me, axis, keepdims=False)
+    cut = lax.dynamic_slice_in_dim
 
     qkv = qkv_weight[0]
-    q_part = pick(qkv[:, :query_width].reshape(shard, n, 2, HEAD_DIM), 1)
-    k_part = pick(qkv[:, query_width : query_width + key_width].reshape(shard, n, 1, HEAD_DIM), 1)
-    v_part = pick(qkv[:, query_width + key_width :].reshape(shard, n, HEAD_DIM), 1)
-    qk = spread(jnp.concatenate([q_part, k_part], axis=1)).reshape(shard, 3 * LANES)
-    qkv_block = jnp.concatenate([qk, jnp.pad(v_part, ((0, 0), (0, LANES - HEAD_DIM)))], axis=1)
-    out_rows = shard // n
-    out_block = pick(out_weight[0].reshape(n, out_rows, width), 0)
-    gate_up_block = pick(gate_up_weight[0].reshape(shard, 2, planes, n, wide // planes // n), 3)
-    gate_up_block = lax.all_gather(gate_up_block, "fsdp", axis=0, tiled=True)
-    gate_up_block = gate_up_block.reshape(planes * shard, 2 * wide // n)
-    down_block = pick(down_weight[0].reshape(n, -1, width), 0)
-    down_block = lax.all_gather(down_block, "fsdp", axis=0, tiled=True)
-    upstream = cotangent[0]
+    q_part = cut(qkv, me * 2 * HEAD_DIM, 2 * HEAD_DIM, 1)
+    k_part = cut(qkv, query_width + me * HEAD_DIM, HEAD_DIM, 1)
+    v_part = cut(qkv, query_width + key_width + me * HEAD_DIM, HEAD_DIM, 1)
+    half = HEAD_DIM // 2
+    gap = jnp.zeros((shard, 64 - half), qkv.dtype)
+    columns = []
+    for part in (q_part[:, :HEAD_DIM], q_part[:, HEAD_DIM:], k_part):
+        columns += [part[:, :half], gap, part[:, half:], gap]
+    qkv_own = jnp.concatenate(columns + [v_part, gap, gap], axis=1)
+    out_own = cut(out_weight[0], me * (shard // n), shard // n, 0)
+    pieces = [cut(gate_up_weight[0], at * (wide // planes) + me * piece, piece, 2) for at in range(planes)]
+    gate_up_own = jnp.concatenate([x[:, s] for s in range(2) for x in pieces], axis=1)
+    down_own = cut(down_weight[0], me * piece, piece, 0)
     gains = jnp.concatenate([attn_gain, ffn_gain, jnp.zeros((6, shard), attn_gain.dtype)], axis=0).astype(jnp.float32)
-    spot = jnp.full((8, LANES), positions[0, 0], jnp.int32)
-    tokens_all, upstream_all, qkv_block, out_block, spots, gains = first_moves(
-        tokens[0], upstream.astype(jnp.bfloat16), qkv_block, out_block.reshape(out_rows, width), spot, gains
-    )
-    tokens_all = tokens_all.reshape(length, width)
-    qkv_block = qkv_block.reshape(width, -1)
-    gains = gains[:, :2].transpose(1, 0, 2).reshape(2, width)
-    attn_full, ffn_full = gains[0], gains[1]
-    (out_full,) = gathers(2, out_block.reshape(planes * out_rows, width))
-    out_full = out_full.reshape(n, planes, out_rows, width).transpose(1, 0, 2, 3).reshape(planes * shard, width)
-
-    early = spots[:, 0, 0] // (rows // 2)
+    spot = jnp.full((8, LANES), positions[0, 0] // (rows // 2), jnp.int32)
+    turns = table(length)
+    (
+        normed, upstream_all, second_all, hidden, gate_up_low, qkv_block, down_block, q, k, v, att, lse, low,
+        middle_grad, middle, ffn_partial, spots, gains, attended_grad, middle_cols,
+    ) = front_moves(
+        tokens[0], cotangent[0].astype(jnp.bfloat16), spot, gains, qkv_own, out_own, gate_up_own, down_own,
+        turns.reshape(2 * n, rows // 2, LANES), cotangent[0],
+    )
+    early = spots[:, 0, 0]
     span = jnp.stack([early, 2 * n - 1 - early], axis=1).reshape(2 * n)
-    order = jnp.sum(
+    order = jnp.max(
         jnp.where(span[None, :] == jnp.arange(2 * n)[:, None], jnp.arange(2 * n)[None, :], 0), axis=1
     )
     spans = jnp.concatenate([span, order]).astype(jnp.int32)
-    cosine, sine = tables(length)
-
-    normed, q, k, v, att, low, lse = attend(spans, tokens_all, attn_full[None], qkv_block, cosine, sine)
-
-    second_all, hidden, gate_up_low, attended_grad, middle_cols, middle_grad, result, ffn_partial = middle_moves(
-        low.reshape(n, rows, -1), tokens[0], upstream, upstream_all, out_full, gate_up_block, down_block, ffn_full[None]
-    )
-    own = wide // n
-    second_all = second_all.reshape(length, width)
-    hidden = hidden.reshape(length, own)
-    gate_up_low = gate_up_low.reshape(length, 2 * own)
+
+    def flat(x):
+        return x.reshape(length, -1)
 
     def reduce_planes(block):
         return lax.psum_scatter(block.astype(jnp.bfloat16), "fsdp", scatter_dimension=0, tiled=True)
 
-    down_grad = reduce_planes(tn(hidden, upstream_all.reshape(length, width)))
-    gate_up_grad = reduce_planes(tn(second_all, gate_up_low))
-    projected_grad = attend_back(
-        spans, attended_grad.reshape(length, -1), q, k, v, att, lse, cosine, sine
-    )
-    stream_grad, gains, low_all, down_grad, gate_up_grad = last_moves(
-        projected_grad.reshape(n, rows, -1), qkv_block, tokens[0], middle_grad, attn_full[None], ffn_partial,
-        low, down_grad, gate_up_grad,
+    down_grad = reduce_planes(tn(flat(hidden), flat(upstream_all)))
+    gate_up_grad = reduce_planes(tn(flat(second_all), flat(gate_up_low)))
+    projected_grad = attend_back(spans, flat(attended_grad), q, k, v, att, lse, turns)
+    stream_grad, result, gain_grads, low_all, down_grad, gate_up_grad = last_moves(
+        projected_grad.reshape(n, rows, -1), qkv_block, tokens[0], middle_grad, gains[0:1], ffn_partial,
+        flat(low), down_grad, gate_up_grad, hidden, down_block, middle,
     )
     low_all = low_all.transpose(1, 0, 2).reshape(length, query_width)
-    gains = gains.reshape(2, planes, shard)
-    gains = lax.dynamic_index_in_dim(gains, lax.axis_index("fsdp"), 1, keepdims=False)
-    qkv_grad = reduce_planes(tn(normed, projected_grad))
-    out_grad = reduce_planes(tn(low_all, middle_cols.reshape(length, -1)))
+    gain_grads = gain_grads.reshape(2, planes, shard)
+    gain_grads = lax.dynamic_index_in_dim(gain_grads, lax.axis_index("fsdp"), 1, keepdims=False)
+    qkv_grad = reduce_planes(tn(flat(normed), projected_grad))
+    out_grad = reduce_planes(tn(low_all, flat(middle_cols)))
     qkv_grad, out_grad = gathers(7, qkv_grad, out_grad)
     pieces = qkv_grad.reshape(n, shard, 4, LANES).transpose(1, 0, 2, 3)
     qkv_grad = jnp.concatenate(
@@ -1374,8 +1420,8 @@
         out_grad[None],
         gate_up_grad[None],
         down_grad[None],
-        gains[0][None],
-        gains[1][None],
+        gain_grads[0][None],
+        gain_grads[1][None],
     )
 
 

time: 672 us -> 583 us (0.87)
  Pallas kernels: 413 us -> 357 us
  local copies, waits for them, and re-layouts: 121 us -> 95 us
    pallas_call x4 -> x2, Pallas kernels: 347 us -> 318 us  [the longest x1 189 us: front_moves(): pl.pallas_call(front_kernel, out_shape=(shape((n, rows, width), bf), shap...]
    pallas_call x2 -> x1, Pallas kernels: 54.8 us -> 27.3 us  [gathers(): pl.pallas_call(functools.partial(gathers_kernel, count), out_shape=tuple(...]
    unnamed x34 -> x35, local copies, waits for them, and re-layouts: 30.3 us -> 15.6 us
    reshape x4 -> x1, local copies, waits for them, and re-layouts: 11.2 us -> 0.01 us  [fast_body(): gain_grads = gain_grads.reshape(2, planes, shard)]
  transfers between devices with their start and end apart: 6 -> 4, of which waited for: 2 -> 2; matrix products, arithmetic and copies ran while one was open for 17% -> 14% of each run, Pallas kernels for 40% -> 24%
where the time goes in v2:
time: 583 us; the launch traced here: 578 us
  Pallas kernels  357 us (61%)
  local copies, waits for them, and re-layouts  95 us (16%)
  waiting for transfers between devices  66.7 us (11%)
  matrix products  26.4 us (5%)
  between operations  16.4 us (3%)
  other arithmetic  15.9 us (3%)
    pallas_call x1, Pallas kernels, front_moves(): pl.pallas_call(front_kernel, out_shape=(shape((n, rows, width), bf), shap...  189 us
    pallas_call x1, Pallas kernels, last_moves(): pl.pallas_call(last_kernel, out_shape=(shape((rows, width), f32), shape((...  129 us
    reduce_scatter x4, waiting for transfers between devices, reduce_planes(): lax.psum_scatter(block.astype(jnp.bfloat16), 'fsdp', scatter_dimension=0,...  66.7 us
    convert_element_type x3, local copies, waits for them, and re-layouts, fast_body(): gate_up_grad = gate_up_grad.reshape(shard, 2, wide).astype(jnp.float32)  45.1 us
    pallas_call x1, Pallas kernels, gathers(): pl.pallas_call(functools.partial(gathers_kernel, count), out_shape=tuple(...  27.3 us
    dot_general x4, matrix products, tn(): lax.dot_general(left, right, (((0,), (0,)), ((), ())), preferred_element_...  26.4 us
    unnamed x35, local copies, waits for them, and re-layouts  15.6 us
  transfers between devices with their start and end apart: 4, of which 2 were waited for; matrix products, arithmetic and copies ran while one was open for 14% of the time, Pallas kernels for 24%

profile of v2, /device:TPU:0, one launch (start us, length us, event | category | flops | bytes accessed | tf_op | source)
XLA Modules:
  0.0 577.6 jit_solution(6128032054645120765)
XLA Ops:
  10.4 2.1 bitcast_convert_fusion.2.up_low
  12.5 1.8 constant_dynamic-slice_fusion.2
  19.6 2.9 fusion.2
  26.6 1.8 dynamic-slice_bitcast_fusion.down_own
  32.4 189.5 %front_moves.1 = (bf16[8,192,1536]{2,1,0:T(8,128)(2,1)}, bf16[8,192,1536]{2,1,0:T(8,128)(2,1)}, bf16[8,192,1536]{2,1,0:T(8,128)(2,1)}, bf16[8,192,512]{2,1,0:T(8...) custom-call(bf16[192,1536]{1,0:T(8,128)(2,1)} %bitcast.115, ...), custom_call_target="tpu_custom_call" | custom-call | tf_op jit(solution)/shard_map/front_moves/pallas_call | solution.py:1298
  221.9 6.7 %fusion = bf16[512,1536]{1,0:T(8,128)(2,1)} fusion(bf16[8,192,512]{2,1,0:T(8,128)(2,1)} %get-tuple-element.48.hidden, bf16[8,192,1536]{2,1,0:T(8,128)(2,1)} %get-tuple-element.49), kind=kOutput, calls=%fused_computation.4 | convolution fusion | flops 2416705536 | bytes 7864320 | tf_op jit(solution)/shard_map/dot_general | solution.py:504
  228.7 9.0 %bitcast_convert_fusion = bf16[1536,1024]{1,0:T(8,128)(2,1)} fusion(bf16[8,192,1536]{2,1,0:T(8,128)(2,1)} %get-tuple-element.50, bf16[8,192,1024]{2,1,0:T(8,128)(2,1)S(1)} %copy-done.10), kind=kOutput, calls=%fused_computation | convolution fusion | flops 4833411072 | bytes 11010048 | tf_op jit(solution)/shard_map/dot_general | solution.py:504
  239.7 11.4 %attend_back.1 = bf16[1536,512]{1,0:T(8,128)(2,1)} custom-call(s32[32]{0:T(128)} %pad_add_fusion.1.span, bf16[1536,192]{1,0:T(8,128)(2,1)} %bitcast.121, bf16[3072,128]{1,0:T(8,128)(2,1)} %get-tuple-element.38.q_ref, bf16[1536,128]{1,0:T(8,128)(2,1)} %get-tuple-element.39.k_ref, bf16[1536,128]{1,0:T(8,128)(2,1)} %get-tuple-element.40.v_ref, ...), custom_call_target="tpu_custom_call" | custom-call | tf_op jit(solution)/shard_map/attend_back/pallas_call | solution.py:1326
  251.1 6.7 %convolution_convert_fusion = bf16[1536,512]{1,0:T(8,128)(2,1)} fusion(bf16[1536,1536]{1,0:T(8,128)(2,1)} %bitcast.124, bf16[1536,512]{1,0:T(8,128)(2,1)} %attend_back.1), kind=kOutput, calls=%fused_computation.5 | convolution fusion | flops 2416705536 | bytes 7864320 | tf_op jit(solution)/shard_map/dot_general | solution.py:504
  258.7 4.5 reduce-scatter.5.cloned.1.call-done.down_part
  263.2 62.2 %reduce-scatter.7.cloned.1.call-done.gu_part = bf16[384,1024]{1,0:T(8,128)(2,1)} async-done(((bf16[1536,1024]{1,0:T(8,128)(2,1)}), bf16[384,1024]{1,0:T(8,128)(2,1)}) %reduce-scatter.7.cloned.1.call-update) | async-done | bytes 786448 | tf_op jit(solution)/shard_map/reduce_scatter | solution.py:1388
  325.4 128.5 %last_moves.1 = (f32[192,1536]{1,0:T(8,128)}, bf16[192,1536]{1,0:T(8,128)(2,1)}, f32[8,384]{1,0:T(8,128)}, bf16[8,1536,192]{2,1,0:T(8,128)(2,1)}, bf16[8,128,153...) custom-call(bf16[8,192,512]{2,1,0:T(8,128)(2,1)} %bitcast.110, bf16[4,384,512]{2,1,0:T(8,128)(2,1)} %get-tuple-element.43.qkv_w, ...), custom_call_target="tpu_custom_call" | custom-call | tf_op jit(solution)/shard_map/last_moves/pallas_call | solution.py:992
  453.9 8.0 %copy.60 = bf16[1536,8,192]{0,2,1:T(8,128)(2,1)} copy(bf16[1536,8,192]{2,0,1:T(8,128)(2,1)} %bitcast.109) | data formatting | bytes 9437184 | tf_op jit(solution)/shard_map/transpose | solution.py:1397
  461.9 4.0 convolution_convert_fusion.1
  467.1 12.9 %reshape.190 = f32[8,384,2,4,128]{4,3,2,1,0:T(4,128)} reshape(bf16[8,384,1024]{2,1,0:T(8,128)(2,1)} %get-tuple-element.61) | data formatting | bytes 18874368 | tf_op jit(solution)/shard_map/convert_element_type | solution.py:1414
  480.0 16.5 %copy.66 = f32[384,2,4,8,128]{4,3,2,1,0:T(8,128)} copy(f32[384,2,4,8,128]{4,2,1,0,3:T(4,128)} %bitcast.102) | data formatting | bytes 25165824 | tf_op jit(solution)/shard_map/convert_element_type | solution.py:1414
  496.5 15.7 %reshape.188 = f32[1,384,2,4096]{3,2,1,0:T(2,128)} reshape(f32[384,2,4,8,128]{4,3,2,1,0:T(8,128)} %copy.66) | data formatting | bytes 25165824 | tf_op jit(solution)/shard_map/convert_element_type | solution.py:1414
  512.8 3.6 bitcast_convert_fusion.1
  516.4 27.3 %gathers.1 = (bf16[8,384,512]{2,1,0:T(8,128)(2,1)}, bf16[8,384,192]{2,1,0:T(8,128)(2,1)}) custom-call(bf16[384,512]{1,0:T(8,128)(2,1)} %reduce-scatter.9.cloned.1.call-done.refs_0_, bf16[384,192]{1,0:T(8,128)(2,1)} %reduce-scatter.11.cloned.1.call-done.refs_1_), custom_call_target="tpu_custom_call" | custom-call | tf_op jit(solution)/shard_map/gathers/pallas_call | solution.py:1026
  543.7 3.5 copy.69
  553.2 2.4 maximum_convert_fusion
  555.7 6.0 %copy.67 = f32[1,384,3072]{2,1,0:T(8,128)} copy(f32[1,384,3072]{1,2,0:T(8,128)} %maximum_convert_fusion) | data formatting | bytes 9437184
  563.4 2.2 copy.65
  565.6 3.2 copy.68
  (80 shorter events, 28.8 us)
Async XLA Ops:
  7.2 256.0 %reduce-scatter.5.cloned.1.call-start = ((), (), s32[]{:S(2)}) async-start(), calls=%async_computation.4 | async-start | bytes 1966080 | tf_op jit(solution)/shard_map/reduce_scatter | solution.py:1388
  19.6 10.0 %copy-start.8 = (bf16[1,384]{1,0:T(2,128)(2,1)S(1)}, bf16[1,384]{1,0:T(2,128)(2,1)}, u32[]{:S(2)}) copy-start(bf16[1,384]{1,0:T(2,128)(2,1)} %param.16) | copy-start | bytes 2308
  19.6 10.0 %copy-start.9 = (bf16[1,384]{1,0:T(2,128)(2,1)S(1)}, bf16[1,384]{1,0:T(2,128)(2,1)}, u32[]{:S(2)}) copy-start(bf16[1,384]{1,0:T(2,128)(2,1)} %param.15) | copy-start | bytes 2308
  221.9 6.8 %copy-start.10 = (bf16[8,192,1024]{2,1,0:T(8,128)(2,1)S(1)}, bf16[8,192,1024]{2,1,0:T(8,128)(2,1)}, u32[]{:S(2)}) copy-start(bf16[8,192,1024]{2,1,0:T(8,128)(2,1)} %get-tuple-element.51) | copy-start | bytes 9437188
  228.6 96.7 %reduce-scatter.7.cloned.1.call-start = ((), (), s32[]{:S(2)}) async-start(), calls=%async_computation.5 | async-start | bytes 3932160 | tf_op jit(solution)/shard_map/reduce_scatter | solution.py:1388
  237.7 278.7 %reduce-scatter.9.cloned.1.call-start = ((), (), s32[]{:S(2)}) async-start(), calls=%async_computation.6 | async-start | bytes 1966080 | tf_op jit(solution)/shard_map/reduce_scatter | solution.py:1388
  251.1 7.0 %copy-start.7 = (f32[2,1536]{1,0:T(2,128)S(1)}, f32[2,1536]{1,0:T(2,128)}, u32[]{:S(2)}) copy-start(f32[2,1536]{1,0:T(2,128)} %get-tuple-element.45) | copy-start | bytes 36868
  257.8 258.6 %reduce-scatter.11.cloned.1.call-start = ((), (), s32[]{:S(2)}) async-start(), calls=%async_computation.7 | async-start | bytes 983040 | tf_op jit(solution)/shard_map/reduce_scatter | solution.py:1388
  453.9 8.0 %copy-start.11 = (bf16[8,192,192]{2,1,0:T(8,128)(2,1)S(1)}, bf16[8,192,192]{2,1,0:T(8,128)(2,1)}, u32[]{:S(2)}) copy-start(bf16[8,192,192]{2,1,0:T(8,128)(2,1)} %get-tuple-element.58) | copy-start | bytes 1769476
  496.5 15.7 %copy-start.6 = (f32[8,384]{1,0:T(8,128)S(1)}, f32[8,384]{1,0:T(8,128)}, u32[]{:S(2)}) copy-start(f32[8,384]{1,0:T(8,128)} %get-tuple-element.63) | copy-start | bytes 36868
  496.5 16.3 %copy-start = (bf16[8,128,1536]{2,1,0:T(8,128)(2,1)S(1)}, bf16[8,128,1536]{2,1,0:T(8,128)(2,1)}, u32[]{:S(2)}) copy-start(bf16[8,128,1536]{2,1,0:T(8,128)(2,1)} %get-tuple-element.62) | copy-start | bytes 9437188
  551.7 1.3 copy-start.2
  551.7 1.3 copy-start.3
  552.1 1.2 copy-start.1
  565.6 3.2 copy-start.5
  565.6 4.0 copy-start.4
Sparse Core Ops, SparseCore 0:
  228.8 34.3 reduce-scatter.4
  266.0 59.2 reduce-scatter.6
  327.7 35.3 reduce-scatter.8
  467.2 21.2 reduce-scatter.10

commit v3 on v2

--- a/solution.py
+++ b/solution.py
@@ -511,71 +511,6 @@
     return key_at <= query_at
 
 
-def back_kernel(
-    span, grad_ref, q_ref, k_ref, v_ref, att_ref, lse_ref, turn_ref,
-    out_ref, dk_ref, dv_ref,
-):
-    length = k_ref.shape[0]
-    half = 96
-    pairs = length // (2 * half)
-    scaling = HEAD_DIM ** (-0.5)
-    mask = causal(2 * half)
-    lane = lax.broadcasted_iota(jnp.int32, (half, LANES), 1)
-    keys_t = k_ref[...].astype(jnp.float32).T.astype(jnp.bfloat16)
-    for pair in reversed(range(pairs)):
-        width = (pair + 1) * 2 * half
-        q = q_ref[pl.ds(pair * 4 * half, 4 * half), :]
-        firsts, seconds = [], []
-        for part in range(2):
-            at = span[2 * pairs + 2 * pair + part]
-            rows = pl.ds(pl.multiple_of(at * half, half), half)
-            left = grad_ref[rows, 0:LANES].astype(jnp.float32)
-            right = jnp.concatenate(
-                [grad_ref[rows, LANES : 2 * half].astype(jnp.float32), jnp.zeros((half, 64), jnp.float32)], axis=1
-            )
-            firsts.append(jnp.where(lane < half, left, 0.0))
-            seconds.append(pltpu.roll(jnp.where(lane < half, right, left), LANES - half, 1))
-        seconds = [jnp.where(lane < half, s, 0.0) for s in seconds]
-        grads = jnp.concatenate(firsts + seconds, axis=0)
-        delta = jnp.sum(grads.T * att_ref[pl.ds(pair * LANES, LANES), :], axis=0, keepdims=True)
-        grads = grads.astype(jnp.bfloat16)
-        keys = k_ref[pl.ds(0, width), :]
-        weights = jnp.exp(nt(keys, q) * scaling - lse_ref[pl.ds(pair, 1), :])
-        last = jnp.where(mask, weights[width - 2 * half :], 0.0)
-        weights = last if pair == 0 else jnp.concatenate([weights[: width - 2 * half], last], axis=0)
-        dp = nt(v_ref[pl.ds(0, width), :], grads)
-        ds = (weights * (dp - delta)).astype(jnp.bfloat16)
-        dk = nn(ds, q) * scaling
-        dv = nn(weights.astype(jnp.bfloat16), grads)
-        if pair == pairs - 1:
-            dk_ref[...] = dk
-            dv_ref[...] = dv
-        else:
-            dk_ref[pl.ds(0, width), :] += dk
-            dv_ref[pl.ds(0, width), :] += dv
-        dq = nn(keys_t[:, :width], ds).T * scaling
-        for part in range(2):
-            at = span[2 * pairs + 2 * pair + part]
-            rows = pl.ds(pl.multiple_of(at * half, half), half)
-            spot = pl.ds((2 * pair + part) * half, half)
-            cosine, sine = wave(turn_ref[spot, :])
-            for head in range(2):
-                z = dq[(2 * head + part) * half : (2 * head + part + 1) * half]
-                out_ref[rows, head * LANES : (head + 1) * LANES] = (
-                    z * cosine - pltpu.roll(z, 64, 1) * sine
-                ).astype(jnp.bfloat16)
-    for block in range(2 * pairs):
-        at = span[2 * pairs + block]
-        rows = pl.ds(pl.multiple_of(at * half, half), half)
-        spot = pl.ds(block * half, half)
-        z = dk_ref[spot, :]
-        cosine, sine = wave(turn_ref[spot, :])
-        out_ref[rows, 2 * LANES : 3 * LANES] = (
-            z * cosine - pltpu.roll(z, 64, 1) * sine
-        ).astype(jnp.bfloat16)
-        out_ref[rows, 3 * LANES :] = dv_ref[spot, :].astype(jnp.bfloat16)
-
-
 def vm(count):
     return [pl.BlockSpec(memory_space=pltpu.VMEM)] * count
 
@@ -886,152 +821,6 @@
 
 def flip(place, i):
     return place.me + (i % 2) * place.dp + ((i // 2) % 2) * place.dx + (i // 4) * place.dy
-
-
-def last_kernel(
-    pgrad, qkv_w, tok, middle_grad, gain, ffn_gain, low, down_part, gu_part, hidden, down_w, middle,
-    grad, result, gains, low_all, down_all, gu_all,
-    mine, theirs, first, out, second, theirs2, first2, out2, second2, gain_sum, mine_gain, ctx_gain, plane_sum, plane_gain,
-    reduce_sem, reduce_sem2, gather_sem, down_sem, gu_sem, gain_sem, plane_sem,
-):
-    place = Place()
-    greet(place, planes=True)
-    grads = Reduce(place, mine, theirs, first, out, second, reduce_sem)
-    pgrad_width = tok.shape[1]
-
-    def push(k, carry):
-        theirs[k] = nt(pgrad[flip(place, 2 * k + 1)], qkv_w[...].reshape(pgrad_width, -1)).astype(jnp.bfloat16)
-        grads.push(k)
-        return carry
-
-    def keep(k, carry):
-        mine[k] = nt(pgrad[flip(place, 2 * k)], qkv_w[...].reshape(pgrad_width, -1))
-        return carry
-
-    lax.fori_loop(0, 4, push, 0)
-    lax.fori_loop(0, 4, keep, 0)
-    grads.across()
-    grads.beside()
-    sums = Reduce(place, mine, theirs2, first2, out2, second2, reduce_sem2)
-
-    def other(k, carry):
-        theirs2[k] = nn(hidden[flip(place, 2 * k + 1)], down_w[...].reshape(-1, pgrad_width)).astype(jnp.bfloat16)
-        sums.push(k)
-        return carry
-
-    def ours(k, carry):
-        mine[k] = nn(hidden[flip(place, 2 * k)], down_w[...].reshape(-1, pgrad_width))
-        return carry
-
-    lax.fori_loop(0, 4, other, 0)
-    grads.turn()
-    moves = [
-        Gather(place, low, low_all, gather_sem),
-        Gather(place, down_part, down_all, down_sem),
-        Gather(place, gu_part, gu_all, gu_sem),
-    ]
-    moves[0].start()
-    gain_sum[...] = jnp.zeros_like(gain_sum)
-
-    def norm_back(part, normed_grad):
-        x = tok[part, :].astype(jnp.float32)
-        factor = lax.rsqrt(jnp.mean(x * x, axis=-1, keepdims=True) + epsilon)
-        unit = x * factor
-        gain_sum[...] += jnp.sum(normed_grad * unit, axis=0, keepdims=True)
-        scaled = normed_grad * gain[...]
-        inner = jnp.mean(scaled * unit, axis=-1, keepdims=True)
-        grad[part, :] = middle_grad[part, :] + factor * (scaled - unit * inner)
-
-    grads.total(norm_back)
-    gain_grad = gain_sum[...]
-    shard = mine_gain.shape[1]
-    count = mine_gain.shape[0] // 2
-    for at in range(count):
-        mine_gain[pl.ds(at, 1), :] = gain_grad[:, at * shard : (at + 1) * shard]
-        mine_gain[pl.ds(count + at, 1), :] = ffn_gain[:, at * shard : (at + 1) * shard]
-    ctx_sum = Share(place, mine_gain, ctx_gain, gain_sem)
-    ctx_sum.start()
-    for at, move in enumerate(moves):
-        if at:
-            move.start()
-        move.relay()
-        move.rest()
-    lax.fori_loop(0, 4, ours, 0)
-    sums.across()
-    sums.beside()
-    sums.turn()
-
-    def finish_rows(part, down_sum):
-        result[part, :] = (middle[part, :] + down_sum).astype(jnp.bfloat16)
-
-    sums.total(finish_rows)
-    ctx_sum.finish()
-    plane_sum[...] = jnp.sum(ctx_gain[...], axis=0)
-    planes = PlaneShare(place, plane_sum, plane_gain, plane_sem)
-    planes.start()
-    for move in moves:
-        move.partner()
-    planes.finish()
-    gains[...] = jnp.sum(plane_gain[...], axis=0)
-    for move in moves:
-        move.finish()
-    grads.finish()
-    sums.finish()
-
-
-def last_moves(pgrad, qkv_w, tok, middle_grad, gain, ffn_gain, low, down_part, gu_part, hidden, down_w, middle):
-    n, planes = lax.axis_size("ctx"), lax.axis_size("fsdp")
-    rows, width = tok.shape
-    bf, f32 = jnp.bfloat16, jnp.float32
-    shape = jax.ShapeDtypeStruct
-    dma = pltpu.SemaphoreType.DMA
-    halves = pltpu.VMEM((6, rows // 2, width), bf)
-    quads = pltpu.VMEM((4, rows, width), bf)
-    small = (2 * planes, width // planes)
-    many = lambda x: shape((n,) + x.shape, x.dtype)
-    return pl.pallas_call(
-        last_kernel,
-        out_shape=(
-            shape((rows, width), f32), shape((rows, width), bf), shape(small, f32), many(low), many(down_part), many(gu_part),
-        ),
-        in_specs=vm(12),
-        out_specs=vm(3) + anywhere(3),
-        scratch_shapes=[
-            pltpu.VMEM((4, rows, width), f32), quads, quads, halves, halves, quads, quads, halves, halves, pltpu.VMEM((1, width), f32),
-            pltpu.VMEM(small, f32), pltpu.VMEM((n,) + small, f32), pltpu.VMEM(small, f32), pltpu.VMEM((planes,) + small, f32),
-            dma((2, Reduce.sems)), dma((2, Reduce.sems)), dma((2, Gather.sems)), dma((2, Gather.sems)), dma((2, Gather.sems)), dma((2, n)), dma((2, planes)),
-        ],
-        compiler_params=pltpu.CompilerParams(collective_id=6, has_side_effects=True, vmem_limit_bytes=67043328),
-        name="last_moves",
-    )(pgrad, qkv_w, tok, middle_grad, gain, ffn_gain, low, down_part, gu_part, hidden, down_w, middle)
-
-
-def gathers_kernel(count, *refs):
-    place = Place()
-    greet(place)
-    moves = [Gather(place, refs[at], refs[count + at], refs[2 * count + at]) for at in range(count)]
-    for move in moves:
-        move.start()
-        move.relay()
-        move.rest()
-    for move in moves:
-        move.partner()
-    for move in moves:
-        move.finish()
-
-
-def gathers(number, *arrays):
-    n = lax.axis_size("ctx")
-    count = len(arrays)
-    return pl.pallas_call(
-        functools.partial(gathers_kernel, count),
-        out_shape=tuple(jax.ShapeDtypeStruct((n,) + x.shape, x.dtype) for x in arrays),
-        in_specs=vm(count),
-        out_specs=anywhere(count),
-        scratch_shapes=[pltpu.SemaphoreType.DMA((2, Gather.sems))] * count,
-        compiler_params=pltpu.CompilerParams(collective_id=number, has_side_effects=True),
-        name="gathers",
-    )(*arrays)
 
 
 class Steps:
@@ -1321,16 +1110,366 @@
     )(tok, up_low, spot, gain_own, qkv_own, out_own, gu_own, down_own, turns, up)
 
 
-def attend_back(spans, grad, q, k, v, att, lse, turns):
-    length = k.shape[0]
+class PlaneReduce:
+    def __init__(self, place, block, recv, sem):
+        self.place, self.block, self.recv, self.sem = place, block, recv, sem
+
+    def hop(self, ok, part, slot, target, first, wait):
+        copy = send(
+            self.block.at[part], self.recv.at[slot], self.sem.at[0, part], self.sem.at[1, slot], fsdp=target
+        )
+
+        @pl.when(ok)
+        def _():
+            if wait:
+                copy.wait_send()
+                return
+            if not first:
+                self.merge(part, part)
+            copy.start()
+
+    def merge(self, part, slot):
+        piece = self.recv.at[slot]
+        pltpu.make_async_copy(piece, piece, self.sem.at[1, slot]).wait()
+        total = self.block[part].astype(jnp.float32) + self.recv[slot].astype(jnp.float32)
+        self.block[part] = total.astype(jnp.bfloat16)
+
+    def ends(self, i, wait=False):
+        z = self.place.z
+        low = z == 0
+        part = jnp.where(low, 3 - i, i)
+        slot = part if i < 2 else jnp.where(low, part, 4)
+        self.hop(jnp.logical_or(low, z == 3), part, slot, jnp.where(low, 1, 2), True, wait)
+
+    def inner(self, up, down, slot_up, slot_down, to_up, to_down, wait=False):
+        z = self.place.z
+        low = z == 1
+        part = jnp.where(low, up, down)
+        slot = jnp.where(low, slot_up, slot_down)
+        self.hop(jnp.logical_or(low, z == 2), part, slot, jnp.where(low, to_up, to_down), False, wait)
+
+    def start(self, wait=False):
+        for i in range(3):
+            self.ends(i, wait)
+
+    def step1(self, wait=False):
+        self.inner(3, 0, 3, 0, 2, 1, wait)
+
+    def step2(self, wait=False):
+        self.inner(2, 1, 2, 4, 2, 1, wait)
+        self.inner(0, 3, 4, 3, 0, 3, wait)
+
+    def total(self):
+        z = self.place.z
+
+        @pl.when(z > 0)
+        def _():
+            self.merge(z, z)
+
+        @pl.when(z < 3)
+        def _():
+            self.merge(z, 4)
+
+    def own(self):
+        return self.block.at[self.place.z]
+
+    def finish(self):
+        self.start(True)
+        self.step1(True)
+        self.step2(True)
+
+
+def back_moves_kernel(
+    early_ref, hidden, agrad, mcols, low, q_ref, k_ref, v_ref, att_ref, lse_ref, turn_ref, qkv_w, down_w, tok, gain,
+    ffn_gain, middle, second_all, gul, up_all, normed, middle_grad,
+    grad, result, gains, low_all, down_all, gu_all, out_all, qkv_all,
+    wide_a, wide_b, low_buf, down_g, gu_g, out_g, qkv_g, down_r, gu_r, out_r, qkv_r,
+    mine, theirs, first, out, second, dk_ref, dv_ref, pg_sorted, pgrad,
+    gain_sum, mine_gain, ctx_gain, plane_sum, plane_gain,
+    free, local_sem, sum_sem, reduce_sem, low_sem, down_zs, gu_zs, out_zs, qkv_zs, down_cs, gu_cs, out_cs, qkv_cs,
+    gain_sem, plane_sem,
+):
+    place = Place()
+    n = place.n
+    rows = tok.shape[0]
+    half = rows // 2
+    pairs = 8
+    width = tok.shape[1]
+    length = n * rows
+    loads = [
+        pltpu.make_async_copy(source, target, local_sem.at[at])
+        for at, (source, target) in enumerate((
+            (up_all, wide_b), (second_all, wide_a), (gul, wide_b.at[:, :, pl.ds(0, gul.shape[2])]),
+            (normed, wide_a), (middle_grad, grad),
+        ))
+    ]
+    loads[0].start()
+    loads[1].start()
+    loads[4].start()
+    greet(place, planes=True)
+    early = [early_ref[j] for j in range(pairs)]
+    holder = []
+    for t in range(pairs):
+        at = 0
+        for j in range(pairs):
+            at = jnp.where(early[j] == t, j, at)
+        holder.append(at)
+
+    def block_of(s):
+        return 2 * holder[s] if s < pairs else 2 * holder[2 * pairs - 1 - s] + 1
+
+    def span_of(b):
+        return early[b // 2] if b % 2 == 0 else 2 * pairs - 1 - early[b // 2]
+
+    down_z = PlaneReduce(place, down_g, down_r, down_zs)
+    gu_z = PlaneReduce(place, gu_g, gu_r, gu_zs)
+    out_z = PlaneReduce(place, out_g, out_r, out_zs)
+    qkv_z = PlaneReduce(place, qkv_g, qkv_r, qkv_zs)
+    sums = Reduce(place, mine, theirs, first, out, second, sum_sem)
+    lows = Gather(place, low, low_all, low_sem)
+
+    loads[0].wait()
+    piece = down_g.shape[1]
+
+    def down_block(t, carry):
+        left = hidden[:, :, pl.ds(pl.multiple_of(t * piece, piece), piece)].reshape(length, piece)
+        down_g[t] = tn(left, wide_b[...].reshape(length, width)).astype(jnp.bfloat16)
+        return carry
+
+    lax.fori_loop(0, 4, down_block, 0)
+    down_z.start()
+    loads[2].start()
+
+    def other(k, carry):
+        theirs[k] = nn(hidden[flip(place, 2 * k + 1)], down_w[...].reshape(-1, width)).astype(jnp.bfloat16)
+        sums.push(k)
+        return carry
+
+    def ours(k, carry):
+        mine[k] = nn(hidden[flip(place, 2 * k)], down_w[...].reshape(-1, width))
+        return carry
+
+    lax.fori_loop(0, 4, other, 0)
+    lax.fori_loop(0, 4, ours, 0)
+    sums.across()
+    sums.beside()
+    loads[1].wait()
+    loads[2].wait()
+    shard = gu_g.shape[1]
+
+    def gu_block(t, carry):
+        left = wide_a[:, :, pl.ds(pl.multiple_of(t * shard, shard), shard)].reshape(length, shard)
+        right = wide_b[:, :, pl.ds(0, gul.shape[2])].reshape(length, gul.shape[2])
+        gu_g[t] = tn(left, right).astype(jnp.bfloat16)
+        return carry
+
+    lax.fori_loop(0, 4, gu_block, 0)
+    gu_z.start()
+    loads[3].start()
+    down_z.step1()
+    sums.turn()
+    lows.start()
+
+    def finish_rows(part, down_sum):
+        result[part, :] = (middle[part, :] + down_sum).astype(jnp.bfloat16)
+
+    def sums_done():
+        sums.total(finish_rows)
+        sums.finish()
+        for rank in (place.p, place.x, place.y):
+            pl.semaphore_signal(free, inc=1, device_id={"ctx": rank}, device_id_type=MESH)
+
+    downs = Gather(place, down_z.own(), down_all, down_cs)
+    gus = Gather(place, gu_z.own(), gu_all, gu_cs)
+    steps = Steps(
+        sums_done, down_z.step2, lows.relay, lambda: (down_z.total(), gu_z.step1()), lows.rest,
+        downs.start, downs.relay, lambda: (lows.partner(), downs.rest()),
+    )
+    scaling = HEAD_DIM ** (-0.5)
+    mask = causal(2 * half)
+    lane = lax.broadcasted_iota(jnp.int32, (half, LANES), 1)
+    keys_t = k_ref[...].astype(jnp.float32).T.astype(jnp.bfloat16)
+    for pair in reversed(range(pairs)):
+        q = q_ref[pl.ds(pair * 4 * half, 4 * half), :]
+        firsts, seconds = [], []
+        for part in range(2):
+            piece_of = agrad[block_of(2 * pair + part)].astype(jnp.float32)
+            left = piece_of[:, 0:LANES]
+            right = jnp.concatenate([piece_of[:, LANES : 2 * half], jnp.zeros((half, 64), jnp.float32)], axis=1)
+            firsts.append(jnp.where(lane < half, left, 0.0))
+            seconds.append(pltpu.roll(jnp.where(lane < half, right, left), LANES - half, 1))
+        seconds = [jnp.where(lane < half, s, 0.0) for s in seconds]
+        grads = jnp.concatenate(firsts + seconds, axis=0)
+        delta = jnp.sum(grads.T * att_ref[pl.ds(pair * LANES, LANES), :], axis=0, keepdims=True)
+        grads = grads.astype(jnp.bfloat16)
+        before = pair * 2 * half
+        cuts = [(before, 2 * half)] + [(at, min(768, before - at)) for at in range(0, before, 768)]
+        dq_t = None
+        for at, count in cuts:
+            keys = pl.ds(at, count)
+            weights = jnp.exp(nt(k_ref[keys, :], q) * scaling - lse_ref[pl.ds(pair, 1), :])
+            if at == before:
+                weights = jnp.where(mask, weights, 0.0)
+            dp = nt(v_ref[keys, :], grads)
+            ds = (weights * (dp - delta)).astype(jnp.bfloat16)
+            dk = nn(ds, q) * scaling
+            dv = nn(weights.astype(jnp.bfloat16), grads)
+            if pair == pairs - 1:
+                dk_ref[keys, :] = dk
+                dv_ref[keys, :] = dv
+            else:
+                dk_ref[keys, :] += dk
+                dv_ref[keys, :] += dv
+            term = nn(keys_t[:, at : at + count], ds)
+            dq_t = term if dq_t is None else dq_t + term
+        dq = dq_t.T * scaling
+        for part in range(2):
+            cosine, sine = wave(turn_ref[2 * pair + part])
+            for head in range(2):
+                z = dq[(2 * head + part) * half : (2 * head + part + 1) * half]
+                pg_sorted[2 * pair + part, :, head * LANES : (head + 1) * LANES] = (
+                    z * cosine - pltpu.roll(z, 64, 1) * sine
+                ).astype(jnp.bfloat16)
+        steps.next()
+    for s in range(2 * pairs):
+        spot = pl.ds(s * half, half)
+        cosine, sine = wave(turn_ref[s])
+        z = dk_ref[spot, :]
+        pg_sorted[s, :, 2 * LANES : 3 * LANES] = (z * cosine - pltpu.roll(z, 64, 1) * sine).astype(jnp.bfloat16)
+        pg_sorted[s, :, 3 * LANES :] = dv_ref[spot, :].astype(jnp.bfloat16)
+    for b in range(2 * pairs):
+        pgrad[b // 2, pl.ds((b % 2) * half, half), :] = pg_sorted[span_of(b)]
+    steps.rest()
+
+    loads[3].wait()
+
+    def qkv_block(t, carry):
+        left = wide_a[:, :, pl.ds(pl.multiple_of(t * shard, shard), shard)].reshape(length, shard)
+        qkv_g[t] = tn(left, pgrad[...].reshape(length, 4 * LANES)).astype(jnp.bfloat16)
+        return carry
+
+    lax.fori_loop(0, 4, qkv_block, 0)
+    qkv_z.start()
+    pl.semaphore_wait(free, 3)
+    grads = Reduce(place, mine, theirs, first, out, second, reduce_sem)
+
+    def push(k, carry):
+        theirs[k] = nt(pgrad[flip(place, 2 * k + 1)], qkv_w[...].reshape(width, -1)).astype(jnp.bfloat16)
+        grads.push(k)
+        return carry
+
+    def keep(k, carry):
+        mine[k] = nt(pgrad[flip(place, 2 * k)], qkv_w[...].reshape(width, -1))
+        return carry
+
+    lax.fori_loop(0, 4, push, 0)
+    lax.fori_loop(0, 4, keep, 0)
+    grads.across()
+    grads.beside()
+    lows.keep.wait()
+    for t in range(4):
+        for side in range(2):
+            src = 2 * t + side
+            fetch = pltpu.make_async_copy(low_all.at[src], low_buf, local_sem.at[5 + src])
+            fetch.start()
+            fetch.wait()
+            out_g[t, pl.ds(side * rows, rows), :] = tn(
+                low_buf[...].reshape(length, rows), mcols[...].reshape(length, rows)
+            ).astype(jnp.bfloat16)
+    out_z.start()
+    gu_z.step2()
+    downs.partner()
+    grads.turn()
+    gain_sum[...] = jnp.zeros_like(gain_sum)
+    loads[4].wait()
+
+    def norm_back(part, normed_grad):
+        x = tok[part, :].astype(jnp.float32)
+        factor = lax.rsqrt(jnp.mean(x * x, axis=-1, keepdims=True) + epsilon)
+        unit = x * factor
+        gain_sum[...] += jnp.sum(normed_grad * unit, axis=0, keepdims=True)
+        scaled = normed_grad * gain[...]
+        inner = jnp.mean(scaled * unit, axis=-1, keepdims=True)
+        grad[part, :] = grad[part, :] + factor * (scaled - unit * inner)
+
+    grads.total(norm_back)
+    gain_grad = gain_sum[...]
+    count = mine_gain.shape[0] // 2
+    for at in range(count):
+        mine_gain[pl.ds(at, 1), :] = gain_grad[:, at * shard : (at + 1) * shard]
+        mine_gain[pl.ds(count + at, 1), :] = ffn_gain[:, at * shard : (at + 1) * shard]
+    ctx_sum = Share(place, mine_gain, ctx_gain, gain_sem)
+    ctx_sum.start()
+    qkv_z.step1()
+    gu_z.total()
+    gus.start()
+    out_z.step1()
+    ctx_sum.finish()
+    plane_sum[...] = jnp.sum(ctx_gain[...], axis=0)
+    planes = PlaneShare(place, plane_sum, plane_gain, plane_sem)
+    planes.start()
+    gus.relay()
+    qkv_z.step2()
+    gus.rest()
+    out_z.step2()
+    planes.finish()
+    gains[...] = jnp.sum(plane_gain[...], axis=0)
+    qkv_z.total()
+    qkvs = Gather(place, qkv_z.own(), qkv_all, qkv_cs)
+    qkvs.start()
+    gus.partner()
+    out_z.total()
+    outs = Gather(place, out_z.own(), out_all, out_cs)
+    qkvs.relay()
+    outs.start()
+    qkvs.rest()
+    outs.relay()
+    outs.rest()
+    qkvs.partner()
+    outs.partner()
+    for move in (down_z, gu_z, out_z, qkv_z, downs, gus, outs, qkvs, grads):
+        move.finish()
+    lows.finish(kept=True)
+
+
+def back_moves(early, hidden, agrad, mcols, low, q, k, v, att, lse, turns, qkv_w, down_w, tok, gain, ffn_gain, middle,
+               second_all, gul, up_all, normed, middle_grad):
+    n, planes = lax.axis_size("ctx"), lax.axis_size("fsdp")
+    rows, width = tok.shape
+    length = n * rows
+    wide = hidden.shape[2]
+    shard = width // planes
+    bf, f32 = jnp.bfloat16, jnp.float32
+    shape = jax.ShapeDtypeStruct
+    dma = pltpu.SemaphoreType.DMA
+    halves = pltpu.VMEM((6, rows // 2, width), bf)
+    quads = pltpu.VMEM((4, rows, width), bf)
+    small = (2 * planes, shard)
+    parts = ((wide // planes, width), (shard, 2 * wide), (shard, rows), (shard, 4 * LANES))
+    ring = dma((2, Gather.sems))
     return pl.pallas_call(
-        back_kernel,
-        out_shape=jax.ShapeDtypeStruct((length, 4 * LANES), jnp.bfloat16),
-        in_specs=[pl.BlockSpec(memory_space=pltpu.SMEM)] + vm(7),
-        out_specs=pl.BlockSpec(memory_space=pltpu.VMEM),
-        scratch_shapes=[pltpu.VMEM((length, LANES), jnp.float32)] * 2,
-        name="attend_back",
-    )(spans, grad, q, k, v, att, lse, turns)
+        back_moves_kernel,
+        out_shape=(
+            shape((rows, width), f32), shape((rows, width), bf), shape(small, f32), shape((n,) + low.shape, bf),
+        ) + tuple(shape((n,) + part, bf) for part in parts),
+        in_specs=[pl.BlockSpec(memory_space=pltpu.SMEM)] + vm(16) + anywhere(5),
+        out_specs=vm(3) + anywhere(5),
+        scratch_shapes=[pltpu.VMEM((n, rows, width), bf)] * 2 + [pltpu.VMEM(low.shape, bf)]
+        + [pltpu.VMEM((planes,) + part, bf) for part in parts]
+        + [pltpu.VMEM((planes + 1,) + part, bf) for part in parts]
+        + [
+            pltpu.VMEM((4, rows, width), f32), quads, quads, halves, halves,
+            pltpu.VMEM((length, LANES), f32), pltpu.VMEM((length, LANES), f32),
+            pltpu.VMEM((16, 96, 4 * LANES), bf), pltpu.VMEM((n, rows, 4 * LANES), bf),
+            pltpu.VMEM((1, width), f32), pltpu.VMEM(small, f32), pltpu.VMEM((n,) + small, f32),
+            pltpu.VMEM(small, f32), pltpu.VMEM((planes,) + small, f32),
+            pltpu.SemaphoreType.REGULAR, dma((13,)), dma((2, Reduce.sems)), dma((2, Reduce.sems)), ring,
+            dma((2, 5)), dma((2, 5)), dma((2, 5)), dma((2, 5)), ring, ring, ring, ring, dma((2, n)), dma((2, planes)),
+        ],
+        compiler_params=pltpu.CompilerParams(collective_id=6, has_side_effects=True, vmem_limit_bytes=67043328),
+        name="back_moves",
+    )(early, hidden, agrad, mcols, low, q, k, v, att, lse, turns, qkv_w, down_w, tok, gain, ffn_gain, middle,
+      second_all, gul, up_all, normed, middle_grad)
 
 
 def fast_body(
@@ -1374,32 +1513,13 @@
         tokens[0], cotangent[0].astype(jnp.bfloat16), spot, gains, qkv_own, out_own, gate_up_own, down_own,
         turns.reshape(2 * n, rows // 2, LANES), cotangent[0],
     )
-    early = spots[:, 0, 0]
-    span = jnp.stack([early, 2 * n - 1 - early], axis=1).reshape(2 * n)
-    order = jnp.max(
-        jnp.where(span[None, :] == jnp.arange(2 * n)[:, None], jnp.arange(2 * n)[None, :], 0), axis=1
-    )
-    spans = jnp.concatenate([span, order]).astype(jnp.int32)
-
-    def flat(x):
-        return x.reshape(length, -1)
-
-    def reduce_planes(block):
-        return lax.psum_scatter(block.astype(jnp.bfloat16), "fsdp", scatter_dimension=0, tiled=True)
-
-    down_grad = reduce_planes(tn(flat(hidden), flat(upstream_all)))
-    gate_up_grad = reduce_planes(tn(flat(second_all), flat(gate_up_low)))
-    projected_grad = attend_back(spans, flat(attended_grad), q, k, v, att, lse, turns)
-    stream_grad, result, gain_grads, low_all, down_grad, gate_up_grad = last_moves(
-        projected_grad.reshape(n, rows, -1), qkv_block, tokens[0], middle_grad, gains[0:1], ffn_partial,
-        flat(low), down_grad, gate_up_grad, hidden, down_block, middle,
-    )
-    low_all = low_all.transpose(1, 0, 2).reshape(length, query_width)
+    stream_grad, result, gain_grads, _, down_grad, gate_up_grad, out_grad, qkv_grad = back_moves(
+        spots[:, 0, 0], hidden, attended_grad.reshape(2 * n, rows // 2, -1), middle_cols, low, q, k, v, att, lse,
+        turns.reshape(2 * n, rows // 2, LANES), qkv_block, down_block, tokens[0], gains[0:1], ffn_partial, middle,
+        second_all, gate_up_low, upstream_all, normed, middle_grad,
+    )
     gain_grads = gain_grads.reshape(2, planes, shard)
     gain_grads = lax.dynamic_index_in_dim(gain_grads, lax.axis_index("fsdp"), 1, keepdims=False)
-    qkv_grad = reduce_planes(tn(flat(normed), projected_grad))
-    out_grad = reduce_planes(tn(low_all, flat(middle_cols)))
-    qkv_grad, out_grad = gathers(7, qkv_grad, out_grad)
     pieces = qkv_grad.reshape(n, shard, 4, LANES).transpose(1, 0, 2, 3)
     qkv_grad = jnp.concatenate(
         [
@@ -1426,7 +1546,7 @@
 
 
 def solution(mesh):
-    split = mesh.shape["ctx"] == KV_HEADS
+    split = mesh.shape["ctx"] == KV_HEADS and mesh.shape["fsdp"] == 4
     placed = (
         P("fsdp", "ctx", None),
         P("fsdp", "ctx"),

time: 583 us -> 478 us (0.82)
  waiting for transfers between devices: 66.7 us -> 0 us
  matrix products: 26.4 us -> 0 us
  between operations: 16.4 us -> 3.2 us
    reduce_scatter x4 -> x0, waiting for transfers between devices: 66.7 us -> none  [reduce_planes(): lax.psum_scatter(block.astype(jnp.bfloat16), 'fsdp', scatter_dimension=0,...]
    dot_general x4 -> x0, matrix products: 26.4 us -> none  [tn(): lax.dot_general(left, right, (((0,), (0,)), ((), ())), preferred_element_...]
    transpose x1 -> x0, local copies, waits for them, and re-layouts: 8.03 us -> none  [fast_body(): low_all = low_all.transpose(1, 0, 2).reshape(length, query_width)]
    unnamed x35 -> x23, local copies, waits for them, and re-layouts: 15.6 us -> 18.1 us
    pallas_call x3 -> x1, Pallas kernels: 167 us -> 169 us  [back_moves(): pl.pallas_call(back_moves_kernel, out_shape=(shape((rows, width), f32), s...]
  transfers between devices with their start and end apart: 4 -> 0, of which waited for: 2 -> 0; matrix products, arithmetic and copies ran while one was open for 14% -> 0% of each run, Pallas kernels for 24% -> 0%
where the time goes in v3:
time: 478 us; the launch traced here: 469 us
  Pallas kernels  358 us (75%)
  local copies, waits for them, and re-layouts  90.5 us (19%)
  other arithmetic  17.3 us (4%)
    pallas_call x1, Pallas kernels, front_moves(): pl.pallas_call(front_kernel, out_shape=(shape((n, rows, width), bf), shap...  188 us
    pallas_call x1, Pallas kernels, back_moves(): pl.pallas_call(back_moves_kernel, out_shape=(shape((rows, width), f32), s...  169 us
    convert_element_type x3, local copies, waits for them, and re-layouts, fast_body(): gate_up_grad = gate_up_grad.reshape(shard, 2, wide).astype(jnp.float32)  44.8 us
    unnamed x23, local copies, waits for them, and re-layouts  18.1 us

profile of v3, /device:TPU:0, one launch (start us, length us, event | category | flops | bytes accessed | tf_op | source)
XLA Modules:
  0.0 468.8 jit_solution(9422494614248307568)
XLA Ops:
  0.6 1.8 constant_dynamic-slice_fusion.2
  11.6 1.9 dynamic-slice_bitcast_fusion.down_own
  13.4 1.6 dynamic-slice_bitcast_fusion.2.out_own
  18.1 2.9 fusion.1
  23.8 188.4 %front_moves.1 = (bf16[8,192,1536]{2,1,0:T(8,128)(2,1)}, bf16[8,192,1536]{2,1,0:T(8,128)(2,1)}, bf16[8,192,1536]{2,1,0:T(8,128)(2,1)}, bf16[8,192,512]{2,1,0:T(8...) custom-call(bf16[192,1536]{1,0:T(8,128)(2,1)} %bitcast.93, ...), custom_call_target="tpu_custom_call" | custom-call | tf_op jit(solution)/shard_map/front_moves/pallas_call | solution.py:1087
  212.2 1.3 slice.106.gain
  213.5 1.5 slice_reduce_fusion.early_ref
  215.0 169.5 %back_moves.1 = (f32[192,1536]{1,0:T(8,128)}, bf16[192,1536]{1,0:T(8,128)(2,1)}, f32[8,384]{1,0:T(8,128)}, bf16[8,8,192,192]{3,2,1,0:T(8,128)(2,1)}, bf16[8,128,...) custom-call(s32[8]{0:T(128)} %slice_reduce_fusion.early_ref, ...), custom_call_target="tpu_custom_call" | custom-call | tf_op jit(solution)/shard_map/back_moves/pallas_call | solution.py:1450
  384.5 12.9 %reshape.152 = f32[8,384,2,4,128]{4,3,2,1,0:T(4,128)} reshape(bf16[8,384,1024]{2,1,0:T(8,128)(2,1)} %get-tuple-element.59) | data formatting | bytes 18874368 | tf_op jit(solution)/shard_map/convert_element_type | solution.py:1534
  397.3 16.4 %copy.33 = f32[384,2,4,8,128]{4,3,2,1,0:T(8,128)} copy(f32[384,2,4,8,128]{4,2,1,0,3:T(4,128)} %bitcast.80) | data formatting | bytes 25165824 | tf_op jit(solution)/shard_map/convert_element_type | solution.py:1534
  413.7 15.6 %reshape.150 = f32[1,384,2,4096]{3,2,1,0:T(2,128)} reshape(f32[384,2,4,8,128]{4,3,2,1,0:T(8,128)} %copy.33) | data formatting | bytes 25165824 | tf_op jit(solution)/shard_map/convert_element_type | solution.py:1534
  429.3 3.4 copy.36
  435.0 2.5 copy.30
  437.5 1.7 fusion.13
  439.1 1.3 pad_maximum_fusion.1
  440.4 2.4 copy.31
  442.9 3.9 maximum_convert_fusion
  446.8 6.0 %copy.34 = f32[1,384,3072]{2,1,0:T(8,128)} copy(f32[1,384,3072]{1,2,0:T(8,128)} %maximum_convert_fusion) | data formatting | bytes 9437184
  452.9 1.7 convert_bitcast_fusion
  454.6 2.2 copy.32
  456.7 3.2 copy.35
  459.9 3.6 bitcast_convert_fusion
  464.1 1.9 copy.50
  466.0 2.4 copy.51
  (42 shorter events, 15.8 us)
Async XLA Ops:
  8.9 6.1 %copy-start.5 = (s32[1,192]{1,0:T(1,128)S(1)}, s32[1,192]{1,0:T(1,128)}, u32[]{:S(2)}) copy-start(s32[1,192]{1,0:T(1,128)} %param.10) | copy-start | bytes 2308
  11.5 10.6 %copy-start = (f32[1,192,1536]{2,1,0:T(8,128)S(1)}, f32[1,192,1536]{2,1,0:T(8,128)}, u32[]{:S(2)}) copy-start(f32[1,192,1536]{2,1,0:T(8,128)} %param.17) | copy-start | bytes 3538948
  21.0 2.1 copy-start.3
  21.0 2.1 copy-start.4
  456.7 3.2 copy-start.1
  459.9 3.6 copy-start.2

commit v4 on v3

--- a/solution.py
+++ b/solution.py
@@ -1472,6 +1472,79 @@
       second_all, gul, up_all, normed, middle_grad)
 
 
+def pack_kernel(down, gu, out, qkv, grad, result, down_o, gu_o, out_o, qkv_o, grad_o, result_o):
+    devices, rows = gu.shape[0], gu.shape[1]
+    f32 = jnp.float32
+    lane = lax.broadcasted_iota(jnp.int32, (rows, LANES), 1)
+    half = HEAD_DIM // 2
+    down_o[...] = down[0].astype(f32)
+    grad_o[...] = grad[...]
+    result_o[...] = result[...]
+    tiles = gu_o.shape[0] // rows
+    spans = gu.shape[2] // (2 * LANES)
+    for c in range(devices):
+        for s in range(2):
+            for z in range(spans):
+                piece = gu[c, :, (s * spans + z) * LANES : (s * spans + z + 1) * LANES].astype(f32)
+                gu_o[pl.ds((z * devices + c) * 2 + s, rows, stride=tiles), :] = piece
+
+    def head(c, at, halves):
+        x = qkv[c, :, at * LANES : (at + 1) * LANES].astype(f32)
+        return jnp.where(lane < half, x, pltpu.roll(x, LANES - 64 + half, 1)) if halves else x
+
+    def store(at, heads):
+        second, third, fourth = pltpu.roll(heads[1], 96, 1), pltpu.roll(heads[2], 64, 1), pltpu.roll(heads[3], 32, 1)
+        qkv_o[:, at : at + LANES] = jnp.where(lane < 96, heads[0], second)
+        qkv_o[:, at + LANES : at + 2 * LANES] = jnp.where(lane < 64, second, third)
+        qkv_o[:, at + 2 * LANES : at + 3 * LANES] = jnp.where(lane < 32, third, fourth)
+
+    for c in range(0, devices, 2):
+        store(c * 192, [head(c + i // 2, i % 2, True) for i in range(4)])
+    for c in range(0, devices, 4):
+        store(HEADS * HEAD_DIM + c * 96, [head(c + i, 2, True) for i in range(4)])
+        store((HEADS + KV_HEADS) * HEAD_DIM + c * 96, [head(c + i, 3, False) for i in range(4)])
+    for c in range(0, devices, 2):
+        at = c * 192
+        first = out[c].astype(f32)
+        second = out[c + 1].astype(f32)
+        tail = jnp.concatenate([first[:, LANES:], jnp.zeros((rows, 64), f32)], axis=1)
+        next_tail = jnp.concatenate([second[:, LANES:], jnp.zeros((rows, 64), f32)], axis=1)
+        turned = pltpu.roll(second[:, :LANES], 64, 1)
+        out_o[:, at : at + LANES] = first[:, :LANES]
+        out_o[:, at + LANES : at + 2 * LANES] = jnp.where(lane < 64, tail, turned)
+        out_o[:, at + 2 * LANES : at + 3 * LANES] = jnp.where(lane < 64, turned, pltpu.roll(next_tail, 64, 1))
+
+
+def pack(down, gu, out, qkv, grad, result):
+    n, shard = gu.shape[0], gu.shape[1]
+    rows = shard // n
+    width = down.shape[2]
+    f32 = jnp.float32
+    spec = pl.BlockSpec
+    shape = jax.ShapeDtypeStruct
+    tiles = n * gu.shape[2] // LANES
+    quarter = grad.shape[0] // 4
+    return pl.pallas_call(
+        pack_kernel,
+        grid=(n,),
+        out_shape=(
+            shape((n * down.shape[1], width), f32), shape((shard * tiles, LANES), f32), shape((shard, n * out.shape[2]), f32),
+            shape((shard, (HEADS + 2 * KV_HEADS) * HEAD_DIM), f32), shape(grad.shape, f32), shape(result.shape, result.dtype),
+        ),
+        in_specs=[
+            spec((1,) + down.shape[1:], lambda i: (i, 0, 0)), spec((n, rows, gu.shape[2]), lambda i: (0, i, 0)),
+            spec((n, rows, out.shape[2]), lambda i: (0, i, 0)), spec((n, rows, qkv.shape[2]), lambda i: (0, i, 0)),
+            spec((quarter, width), lambda i: (i // 2, 0)), spec((quarter, width), lambda i: (i // 2, 0)),
+        ],
+        out_specs=[
+            spec((down.shape[1], width), lambda i: (i, 0)), spec((rows * tiles, LANES), lambda i: (i, 0)),
+            spec((rows, n * out.shape[2]), lambda i: (i, 0)), spec((rows, (HEADS + 2 * KV_HEADS) * HEAD_DIM), lambda i: (i, 0)),
+            spec((quarter, width), lambda i: (i // 2, 0)), spec((quarter, width), lambda i: (i // 2, 0)),
+        ],
+        name="pack",
+    )(down, gu, out, qkv, grad, result)
+
+
 def fast_body(
     tokens, positions, qkv_weight, out_weight, gate_up_weight, down_weight, attn_gain, ffn_gain, cotangent
 ):
@@ -1520,19 +1593,10 @@
     )
     gain_grads = gain_grads.reshape(2, planes, shard)
     gain_grads = lax.dynamic_index_in_dim(gain_grads, lax.axis_index("fsdp"), 1, keepdims=False)
-    pieces = qkv_grad.reshape(n, shard, 4, LANES).transpose(1, 0, 2, 3)
-    qkv_grad = jnp.concatenate(
-        [
-            gathered_spread(pieces[:, :, 0:2]).reshape(shard, query_width),
-            gathered_spread(pieces[:, :, 2]).reshape(shard, key_width),
-            pieces[:, :, 3, :HEAD_DIM].reshape(shard, key_width),
-        ],
-        axis=1,
-    ).astype(jnp.float32)
-    out_grad = out_grad.transpose(1, 0, 2).reshape(shard, width).astype(jnp.float32)
-    gate_up_grad = gate_up_grad.reshape(n, shard, 2, planes, -1).transpose(1, 2, 3, 0, 4)
-    gate_up_grad = gate_up_grad.reshape(shard, 2, wide).astype(jnp.float32)
-    down_grad = down_grad.reshape(-1, width).astype(jnp.float32)
+    down_grad, gate_up_grad, out_grad, qkv_grad, stream_grad, result = pack(
+        down_grad, gate_up_grad, out_grad, qkv_grad, stream_grad, result
+    )
+    gate_up_grad = gate_up_grad.reshape(shard, wide // LANES, 2, LANES).transpose(0, 2, 1, 3).reshape(shard, 2, wide)
     return (
         result[None],
         stream_grad[None],

time: 478 us -> 415 us (0.87)
  local copies, waits for them, and re-layouts: 90.5 us -> 18.9 us
  Pallas kernels: 358 us -> 379 us
  other arithmetic: 17.3 us -> 5.61 us
    convert_element_type x4 -> x0, local copies, waits for them, and re-layouts: 47 us -> none  [the longest x3 44.8 us: fast_body(): gate_up_grad = gate_up_grad.reshape(shard, 2, wide).astype(jnp.float32)]
    pallas_call x0 -> x1, Pallas kernels: none -> 21 us  [pack(): pl.pallas_call(pack_kernel, grid=(n,), out_shape=(shape((n * down.shape[1...]
    unnamed x23 -> x17, local copies, waits for them, and re-layouts: 18.1 us -> 4.56 us
    convert_element_type x3 -> x0, other arithmetic: 9.21 us -> none  [the longest x1 3.95 us: fast_body(): qkv_grad = jnp.concatenate([gathered_spread(pieces[:, :, 0:2]).reshape(sh...]
    slice x5 -> x0, local copies, waits for them, and re-layouts: 5.26 us -> none  [the longest x2 3.42 us: fast_body(): pieces[:, :, 2]]
where the time goes in v4:
time: 415 us; the launch traced here: 407 us
  Pallas kernels  379 us (91%)
  local copies, waits for them, and re-layouts  18.9 us (5%)
  other arithmetic  5.61 us (1%)
    pallas_call x1, Pallas kernels, front_moves(): pl.pallas_call(front_kernel, out_shape=(shape((n, rows, width), bf), shap...  189 us
    pallas_call x1, Pallas kernels, back_moves(): pl.pallas_call(back_moves_kernel, out_shape=(shape((rows, width), f32), s...  169 us
    pallas_call x1, Pallas kernels, pack(): pl.pallas_call(pack_kernel, grid=(n,), out_shape=(shape((n * down.shape[1...  21 us

profile of v4, /device:TPU:0, one launch (start us, length us, event | category | flops | bytes accessed | tf_op | source)
XLA Modules:
  0.0 406.8 jit_solution(16504843507209004154)
XLA Ops:
  0.6 1.8 constant_dynamic-slice_fusion.2
  2.5 0.6 fusion.9
  3.2 0.6 fusion.8
  3.9 0.7 fusion.7
  4.5 0.6 fusion.6
  5.2 0.6 fusion.5
  5.8 0.6 fusion.4
  6.5 0.6 fusion.3
  7.1 0.6 fusion.2.gu_own
  7.8 1.1 dynamic-slice_bitcast_fusion.3
  8.9 1.1 dynamic-slice_bitcast_fusion.1
  10.3 1.3 concatenate.17.qkv_own
  11.6 1.9 dynamic-slice_bitcast_fusion.down_own
  13.4 1.6 dynamic-slice_bitcast_fusion.2.out_own
  17.5 0.6 broadcast_in_dim.26.spot
  18.1 2.9 fusion.1
  21.0 1.2 select_maximum_fusion
  22.2 0.9 bitcast_convert_fusion.up_low
  23.1 0.7 maximum_convert_fusion.gain_own
  23.8 188.6 %front_moves.1 = (bf16[8,192,1536]{2,1,0:T(8,128)(2,1)}, bf16[8,192,1536]{2,1,0:T(8,128)(2,1)}, bf16[8,192,1536]{2,1,0:T(8,128)(2,1)}, bf16[8,192,512]{2,1,0:T(8...) custom-call(bf16[192,1536]{1,0:T(8,128)(2,1)} %bitcast.74, ...), custom_call_target="tpu_custom_call" | custom-call | tf_op jit(solution)/shard_map/front_moves/pallas_call | solution.py:1087
  212.4 1.3 slice.85.gain
  213.7 1.5 slice_reduce_fusion.early_ref
  215.2 169.5 %back_moves.1 = (f32[192,1536]{1,0:T(8,128)}, bf16[192,1536]{1,0:T(8,128)(2,1)}, f32[8,384]{1,0:T(8,128)}, bf16[8,8,192,192]{3,2,1,0:T(8,128)(2,1)}, bf16[8,128,...) custom-call(s32[8]{0:T(128)} %slice_reduce_fusion.early_ref, ...), custom_call_target="tpu_custom_call" | custom-call | tf_op jit(solution)/shard_map/back_moves/pallas_call | solution.py:1450
  384.7 21.0 %pack.1 = (f32[1024,1536]{1,0:T(8,128)}, f32[24576,128]{1,0:T(8,128)}, f32[384,1536]{1,0:T(8,128)}, f32[384,3072]{1,0:T(8,128)}, f32[192,1536]{1,0:T(8,128)}, /*index=5*/bf16[192,1536]{1,0:T(8,128)(2,1)}) custom-call(bf16[8,128,1536]{2,1,0:T(8,128)(2,1)} %get-tuple-element.61.down, bf16[8,384,1024]{2,1,0:T(8,128)(2,1)} %get-tuple-element.62.gu, ...), custom_call_target="tpu_custom_call" | custom-call | tf_op jit(solution)/shard_map/pack/pallas_call | solution.py:1527
  (21 shorter events, 1.5 us)
Async XLA Ops:
  8.9 6.1 %copy-start.4 = (s32[1,192]{1,0:T(1,128)S(1)}, s32[1,192]{1,0:T(1,128)}, u32[]{:S(2)}) copy-start(s32[1,192]{1,0:T(1,128)} %param.10) | copy-start | bytes 2308
  11.5 10.6 %copy-start = (f32[1,192,1536]{2,1,0:T(8,128)S(1)}, f32[1,192,1536]{2,1,0:T(8,128)}, u32[]{:S(2)}) copy-start(f32[1,192,1536]{2,1,0:T(8,128)} %param.17) | copy-start | bytes 3538948
  21.0 2.1 copy-start.2
  21.0 2.1 copy-start.3
  384.7 21.1 %copy-start.1 = (f32[8,384]{1,0:T(8,128)S(1)}, f32[8,384]{1,0:T(8,128)}, u32[]{:S(2)}) copy-start(f32[8,384]{1,0:T(8,128)} %get-tuple-element.73) | copy-start | bytes 36868

commit v5 on v4

--- a/solution.py
+++ b/solution.py
@@ -565,9 +565,17 @@
         self.met = False
 
     def go(self, source, target, index, rank):
-        copy = send(source, target, self.sem.at[0, index], self.sem.at[1, index], ctx=rank)
-        copy.start()
-        self.started.append(copy)
+        send(source, target, self.sem.at[0, index], self.sem.at[1, index], ctx=rank).start()
+        self.started.append(index)
+
+    def whole_block(self, index):
+        return index == 6
+
+    def sent(self):
+        p = self.place
+        for index in self.started:
+            part = self.whole(p.me) if self.whole_block(index) else self.part(p.me, 0)
+            send(part, part, self.sem.at[0, index], self.sem.at[1, index], ctx=p.p).wait_send()
 
     def part(self, rank, half):
         return self.out.at[rank, pl.ds(half * self.half, self.half)]
@@ -624,8 +632,7 @@
     def finish(self, kept=False):
         if not kept:
             self.keep.wait()
-        for copy in self.started:
-            copy.wait_send()
+        self.sent()
 
 
 class PlaneGather:
@@ -776,11 +783,13 @@
 
     def go(self, index, value, rank):
         self.out[index] = value.astype(jnp.bfloat16)
-        copy = send(
+        self.turned(index, rank).start()
+        self.started.append((index, rank))
+
+    def turned(self, index, rank):
+        return send(
             self.out.at[index], self.second.at[index], self.sem.at[0, 4 + index], self.sem.at[1, 4 + index], ctx=rank
         )
-        copy.start()
-        self.started.append(copy)
 
     def top(self, slot):
         return self.mine[slot, pl.ds(0, self.half), :]
@@ -815,12 +824,138 @@
 
     def finish(self):
         self.pushed()
-        for copy in self.started:
-            copy.wait_send()
+        for index, rank in self.started:
+            self.turned(index, rank).wait_send()
 
 
 def flip(place, i):
     return place.me + (i % 2) * place.dp + ((i // 2) % 2) * place.dx + (i // 4) * place.dy
+
+
+class HalfGather(Gather):
+    sems = 16
+
+    def __init__(self, place, own, out, sem):
+        self.place, self.own, self.out, self.sem = place, own, out, sem
+        self.half = out.shape[1]
+        self.started = []
+        self.met = False
+
+    def part(self, rank, half):
+        return self.out.at[2 * rank + half]
+
+    def whole_block(self, index):
+        return False
+
+    def start(self):
+        p = self.place
+        halves = [self.own.at[pl.ds(h * self.half, self.half)] for h in range(2)]
+        self.kept = [
+            pltpu.make_async_copy(halves[h], self.part(p.me, h), self.sem.at[0, (13, 15)[h]]) for h in range(2)
+        ]
+        self.go(halves[0], self.part(p.me, 0), 0, p.x)
+        self.go(halves[1], self.part(p.me, 1), 3, p.y)
+        self.go(halves[0], self.part(p.me, 0), 6, p.p)
+        self.go(halves[1], self.part(p.me, 1), 14, p.p)
+        self.go(halves[1], self.part(p.me, 1), 1, p.x)
+        self.go(halves[0], self.part(p.me, 0), 2, p.y)
+        for copy in self.kept:
+            copy.start()
+
+    def first_partner(self):
+        for h in range(2):
+            self.arrived(self.place.p, h, (6, 14)[h])
+        self.met = True
+
+    def own_in(self):
+        for copy in self.kept:
+            copy.wait()
+
+    def finish(self):
+        self.sent()
+
+
+def packed(block):
+    rows = block.shape[0] // 2
+    tail = jnp.concatenate([block[:, LANES:], jnp.zeros((2 * rows, 64), block.dtype)], axis=1)
+    first = lax.broadcasted_iota(jnp.int32, (rows, LANES), 1) < 64
+    return jnp.concatenate([block[:, :LANES], jnp.where(first, tail[:rows], pltpu.roll(tail[rows:], 64, 1))], axis=0)
+
+
+def unpacked(block):
+    rows = block.shape[0] // 3
+    tail = block[2 * rows :].astype(jnp.float32)
+    tails = jnp.concatenate([tail, pltpu.roll(tail, 64, 1)], axis=0)[:, :64].astype(block.dtype)
+    return jnp.concatenate([block[: 2 * rows], tails], axis=1)
+
+
+class PlaneReduce:
+    def __init__(self, place, block, recv, sem):
+        self.place, self.block, self.recv, self.sem = place, block, recv, sem
+
+    def hop(self, ok, part, slot, target, first, wait):
+        copy = send(
+            self.block.at[part], self.recv.at[slot], self.sem.at[0, part], self.sem.at[1, slot], fsdp=target
+        )
+
+        @pl.when(ok)
+        def _():
+            if wait:
+                copy.wait_send()
+                return
+            if not first:
+                self.merge(part, part)
+            copy.start()
+
+    def merge(self, part, slot):
+        piece = self.recv.at[slot]
+        pltpu.make_async_copy(piece, piece, self.sem.at[1, slot]).wait()
+        total = self.block[part].astype(jnp.float32) + self.recv[slot].astype(jnp.float32)
+        self.block[part] = total.astype(jnp.bfloat16)
+
+    def ends(self, i, wait=False):
+        z = self.place.z
+        low = z == 0
+        part = jnp.where(low, 3 - i, i)
+        slot = part if i < 2 else jnp.where(low, part, 4)
+        self.hop(jnp.logical_or(low, z == 3), part, slot, jnp.where(low, 1, 2), True, wait)
+
+    def inner(self, up, down, slot_up, slot_down, to_up, to_down, wait=False):
+        z = self.place.z
+        low = z == 1
+        part = jnp.where(low, up, down)
+        slot = jnp.where(low, slot_up, slot_down)
+        self.hop(jnp.logical_or(low, z == 2), part, slot, jnp.where(low, to_up, to_down), False, wait)
+
+    def start(self, wait=False):
+        for i in range(3):
+            self.ends(i, wait)
+
+    def step1(self, wait=False):
+        self.inner(3, 0, 3, 0, 2, 1, wait)
+
+    def step2(self, wait=False):
+        self.inner(2, 1, 2, 4, 2, 1, wait)
+        self.inner(0, 3, 4, 3, 0, 3, wait)
+
+    def total(self):
+        z = self.place.z
+
+        @pl.when(z > 0)
+        def _():
+            self.merge(z, z)
+
+        @pl.when(z < 3)
+        def _():
+            self.merge(z, 4)
+
+    def own(self):
+        return self.block.at[self.place.z]
+
+    def finish(self):
+        self.start(True)
+        self.step1(True)
+        self.step2(True)
 
 
 class Steps:
@@ -852,12 +987,13 @@
 
 def front_kernel(
     tok, up_low, spot, gain_own, qkv_own, out_own, gu_own, down_own, turn_ref, up,
-    normed, up_all, second_all, hidden, gul, qkv_w, down_w, q_ref, k_ref, v_ref, att_ref, lse_ref, low,
-    middle_grad, middle, gain_grad, spots, gains, agrad, mcols,
-    gu_w, out_block, out_w, qr, kr, vr, low_sorted, gain_all, spots_s,
-    attended, mcols_send, own, mine, theirs, first, out, second,
+    middle_grad, gain_grad, spots, gains, down_sum,
+    hidden_o, qkv_o, down_o, q_o, k_o, v_o, att_o, lse_o, middle_o, normed, agrad, low_all, gu_out, mcols,
+    hidden, qkv_w, down_w, q_ref, k_ref, v_ref, att_ref, lse_ref, middle, mcols_send,
+    wide_in, up_all, gul, gu_w, out_block, out_w, low_sorted, gain_all, spots_s, order_s, low,
+    attended, own, mine, theirs, first, out, second, down_g, down_r,
     tok_sem, up_sem, spot_sem, gain_sem, qkv_sem, out_sem, outc_sem, gu_sem, down_sem, local_sem,
-    low_sem, gather_sem, reduce_sem, agrad_sem, mcols_sem,
+    low_sem, gather_sem, reduce_sem, agrad_sem, lows_sem, down_zs, mcols_sem,
 ):
     place = Place()
     n = place.n
@@ -865,10 +1001,12 @@
     half = rows // 2
     pairs = 8
     heads = rows
+    length = n * rows
+    width = tok.shape[1]
     greet(place, planes=True)
     spans = Share(place, spot, spots, spot_sem)
     scales = PlaneShare(place, gain_own, gain_all, gain_sem)
-    tokens = Gather(place, tok, normed, tok_sem)
+    tokens = HalfGather(place, tok, wide_in, tok_sem)
     cots = Gather(place, up_low, up_all, up_sem)
     qkvs = PlaneGather(place, qkv_own, qkv_w, qkv_sem)
     outs = PlaneGather(place, out_own, out_block, out_sem)
@@ -876,21 +1014,29 @@
     gus = PlaneGather(place, gu_own, gu_w, gu_sem)
     downs = PlaneGather(place, down_own, down_w, down_sem)
     fetch = pltpu.make_async_copy(up, middle_grad, local_sem.at[0])
-    fetch.start()
+    given = []
+
+    def give(source, target):
+        copy = pltpu.make_async_copy(source, target, local_sem.at[5 + len(given)])
+        copy.start()
+        given.append(copy)
+
+    tokens.start()
+    qkvs.start()
     spans.start()
     scales.start()
-    qkvs.start()
-    tokens.start()
+    fetch.start()
     tokens.relay()
     qkvs.step(1)
     outs.start()
     qkvs.step(2)
+    tokens.rest()
+    cots.start()
+    outs.step(1)
     downs.start()
-    tokens.rest()
     qkvs.step(3)
-    cots.start()
     tokens.partner()
-    tokens.finish()
+    tokens.own_in()
     spans.finish()
     scales.finish()
     qkvs.keep.wait()
@@ -900,63 +1046,76 @@
         gains[pl.ds(g, 1), :] = jnp.concatenate([gain_all[z, pl.ds(g, 1), :] for z in range(4)], axis=1)
     table.wait()
     early = [spots_s[j, 0, 0] for j in range(pairs)]
-    holder = []
     for t in range(pairs):
         at = 0
         for j in range(pairs):
             at = jnp.where(early[j] == t, j, at)
-        holder.append(at)
-
-    def block_of(s):
-        return 2 * holder[s] if s < pairs else 2 * holder[2 * pairs - 1 - s] + 1
-
-    def span_of(b):
-        return early[b // 2] if b % 2 == 0 else 2 * pairs - 1 - early[b // 2]
-
-    def project(j, carry):
-        x = normed[pl.ds(2 * j, 2)].reshape(2 * rows, -1).astype(jnp.float32)
+        order_s[t] = 2 * at
+        order_s[2 * pairs - 1 - t] = 2 * at + 1
+    cots.relay()
+
+    def project(j, store):
+        x = jnp.concatenate([wide_in[order_s[4 * j + i]] for i in range(4)], axis=0).astype(jnp.float32)
         factor = lax.rsqrt(jnp.mean(x * x, axis=-1, keepdims=True) + epsilon)
         scaled = (x * factor * gains[pl.ds(0, 1), :]).astype(jnp.bfloat16)
-        normed[pl.ds(2 * j, 2)] = scaled.reshape(2, rows, -1)
+        store[pl.ds(2 * (j % 2), 2)] = scaled.reshape(2, rows, -1)
         proj = nn(scaled, qkv_w[...].reshape(-1, 4 * LANES))
         for piece in range(4):
-            c = spots_s[2 * j + piece // 2, 0, 0]
-            cosine, sine = wave(turn_ref[c if piece % 2 == 0 else 2 * pairs - 1 - c])
+            at = 4 * j + piece
+            cosine, sine = wave(turn_ref[at])
             mine_rows = proj[piece * half : (piece + 1) * half]
 
             def turned(part):
                 z = mine_rows[:, part * LANES : (part + 1) * LANES]
                 return (z * cosine + pltpu.roll(z, 64, 1) * sine).astype(jnp.bfloat16)
 
-            qr[4 * j + piece, 0] = turned(0)
-            qr[4 * j + piece, 1] = turned(1)
-            kr[4 * j + piece] = turned(2)
-            vr[4 * j + piece] = mine_rows[:, 3 * LANES :].astype(jnp.bfloat16)
+            base = (2 * j + piece // 2) * 4 * half + (piece % 2) * half
+            q_ref[pl.ds(pl.multiple_of(base, half), half), :] = turned(0)
+            q_ref[pl.ds(pl.multiple_of(base + 2 * half, half), half), :] = turned(1)
+            k_ref[pl.ds(pl.multiple_of(at * half, half), half), :] = turned(2)
+            v_ref[pl.ds(pl.multiple_of(at * half, half), half), :] = mine_rows[:, 3 * LANES :].astype(jnp.bfloat16)
+
+    def project_first(j, carry):
+        project(j, theirs)
         return carry
 
-    lax.fori_loop(0, 4, project, 0)
-    for s in range(2 * pairs):
-        b = block_of(s)
-        base = (s // 2) * 4 * half + (s % 2) * half
-        both = qr[b]
-        q_ref[pl.ds(base, half), :] = both[0]
-        q_ref[pl.ds(base + 2 * half, half), :] = both[1]
-        k_ref[pl.ds(s * half, half), :] = kr[b]
-        v_ref[pl.ds(s * half, half), :] = vr[b]
+    def project_second(j, carry):
+        project(j, first)
+        return carry
+
+    lax.fori_loop(0, 2, project_first, 0)
+    keep_first = pltpu.make_async_copy(theirs, normed.at[pl.ds(0, 4)], local_sem.at[2])
+    keep_first.start()
+    lax.fori_loop(2, 4, project_second, 0)
+    keep_second = pltpu.make_async_copy(first, normed.at[pl.ds(4, 4)], local_sem.at[3])
+    keep_second.start()
+    give(q_ref, q_o)
+    give(k_ref, k_o)
+    give(v_ref, v_o)
+    give(qkv_w, qkv_o)
+    tokens.finish()
+    outs.step(2)
+    cots.rest()
+    outs.step(3)
+    outs.keep.wait()
+    outc.start()
+
+    def next_weights():
+        downs.step(1)
+        gus.start()
 
     steps = Steps(
-        lambda: outs.step(1), cots.relay, lambda: outs.step(2), lambda: outs.step(3),
-        lambda: (outs.keep.wait(), outc.start(), downs.step(1), gus.start()), cots.rest, outc.relay,
-        lambda: (downs.step(2), outc.rest()), lambda: (cots.partner(), outc.partner()),
+        next_weights, lambda: None, lambda: None, lambda: None, outc.relay, lambda: None, lambda: downs.step(2),
+        lambda: None,
     )
     scaling = HEAD_DIM ** (-0.5)
     mask = causal(2 * half)
     lane = lax.broadcasted_iota(jnp.int32, (half, LANES), 1)
     values_t = v_ref[...].astype(jnp.float32).T.astype(jnp.bfloat16)
     for pair in range(pairs):
-        width = (pair + 1) * 2 * half
+        width_of = (pair + 1) * 2 * half
         q = q_ref[pl.ds(pair * 4 * half, 4 * half), :]
-        before = width - 2 * half
+        before = width_of - 2 * half
         parts = [jnp.where(mask, nt(k_ref[pl.ds(before, 2 * half), :], q) * scaling, -1e30)]
         if pair:
             parts.append(nt(k_ref[pl.ds(0, before), :], q) * scaling)
@@ -966,7 +1125,7 @@
         total = sum(jnp.sum(part, axis=0, keepdims=True) for part in parts)
         parts = [(part * (1.0 / total)).astype(jnp.bfloat16) for part in parts]
         lse_ref[pl.ds(pair, 1), :] = top + jnp.log(total)
-        out_t = nn(values_t[:, before:width], parts[0])
+        out_t = nn(values_t[:, before:width_of], parts[0])
         if pair:
             out_t = out_t + nn(values_t[:, :before], parts[1])
         att_ref[pl.ds(pair * LANES, LANES), :] = out_t
@@ -975,62 +1134,124 @@
             left = result[part * half : (part + 1) * half]
             right = pltpu.roll(result[(2 + part) * half : (3 + part) * half], half, 1)
             low_sorted[2 * pair + part, :, 0:LANES] = jnp.where(lane < half, left, right).astype(jnp.bfloat16)
-            low_sorted[2 * pair + part, :, LANES : 2 * half] = right[:, : 2 * half - LANES].astype(jnp.bfloat16)
+            low_sorted[2 * pair + part, :, LANES:] = right.astype(jnp.bfloat16)
         steps.next()
-    for b in range(2 * pairs):
-        low[b // 2, pl.ds((b % 2) * half, half), :] = low_sorted[span_of(b)]
+    give(att_ref, att_o)
+    give(lse_ref, lse_o)
+    for j in range(pairs):
+        upper = low_sorted[early[j]]
+        lower = low_sorted[2 * pairs - 1 - early[j]]
+        low[j, pl.ds(0, half), :] = upper[:, :LANES]
+        low[j, pl.ds(half, half), :] = lower[:, :LANES]
+        tails = jnp.where(
+            lane < 64, upper[:, LANES:].astype(jnp.float32), pltpu.roll(lower[:, LANES:].astype(jnp.float32), 64, 1)
+        )
+        low[j, pl.ds(2 * half, half), :] = tails.astype(jnp.bfloat16)
+    keep_first.wait()
+    keep_second.wait()
     moved = Exchange(place, low, attended, low_sem)
     moved.start()
-    steps.rest()
+    outc.rest()
+    outc.partner()
+    cots.partner()
     outc.keep.wait()
     moved.finish()
-    total = tok[...].astype(jnp.float32)
-    for q in range(8):
-        total = total + nn(attended[q], out_w[q // 2, pl.ds(4 * (q % 2), 4)].reshape(heads, -1))
-    middle[...] = total
+    middle[...] = tok[...].astype(jnp.float32)
+
+    def out_project(q, carry):
+        middle[...] += nn(unpacked(attended[q]), out_w[q // 2, pl.ds(4 * (q % 2), 4)].reshape(heads, -1))
+        return carry
+
+    lax.fori_loop(0, n, out_project, 0)
+    give(middle, middle_o)
+    gus.step(1)
+    total = middle[...]
     factor = lax.rsqrt(jnp.mean(total * total, axis=-1, keepdims=True) + epsilon)
     own[...] = (total * factor * gains[pl.ds(1, 1), :]).astype(jnp.bfloat16)
-    seconds = Gather(place, own, second_all, gather_sem)
+    seconds = HalfGather(place, own, wide_in, gather_sem)
     seconds.start()
-    downs.step(3)
-    gus.step(1)
     seconds.relay()
     gus.step(2)
     seconds.rest()
+    lows = Gather(place, low, low_all, lows_sem)
+    lows.start()
+    seconds.partner()
+    downs.step(3)
+    downs.keep.wait()
+    give(down_w, down_o)
+    cots.keep.wait()
+    seconds.own_in()
+
+    def early_grad(i, carry):
+        rank = flip(place, i)
+        at = pl.multiple_of((i % 2) * hidden.shape[2], LANES)
+        mine[i // 2, :, pl.ds(at, hidden.shape[2])] = nt(up_all[rank], down_w[...].reshape(hidden.shape[2], -1))
+        return carry
+
+    lax.fori_loop(0, n, early_grad, 0)
     gus.step(3)
-    seconds.partner()
     gus.keep.wait()
-    downs.keep.wait()
-    seconds.keep.wait()
-    cots.keep.wait()
     grads = Reduce(place, mine, theirs, first, out, second, reduce_sem)
     wide = hidden.shape[2]
 
     def block(i):
         rank = flip(place, i)
-        gate_up = nn(second_all[rank], gu_w[...].reshape(-1, 2 * wide))
+        gate_up = nn(wide_in[pl.ds(2 * rank, 2)].reshape(rows, -1), gu_w[...].reshape(-1, 2 * wide))
         gate, raised = gate_up[:, :wide], gate_up[:, wide:]
         sigmoid = 1.0 / (1.0 + jnp.exp(-gate))
         silu = gate * sigmoid
         hidden[rank] = (silu * raised).astype(jnp.bfloat16)
-        hidden_grad = nt(up_all[rank], down_w[...].reshape(wide, -1))
+        hidden_grad = mine[i // 2, :, pl.ds(pl.multiple_of((i % 2) * wide, LANES), wide)]
         gul[rank, :, pl.ds(0, wide)] = (hidden_grad * raised * sigmoid * (1.0 + gate * (1.0 - sigmoid))).astype(jnp.bfloat16)
         gul[rank, :, pl.ds(wide, wide)] = (hidden_grad * silu).astype(jnp.bfloat16)
         return nt(gul[rank], gu_w[...].reshape(-1, 2 * wide))
 
-    def pair_of(k, carry):
-        theirs[k] = block(2 * k + 1).astype(jnp.bfloat16)
-        grads.push(k)
-        mine[k] = block(2 * k)
+    def block_at(t, carry):
+        k = lax.rem(t // 2 + 1, 4)
+        value = block(2 * k + 1 - t % 2)
+
+        @pl.when(t % 2 == 0)
+        def _():
+            theirs[k] = value.astype(jnp.bfloat16)
+            grads.push(k)
+
+        @pl.when(t % 2 == 1)
+        def _():
+            mine[k] = value
+
+        @pl.when(t == 2)
+        def _():
+            lows.relay()
+
+        @pl.when(t == 4)
+        def _():
+            grads.beside()
+
+        @pl.when(t == 5)
+        def _():
+            lows.rest()
+
+        @pl.when(t == 6)
+        def _():
+            grads.across()
+
         return carry
 
-    lax.fori_loop(1, 4, pair_of, 0)
-    grads.across()
-    grads.beside()
-    lax.fori_loop(0, 1, pair_of, 0)
+    lax.fori_loop(0, 8, block_at, 0)
+    give(hidden, hidden_o)
     grads.turn()
+    down_z = PlaneReduce(place, down_g, down_r, down_zs)
+    piece = down_g.shape[1]
+
+    def down_block(t, carry):
+        left = hidden[:, :, pl.ds(pl.multiple_of(t * piece, piece), piece)].reshape(length, piece)
+        down_g[t] = tn(left, up_all[...].reshape(length, width)).astype(jnp.bfloat16)
+        return carry
+
+    lax.fori_loop(0, 4, down_block, 0)
+    down_z.start()
     fetch.wait()
-    seconds.finish(kept=True)
+    seconds.finish()
     gain_grad[...] = jnp.zeros_like(gain_grad)
 
     def norm_back(part, second_grad):
@@ -1044,27 +1265,44 @@
         middle_grad[part, :] = grad
         own[part, :] = grad.astype(jnp.bfloat16)
 
+    gus.finish(kept=True)
+    shard = gu_w.shape[1]
+
+    def gu_block(t, carry):
+        left = wide_in[:, :, pl.ds(pl.multiple_of(t * shard, shard), shard)].reshape(length, shard)
+        gu_w[t] = tn(left, gul[...].reshape(length, 2 * wide)).astype(jnp.bfloat16)
+        return carry
+
+    lax.fori_loop(0, 4, gu_block, 0)
+    give(gu_w, gu_out)
+    down_z.step1()
     grads.total(norm_back)
 
     def head_grads(q, carry):
         weight = out_w[q // 2, pl.ds(4 * (q % 2), 4)].reshape(heads, -1)
-        attended[q] = nt(own[...], weight).astype(jnp.bfloat16)
+        attended[q] = packed(nt(own[...], weight)).astype(jnp.bfloat16)
         return carry
 
     lax.fori_loop(0, n, head_grads, 0)
     heads_back = Exchange(place, attended, agrad, agrad_sem)
     heads_back.start()
     for q in range(8):
-        mcols_send[q] = own[:, q * heads : (q + 1) * heads]
+        mcols_send[q] = packed(own[:, q * heads : (q + 1) * heads].astype(jnp.float32)).astype(jnp.bfloat16)
     columns = Exchange(place, mcols_send, mcols, mcols_sem)
     columns.start()
-    for move in (qkvs, outs, gus, downs):
+    down_z.step2()
+    lows.partner()
+    heads_back.finish()
+    down_z.total()
+    down_sum[...] = down_g[place.z]
+    for move in (qkvs, outs, downs, cots, outc):
         move.finish(kept=True)
-    for move in (cots, outc):
-        move.finish(kept=True)
-    heads_back.finish()
+    lows.finish()
     columns.finish()
+    for copy in given:
+        copy.wait()
     grads.finish()
+    down_z.finish()
 
 
 def front_moves(tok, up_low, spot, gain_own, qkv_own, out_own, gu_own, down_own, turns, up):
@@ -1078,115 +1316,51 @@
     pairs = length // 192
     halves = pltpu.VMEM((6, rows // 2, width), bf)
     quads = pltpu.VMEM((4, rows, width), bf)
-    blocks = pltpu.VMEM((n, rows, rows), bf)
+    small = (n, 3 * rows // 2, LANES)
     all_of = lambda x: shape((planes,) + x.shape, x.dtype)
     gathered = lambda x: pltpu.VMEM((planes,) + x.shape, x.dtype)
     ring = dma((2, Gather.sems))
+    half_ring = dma((2, HalfGather.sems))
     line = dma((3, planes))
     swap = dma((2, n))
+    kept = (
+        shape((n, rows, wide), bf), all_of(qkv_own), all_of(down_own),
+        shape((2 * length, LANES), bf), shape((length, LANES), bf), shape((length, LANES), bf),
+        shape((pairs * LANES, 384), f32), shape((pairs, 384), f32), shape((rows, width), f32),
+    )
     return pl.pallas_call(
         front_kernel,
         out_shape=(
-            shape((n, rows, width), bf), shape((n, rows, width), bf), shape((n, rows, width), bf),
-            shape((n, rows, wide), bf), shape((n, rows, 2 * wide), bf), all_of(qkv_own), all_of(down_own),
-            shape((2 * length, LANES), bf), shape((length, LANES), bf), shape((length, LANES), bf),
-            shape((pairs * LANES, 384), f32), shape((pairs, 384), f32), shape((n, rows, rows), bf),
-            shape((rows, width), f32), shape((rows, width), f32), shape((1, width), f32), shape((n,) + spot.shape, spot.dtype),
-            shape((2, width), f32), shape((n, rows, rows), bf), shape((n, rows, rows), bf),
-        ),
+            shape((rows, width), f32), shape((1, width), f32), shape((n,) + spot.shape, spot.dtype), shape((2, width), f32),
+            shape(down_own.shape, bf),
+        ) + kept + (shape((n, rows, width), bf), shape(small, bf), shape((n,) + small, bf), all_of(gu_own), shape(small, bf)),
         in_specs=vm(9) + anywhere(1),
-        out_specs=vm(18) + anywhere(2),
-        scratch_shapes=[
+        out_specs=vm(5) + anywhere(14),
+        scratch_shapes=[pltpu.VMEM(x.shape, x.dtype) for x in kept] + [
+            pltpu.VMEM(small, bf),
+            pltpu.VMEM((2 * n, rows // 2, width), bf), pltpu.VMEM((n, rows, width), bf), pltpu.VMEM((n, rows, 2 * wide), bf),
             gathered(gu_own), gathered(out_own), pltpu.VMEM((planes, n) + out_own.shape, bf),
-            pltpu.VMEM((16, 2, 96, LANES), bf), pltpu.VMEM((16, 96, LANES), bf), pltpu.VMEM((16, 96, LANES), bf),
-            pltpu.VMEM((16, 96, 192), bf), gathered(gain_own), pltpu.SMEM((n,) + spot.shape, jnp.int32),
-            blocks, blocks, pltpu.VMEM((rows, width), bf),
+            pltpu.VMEM((16, 96, 2 * LANES), bf), gathered(gain_own), pltpu.SMEM((n,) + spot.shape, jnp.int32),
+            pltpu.SMEM((2 * n,), jnp.int32), pltpu.VMEM(small, bf),
+            pltpu.VMEM(small, bf), pltpu.VMEM((rows, width), bf),
             pltpu.VMEM((4, rows, width), f32), quads, quads, halves, halves,
-            ring, ring, swap, dma((2, planes)), line, line, ring, line, line, dma((2,)),
-            swap, ring, dma((2, Reduce.sems)), swap, swap,
+            gathered(down_own), pltpu.VMEM((planes + 1,) + down_own.shape, bf),
+            half_ring, ring, swap, dma((2, planes)), line, line, ring, line, line, dma((15,)),
+            swap, half_ring, dma((2, Reduce.sems)), swap, ring, dma((2, planes + 1)), swap,
         ],
         compiler_params=pltpu.CompilerParams(collective_id=1, has_side_effects=True, vmem_limit_bytes=67043328),
         name="front_moves",
     )(tok, up_low, spot, gain_own, qkv_own, out_own, gu_own, down_own, turns, up)
 
 
-class PlaneReduce:
-    def __init__(self, place, block, recv, sem):
-        self.place, self.block, self.recv, self.sem = place, block, recv, sem
-
-    def hop(self, ok, part, slot, target, first, wait):
-        copy = send(
-            self.block.at[part], self.recv.at[slot], self.sem.at[0, part], self.sem.at[1, slot], fsdp=target
-        )
-
-        @pl.when(ok)
-        def _():
-            if wait:
-                copy.wait_send()
-                return
-            if not first:
-                self.merge(part, part)
-            copy.start()
-
-    def merge(self, part, slot):
-        piece = self.recv.at[slot]
-        pltpu.make_async_copy(piece, piece, self.sem.at[1, slot]).wait()
-        total = self.block[part].astype(jnp.float32) + self.recv[slot].astype(jnp.float32)
-        self.block[part] = total.astype(jnp.bfloat16)
-
-    def ends(self, i, wait=False):
-        z = self.place.z
-        low = z == 0
-        part = jnp.where(low, 3 - i, i)
-        slot = part if i < 2 else jnp.where(low, part, 4)
-        self.hop(jnp.logical_or(low, z == 3), part, slot, jnp.where(low, 1, 2), True, wait)
-
-    def inner(self, up, down, slot_up, slot_down, to_up, to_down, wait=False):
-        z = self.place.z
-        low = z == 1
-        part = jnp.where(low, up, down)
-        slot = jnp.where(low, slot_up, slot_down)
-        self.hop(jnp.logical_or(low, z == 2), part, slot, jnp.where(low, to_up, to_down), False, wait)
-
-    def start(self, wait=False):
-        for i in range(3):
-            self.ends(i, wait)
-
-    def step1(self, wait=False):
-        self.inner(3, 0, 3, 0, 2, 1, wait)
-
-    def step2(self, wait=False):
-        self.inner(2, 1, 2, 4, 2, 1, wait)
-        self.inner(0, 3, 4, 3, 0, 3, wait)
-
-    def total(self):
-        z = self.place.z
-
-        @pl.when(z > 0)
-        def _():
-            self.merge(z, z)
-
-        @pl.when(z < 3)
-        def _():
-            self.merge(z, 4)
-
-    def own(self):
-        return self.block.at[self.place.z]
-
-    def finish(self):
-        self.start(True)
-        self.step1(True)
-        self.step2(True)
-
-
 def back_moves_kernel(
-    early_ref, hidden, agrad, mcols, low, q_ref, k_ref, v_ref, att_ref, lse_ref, turn_ref, qkv_w, down_w, tok, gain,
-    ffn_gain, middle, second_all, gul, up_all, normed, middle_grad,
-    grad, result, gains, low_all, down_all, gu_all, out_all, qkv_all,
-    wide_a, wide_b, low_buf, down_g, gu_g, out_g, qkv_g, down_r, gu_r, out_r, qkv_r,
-    mine, theirs, first, out, second, dk_ref, dv_ref, pg_sorted, pgrad,
+    early_ref, tok, gain, ffn_gain, down_sum,
+    gu_i, middle_grad_i, hidden_i, down_i, k_i, q_i, v_i, agrad_i, att_i, lse_i, turn_i, normed_i, middle_i, qkv_i, mcols_i, low_i,
+    grad, result, gains, down_all, gu_all, out_all, qkv_all,
+    gu_g, hidden, down_w, k_ref, q_ref, v_ref, agrad, att_ref, lse_ref, turn_ref, normed_in, middle, qkv_w, mcols_in, low_in, out_g, qkv_g, gu_r, out_r, qkv_r,
+    mine, theirs, first, out, second, dk_ref, dv_ref, pg_sorted, mcols,
     gain_sum, mine_gain, ctx_gain, plane_sum, plane_gain,
-    free, local_sem, sum_sem, reduce_sem, low_sem, down_zs, gu_zs, out_zs, qkv_zs, down_cs, gu_cs, out_cs, qkv_cs,
+    free, local_sem, sum_sem, reduce_sem, gu_zs, out_zs, qkv_zs, down_cs, gu_cs, out_cs, qkv_cs,
     gain_sem, plane_sem,
 ):
     place = Place()
@@ -1199,13 +1373,13 @@
     loads = [
         pltpu.make_async_copy(source, target, local_sem.at[at])
         for at, (source, target) in enumerate((
-            (up_all, wide_b), (second_all, wide_a), (gul, wide_b.at[:, :, pl.ds(0, gul.shape[2])]),
-            (normed, wide_a), (middle_grad, grad),
+            (gu_i, gu_g), (hidden_i, hidden), (down_i, down_w), (k_i, k_ref), (q_i, q_ref), (v_i, v_ref),
+            (agrad_i, agrad), (att_i, att_ref), (lse_i, lse_ref), (turn_i, turn_ref), (middle_i, middle),
+            (normed_i, normed_in), (qkv_i, qkv_w), (mcols_i, mcols_in), (low_i, low_in), (middle_grad_i, grad),
         ))
     ]
-    loads[0].start()
-    loads[1].start()
-    loads[4].start()
+    for load in loads:
+        load.start()
     greet(place, planes=True)
     early = [early_ref[j] for j in range(pairs)]
     holder = []
@@ -1214,31 +1388,17 @@
         for j in range(pairs):
             at = jnp.where(early[j] == t, j, at)
         holder.append(at)
-
-    def block_of(s):
-        return 2 * holder[s] if s < pairs else 2 * holder[2 * pairs - 1 - s] + 1
-
-    def span_of(b):
-        return early[b // 2] if b % 2 == 0 else 2 * pairs - 1 - early[b // 2]
-
-    down_z = PlaneReduce(place, down_g, down_r, down_zs)
     gu_z = PlaneReduce(place, gu_g, gu_r, gu_zs)
     out_z = PlaneReduce(place, out_g, out_r, out_zs)
     qkv_z = PlaneReduce(place, qkv_g, qkv_r, qkv_zs)
     sums = Reduce(place, mine, theirs, first, out, second, sum_sem)
-    lows = Gather(place, low, low_all, low_sem)
-
+    downs = Gather(place, down_sum, down_all, down_cs)
+    gus = Gather(place, gu_z.own(), gu_all, gu_cs)
     loads[0].wait()
-    piece = down_g.shape[1]
-
-    def down_block(t, carry):
-        left = hidden[:, :, pl.ds(pl.multiple_of(t * piece, piece), piece)].reshape(length, piece)
-        down_g[t] = tn(left, wide_b[...].reshape(length, width)).astype(jnp.bfloat16)
-        return carry
-
-    lax.fori_loop(0, 4, down_block, 0)
-    down_z.start()
-    loads[2].start()
+    gu_z.start()
+    downs.start()
+    loads[1].wait()
+    loads[2].wait()
 
     def other(k, carry):
         theirs[k] = nn(hidden[flip(place, 2 * k + 1)], down_w[...].reshape(-1, width)).astype(jnp.bfloat16)
@@ -1251,27 +1411,14 @@
 
     lax.fori_loop(0, 4, other, 0)
     lax.fori_loop(0, 4, ours, 0)
+    downs.relay()
     sums.across()
     sums.beside()
-    loads[1].wait()
-    loads[2].wait()
-    shard = gu_g.shape[1]
-
-    def gu_block(t, carry):
-        left = wide_a[:, :, pl.ds(pl.multiple_of(t * shard, shard), shard)].reshape(length, shard)
-        right = wide_b[:, :, pl.ds(0, gul.shape[2])].reshape(length, gul.shape[2])
-        gu_g[t] = tn(left, right).astype(jnp.bfloat16)
-        return carry
-
-    lax.fori_loop(0, 4, gu_block, 0)
-    gu_z.start()
-    loads[3].start()
-    down_z.step1()
-    sums.turn()
-    lows.start()
-
-    def finish_rows(part, down_sum):
-        result[part, :] = (middle[part, :] + down_sum).astype(jnp.bfloat16)
+    for load in loads[3:11]:
+        load.wait()
+
+    def finish_rows(part, down_out):
+        result[part, :] = (middle[part, :] + down_out).astype(jnp.bfloat16)
 
     def sums_done():
         sums.total(finish_rows)
@@ -1279,11 +1426,17 @@
         for rank in (place.p, place.x, place.y):
             pl.semaphore_signal(free, inc=1, device_id={"ctx": rank}, device_id_type=MESH)
 
-    downs = Gather(place, down_z.own(), down_all, down_cs)
-    gus = Gather(place, gu_z.own(), gu_all, gu_cs)
+    def columns_done():
+        loads[13].wait()
+
+        def unpack(q, carry):
+            mcols[q] = unpacked(mcols_in[q])
+            return carry
+
+        lax.fori_loop(0, n, unpack, 0)
+
     steps = Steps(
-        sums_done, down_z.step2, lows.relay, lambda: (down_z.total(), gu_z.step1()), lows.rest,
-        downs.start, downs.relay, lambda: (lows.partner(), downs.rest()),
+        lambda: None, downs.rest, lambda: None, gu_z.step1, downs.partner, sums.turn, columns_done, lambda: None,
     )
     scaling = HEAD_DIM ** (-0.5)
     mask = causal(2 * half)
@@ -1293,12 +1446,16 @@
         q = q_ref[pl.ds(pair * 4 * half, 4 * half), :]
         firsts, seconds = [], []
         for part in range(2):
-            piece_of = agrad[block_of(2 * pair + part)].astype(jnp.float32)
-            left = piece_of[:, 0:LANES]
-            right = jnp.concatenate([piece_of[:, LANES : 2 * half], jnp.zeros((half, 64), jnp.float32)], axis=1)
+            s = 2 * pair + part
+            side = 0 if s < pairs else 1
+            piece_of = agrad[holder[s] if s < pairs else holder[2 * pairs - 1 - s]].astype(jnp.float32)
+            left = piece_of[side * half : (side + 1) * half]
+            tail = piece_of[2 * half :]
+            right = tail if side == 0 else pltpu.roll(tail, 64, 1)
             firsts.append(jnp.where(lane < half, left, 0.0))
-            seconds.append(pltpu.roll(jnp.where(lane < half, right, left), LANES - half, 1))
-        seconds = [jnp.where(lane < half, s, 0.0) for s in seconds]
+            seconds.append(
+                jnp.where(lane < half, pltpu.roll(jnp.where(lane < half, right, left), LANES - half, 1), 0.0)
+            )
         grads = jnp.concatenate(firsts + seconds, axis=0)
         delta = jnp.sum(grads.T * att_ref[pl.ds(pair * LANES, LANES), :], axis=0, keepdims=True)
         grads = grads.astype(jnp.bfloat16)
@@ -1337,51 +1494,61 @@
         z = dk_ref[spot, :]
         pg_sorted[s, :, 2 * LANES : 3 * LANES] = (z * cosine - pltpu.roll(z, 64, 1) * sine).astype(jnp.bfloat16)
         pg_sorted[s, :, 3 * LANES :] = dv_ref[spot, :].astype(jnp.bfloat16)
-    for b in range(2 * pairs):
-        pgrad[b // 2, pl.ds((b % 2) * half, half), :] = pg_sorted[span_of(b)]
-    steps.rest()
-
-    loads[3].wait()
+
+    loads[11].wait()
+    loads[12].wait()
+    shard = gu_g.shape[1]
 
     def qkv_block(t, carry):
-        left = wide_a[:, :, pl.ds(pl.multiple_of(t * shard, shard), shard)].reshape(length, shard)
-        qkv_g[t] = tn(left, pgrad[...].reshape(length, 4 * LANES)).astype(jnp.bfloat16)
+        left = normed_in[:, :, pl.ds(pl.multiple_of(t * shard, shard), shard)].reshape(length, shard)
+        qkv_g[t] = tn(left, pg_sorted[...].reshape(length, 4 * LANES)).astype(jnp.bfloat16)
         return carry
 
+    sums_done()
     lax.fori_loop(0, 4, qkv_block, 0)
     qkv_z.start()
+    gu_z.step2()
     pl.semaphore_wait(free, 3)
     grads = Reduce(place, mine, theirs, first, out, second, reduce_sem)
 
+    def chunk(i):
+        at = early_ref[flip(place, i)]
+        rows_of = jnp.concatenate([pg_sorted[at], pg_sorted[2 * pairs - 1 - at]], axis=0)
+        return nt(rows_of, qkv_w[...].reshape(width, -1))
+
     def push(k, carry):
-        theirs[k] = nt(pgrad[flip(place, 2 * k + 1)], qkv_w[...].reshape(width, -1)).astype(jnp.bfloat16)
+        theirs[k] = chunk(2 * k + 1).astype(jnp.bfloat16)
         grads.push(k)
         return carry
 
     def keep(k, carry):
-        mine[k] = nt(pgrad[flip(place, 2 * k)], qkv_w[...].reshape(width, -1))
+        mine[k] = chunk(2 * k)
         return carry
 
     lax.fori_loop(0, 4, push, 0)
     lax.fori_loop(0, 4, keep, 0)
     grads.across()
     grads.beside()
-    lows.keep.wait()
-    for t in range(4):
-        for side in range(2):
-            src = 2 * t + side
-            fetch = pltpu.make_async_copy(low_all.at[src], low_buf, local_sem.at[5 + src])
-            fetch.start()
-            fetch.wait()
-            out_g[t, pl.ds(side * rows, rows), :] = tn(
-                low_buf[...].reshape(length, rows), mcols[...].reshape(length, rows)
-            ).astype(jnp.bfloat16)
+    loads[14].wait()
+    loads[15].wait()
+
+    def out_block(src, carry):
+        heads = low_in[src, :, pl.ds(0, rows), :].reshape(length, LANES)
+        tails = low_in[src, :, pl.ds(rows, half), :].reshape(length // 2, LANES)
+        upper = tn(heads, mcols[...].reshape(length, rows))
+        from_a = tn(tails, mcols[:, pl.ds(0, half), :].reshape(length // 2, rows))
+        from_b = tn(tails, mcols[:, pl.ds(half, half), :].reshape(length // 2, rows))
+        at = pl.multiple_of((src % 2) * rows, rows)
+        out_g[src // 2, pl.ds(at, LANES), :] = upper.astype(jnp.bfloat16)
+        out_g[src // 2, pl.ds(pl.multiple_of(at + LANES, 64), 64), :] = (from_a[:64] + from_b[64:]).astype(jnp.bfloat16)
+        return carry
+
+    lax.fori_loop(0, 8, out_block, 0)
     out_z.start()
-    gu_z.step2()
-    downs.partner()
     grads.turn()
+    gu_z.total()
+    gus.start()
     gain_sum[...] = jnp.zeros_like(gain_sum)
-    loads[4].wait()
 
     def norm_back(part, normed_grad):
         x = tok[part, :].astype(jnp.float32)
@@ -1392,6 +1559,7 @@
         inner = jnp.mean(scaled * unit, axis=-1, keepdims=True)
         grad[part, :] = grad[part, :] + factor * (scaled - unit * inner)
 
+    qkv_z.step1()
     grads.total(norm_back)
     gain_grad = gain_sum[...]
     count = mine_gain.shape[0] // 2
@@ -1400,24 +1568,18 @@
         mine_gain[pl.ds(count + at, 1), :] = ffn_gain[:, at * shard : (at + 1) * shard]
     ctx_sum = Share(place, mine_gain, ctx_gain, gain_sem)
     ctx_sum.start()
-    qkv_z.step1()
-    gu_z.total()
-    gus.start()
+    gus.relay()
+    qkv_z.step2()
     out_z.step1()
     ctx_sum.finish()
     plane_sum[...] = jnp.sum(ctx_gain[...], axis=0)
     planes = PlaneShare(place, plane_sum, plane_gain, plane_sem)
     planes.start()
-    gus.relay()
-    qkv_z.step2()
+    out_z.step2()
+    qkv_z.total()
     gus.rest()
-    out_z.step2()
-    planes.finish()
-    gains[...] = jnp.sum(plane_gain[...], axis=0)
-    qkv_z.total()
     qkvs = Gather(place, qkv_z.own(), qkv_all, qkv_cs)
     qkvs.start()
-    gus.partner()
     out_z.total()
     outs = Gather(place, out_z.own(), out_all, out_cs)
     qkvs.relay()
@@ -1425,19 +1587,19 @@
     qkvs.rest()
     outs.relay()
     outs.rest()
+    planes.finish()
+    gains[...] = jnp.sum(plane_gain[...], axis=0)
+    gus.partner()
     qkvs.partner()
     outs.partner()
-    for move in (down_z, gu_z, out_z, qkv_z, downs, gus, outs, qkvs, grads):
+    for move in (gu_z, out_z, qkv_z, downs, gus, outs, qkvs, grads):
         move.finish()
-    lows.finish(kept=True)
-
-
-def back_moves(early, hidden, agrad, mcols, low, q, k, v, att, lse, turns, qkv_w, down_w, tok, gain, ffn_gain, middle,
-               second_all, gul, up_all, normed, middle_grad):
+
+
+def back_moves(early, tok, gain, ffn_gain, down_sum, *moved):
     n, planes = lax.axis_size("ctx"), lax.axis_size("fsdp")
     rows, width = tok.shape
     length = n * rows
-    wide = hidden.shape[2]
     shard = width // planes
     bf, f32 = jnp.bfloat16, jnp.float32
     shape = jax.ShapeDtypeStruct
@@ -1445,31 +1607,29 @@
     halves = pltpu.VMEM((6, rows // 2, width), bf)
     quads = pltpu.VMEM((4, rows, width), bf)
     small = (2 * planes, shard)
-    parts = ((wide // planes, width), (shard, 2 * wide), (shard, rows), (shard, 4 * LANES))
+    parts = (moved[0].shape[1:], (shard, rows), (shard, 4 * LANES))
     ring = dma((2, Gather.sems))
     return pl.pallas_call(
         back_moves_kernel,
-        out_shape=(
-            shape((rows, width), f32), shape((rows, width), bf), shape(small, f32), shape((n,) + low.shape, bf),
-        ) + tuple(shape((n,) + part, bf) for part in parts),
-        in_specs=[pl.BlockSpec(memory_space=pltpu.SMEM)] + vm(16) + anywhere(5),
-        out_specs=vm(3) + anywhere(5),
-        scratch_shapes=[pltpu.VMEM((n, rows, width), bf)] * 2 + [pltpu.VMEM(low.shape, bf)]
-        + [pltpu.VMEM((planes,) + part, bf) for part in parts]
+        out_shape=(shape((rows, width), f32), shape((rows, width), bf), shape(small, f32))
+        + tuple(shape((n,) + part, bf) for part in (down_sum.shape,) + parts),
+        in_specs=[pl.BlockSpec(memory_space=pltpu.SMEM)] + vm(4) + anywhere(len(moved)),
+        out_specs=vm(3) + anywhere(4),
+        scratch_shapes=[pltpu.VMEM(x.shape, x.dtype) for at, x in enumerate(moved) if at != 1]
+        + [pltpu.VMEM((planes,) + part, bf) for part in parts[1:]]
         + [pltpu.VMEM((planes + 1,) + part, bf) for part in parts]
         + [
             pltpu.VMEM((4, rows, width), f32), quads, quads, halves, halves,
-            pltpu.VMEM((length, LANES), f32), pltpu.VMEM((length, LANES), f32),
-            pltpu.VMEM((16, 96, 4 * LANES), bf), pltpu.VMEM((n, rows, 4 * LANES), bf),
+            pltpu.VMEM((length, LANES), f32), pltpu.VMEM((length, LANES), f32), pltpu.VMEM((16, 96, 4 * LANES), bf),
+            pltpu.VMEM((n, rows, rows), bf),
             pltpu.VMEM((1, width), f32), pltpu.VMEM(small, f32), pltpu.VMEM((n,) + small, f32),
             pltpu.VMEM(small, f32), pltpu.VMEM((planes,) + small, f32),
-            pltpu.SemaphoreType.REGULAR, dma((13,)), dma((2, Reduce.sems)), dma((2, Reduce.sems)), ring,
-            dma((2, 5)), dma((2, 5)), dma((2, 5)), dma((2, 5)), ring, ring, ring, ring, dma((2, n)), dma((2, planes)),
+            pltpu.SemaphoreType.REGULAR, dma((16,)), dma((2, Reduce.sems)), dma((2, Reduce.sems)),
+            dma((2, 5)), dma((2, 5)), dma((2, 5)), ring, ring, ring, ring, dma((2, n)), dma((2, planes)),
         ],
         compiler_params=pltpu.CompilerParams(collective_id=6, has_side_effects=True, vmem_limit_bytes=67043328),
         name="back_moves",
-    )(early, hidden, agrad, mcols, low, q, k, v, att, lse, turns, qkv_w, down_w, tok, gain, ffn_gain, middle,
-      second_all, gul, up_all, normed, middle_grad)
+    )(early, tok, gain, ffn_gain, down_sum, *moved)
 
 
 def pack_kernel(down, gu, out, qkv, grad, result, down_o, gu_o, out_o, qkv_o, grad_o, result_o):
@@ -1579,17 +1739,18 @@
     gains = jnp.concatenate([attn_gain, ffn_gain, jnp.zeros((6, shard), attn_gain.dtype)], axis=0).astype(jnp.float32)
     spot = jnp.full((8, LANES), positions[0, 0] // (rows // 2), jnp.int32)
     turns = table(length)
+    turns = turns.reshape(2 * n, rows // 2, LANES)
     (
-        normed, upstream_all, second_all, hidden, gate_up_low, qkv_block, down_block, q, k, v, att, lse, low,
-        middle_grad, middle, ffn_partial, spots, gains, attended_grad, middle_cols,
+        middle_grad, ffn_partial, spots, gains, down_sum, hidden, qkv_block, down_block, q, k, v, att, lse, middle,
+        normed, attended_grad, low_all, gate_up_grad, middle_cols,
     ) = front_moves(
-        tokens[0], cotangent[0].astype(jnp.bfloat16), spot, gains, qkv_own, out_own, gate_up_own, down_own,
-        turns.reshape(2 * n, rows // 2, LANES), cotangent[0],
-    )
-    stream_grad, result, gain_grads, _, down_grad, gate_up_grad, out_grad, qkv_grad = back_moves(
-        spots[:, 0, 0], hidden, attended_grad.reshape(2 * n, rows // 2, -1), middle_cols, low, q, k, v, att, lse,
-        turns.reshape(2 * n, rows // 2, LANES), qkv_block, down_block, tokens[0], gains[0:1], ffn_partial, middle,
-        second_all, gate_up_low, upstream_all, normed, middle_grad,
+        tokens[0], cotangent[0].astype(jnp.bfloat16), spot, gains, qkv_own, out_own, gate_up_own, down_own, turns,
+        cotangent[0],
+    )
+    stream_grad, result, gain_grads, down_grad, gate_up_grad, out_grad, qkv_grad = back_moves(
+        spots[:, 0, 0], tokens[0], gains[0:1], ffn_partial, down_sum,
+        gate_up_grad, middle_grad, hidden, down_block, k, q, v, attended_grad, att, lse, turns, normed, middle,
+        qkv_block, middle_cols, low_all,
     )
     gain_grads = gain_grads.reshape(2, planes, shard)
     gain_grads = lax.dynamic_index_in_dim(gain_grads, lax.axis_index("fsdp"), 1, keepdims=False)

time: 415 us -> 358 us (0.86)
  the two profiles are of different devices: /device:TPU:0 before, /device:TPU:9 now
where the time goes in v5:
time: 358 us; the launch traced here: 352 us
  Pallas kernels  322 us (90%)
  local copies, waits for them, and re-layouts  20.2 us (6%)
  other arithmetic  6.3 us (2%)
    pallas_call x1, Pallas kernels, front_moves(): pl.pallas_call(front_kernel, out_shape=(shape((rows, width), f32), shape(...  179 us
    pallas_call x1, Pallas kernels, back_moves(): pl.pallas_call(back_moves_kernel, out_shape=(shape((rows, width), f32), s...  122 us
    pallas_call x1, Pallas kernels, pack(): pl.pallas_call(pack_kernel, grid=(n,), out_shape=(shape((n * down.shape[1...  21 us

profile of v5, /device:TPU:9, one launch (start us, length us, event | category | flops | bytes accessed | tf_op | source)
XLA Modules:
  0.0 351.8 jit_solution(10719245395521929146)
XLA Ops:
  0.6 1.2 slice.69
  4.5 1.4 maximum_convert_fusion.gain_own
  5.8 1.6 dynamic-slice_bitcast_fusion.2.out_own
  7.4 1.2 dynamic-slice_bitcast_fusion.3
  8.7 1.1 dynamic-slice_bitcast_fusion.1
  10.0 1.3 concatenate.17.qkv_own
  11.3 1.8 dynamic-slice_bitcast_fusion.down_own
  13.0 0.9 bitcast_convert_fusion.up_low
  13.9 1.8 constant_dynamic-slice_fusion.2
  15.9 0.6 fusion.9
  16.5 0.6 fusion.8
  17.2 0.6 fusion.7
  17.8 0.6 fusion.6
  18.4 0.6 fusion.5
  19.1 0.6 fusion.4
  19.7 0.6 fusion.3
  21.0 2.9 fusion.1
  23.9 1.2 select_maximum_fusion
  25.1 178.8 %front_moves.1 = (f32[192,1536]{1,0:T(8,128)}, f32[1,1536]{1,0:T(1,128)}, s32[8,8,128]{2,1,0:T(8,128)}, f32[2,1536]{1,0:T(2,128)}, bf16[128,1536]{1,0:T(8,128)(2...) custom-call(bf16[192,1536]{1,0:T(8,128)(2,1)} %bitcast.73, ...), custom_call_target="tpu_custom_call" | custom-call | tf_op jit(solution)/shard_map/front_moves/pallas_call | solution.py:1331
  203.9 1.5 slice_reduce_fusion.early_ref
  205.4 1.3 slice.85.gain
  206.7 122.4 %back_moves.1 = (f32[192,1536]{1,0:T(8,128)}, bf16[192,1536]{1,0:T(8,128)(2,1)}, f32[8,384]{1,0:T(8,128)}, bf16[8,128,1536]{2,1,0:T(8,128)(2,1)}, bf16[8,384,102...) custom-call(s32[8]{0:T(128)} %slice_reduce_fusion.early_ref, ...), custom_call_target="tpu_custom_call" | custom-call | tf_op jit(solution)/shard_map/back_moves/pallas_call | solution.py:1612
  329.0 0.7 reshape.54
  330.3 21.0 %pack.1 = (f32[1024,1536]{1,0:T(8,128)}, f32[24576,128]{1,0:T(8,128)}, f32[384,1536]{1,0:T(8,128)}, f32[384,3072]{1,0:T(8,128)}, f32[192,1536]{1,0:T(8,128)}, /*index=5*/bf16[192,1536]{1,0:T(8,128)(2,1)}) custom-call(bf16[8,128,1536]{2,1,0:T(8,128)(2,1)} %get-tuple-element.59.down, bf16[8,384,1024]{2,1,0:T(8,128)(2,1)} %get-tuple-element.60.gu, ...), custom_call_target="tpu_custom_call" | custom-call | tf_op jit(solution)/shard_map/pack/pallas_call | solution.py:1687
  (13 shorter events, 2.2 us)
Async XLA Ops:
  7.4 5.6 %copy-start = (f32[1,192,1536]{2,1,0:T(8,128)S(1)}, f32[1,192,1536]{2,1,0:T(8,128)}, u32[]{:S(2)}) copy-start(f32[1,192,1536]{2,1,0:T(8,128)} %param.17) | copy-start | bytes 3538948
